TPU v7x, 128 devices: a whole 4x4x4 slice. The times are simulated.
128 devices in a mesh: band: 32 (over x, z, core), lev: 4 (over y).
Axes of the slice: x: 4, y: 4, z: 4, core: 2. Of those that a mesh axis runs over, the one named last changes fastest.
Arguments:
- checkpoints: float32 [4, 4, 32, 2, 256, 256], P(None, None, 'lev', None, 'band'), may hold values from -0.4 to 0.4
- final_cot: float32 [4, 32, 2, 256, 256], P(None, 'lev', None, 'band'), may hold values from -6 to 6
- obs_cot: float32 [4, 4, 32, 256, 512], P(None, None, None, 'band', 'lev'), may hold values from -0.2 to 0.2
- obs_time: int32 [4], replicated, may hold values from 0 to 3
- wave_order: int32 [256], replicated, may hold values from 0 to 255, each once
- legendre: bfloat16 [256, 256, 256], P('band'), may hold values from -0.375 to 0.375
- w_in: bfloat16 [128, 512], replicated, may hold values from -0.5 to 0.5
- w_out: bfloat16 [512, 128], replicated, may hold values from -0.25 to 0.25
- bias: float32 [512], replicated, may hold values from -3 to 3
Outputs:
- grad_state: float32 [4, 32, 2, 256, 256], P(None, 'lev', None, 'band')
- grad_w_in: float32 [128, 512], replicated
- grad_w_out: float32 [512, 128], replicated
- grad_bias: float32 [512], replicated
Inputs may be any that keep to these rules, and one draw needn't show every extreme that they name: `obs_time`: each number names a step of the rollout. `wave_order`: each of the 256 zonal wavenumbers once.
All inputs are finite; a program needn't handle non-finite values.
Results may differ from a plain program's by a relative error of at most 0.014.
Values may be sent and summed in bfloat16 or wider, within the bound.
No kernel may reach another device: no remote copies, remote signals or barrier semaphores. Data moves between devices by JAX's collectives and lax.ppermute only.
A program may use at most 128 MiB of HBM per device.

v0:
```python
import jax
import jax.numpy as jnp
from jax import lax
from jax.sharding import Mesh
from jax.sharding import PartitionSpec as P

BAND = ("band_0", "band_1", "band_2")
BAND_LEV = ("band_0", "band_1", "band_2", "lev")


dt_scale = 1.0


def in_blocks(array, dim, length):
    lengths = array.shape
    parts = array.reshape(*lengths[:dim], length, lengths[dim] // length, *lengths[dim + 1 :])
    return jnp.moveaxis(parts, dim, 0)


def joined_along(parts, dim):
    parts = jnp.moveaxis(parts, 0, dim)
    lengths = parts.shape
    return parts.reshape(*lengths[:dim], lengths[dim] * lengths[dim + 1], *lengths[dim + 2 :])


def turned_blocks(parts, axes, turns):
    lengths = [lax.axis_size(a) for a in axes]
    parts = parts.reshape(*lengths, *parts.shape[1:])
    for k in turns:
        parts = lax.all_to_all(parts, axes[k], split_axis=k, concat_axis=k, tiled=True)
    return parts.reshape(-1, *parts.shape[len(axes) :])


def two_step_exchange(array, groups, turns, split_dim, concat_dim):
    length = lax.axis_size(groups[0]) * lax.axis_size(groups[1])
    parts = in_blocks(array, split_dim, length)
    return joined_along(turned_blocks(parts, groups, turns), concat_dim)


def packed_total(arrays, axis):
    ends = [0]
    for a in arrays:
        ends.append(ends[-1] + a.size)
    total = lax.psum(jnp.concatenate([a.ravel() for a in arrays]), axis)
    return tuple((total[b:e].reshape(a.shape) for a, b, e in zip(arrays, ends, ends[1:])))


def tables(wave_order, lon_count):
    longitude = jnp.arange(lon_count, dtype=jnp.int32)
    phase_index = wave_order[:, None] * longitude[None, :] % lon_count
    angles = 2.0 * jnp.pi / lon_count * phase_index.astype(jnp.float32)
    return (jnp.cos(angles).astype(jnp.bfloat16), jnp.sin(angles).astype(jnp.bfloat16))


def synth_legendre(masked, spectral):
    sums = jnp.einsum(
        "rjn,vlcrn->jrcvl",
        masked,
        spectral.astype(jnp.bfloat16),
        preferred_element_type=jnp.float32,
    )
    return sums.astype(jnp.bfloat16)


def synth_fourier(coefficients, factor, cosine_table, sine_table):
    scale = factor.astype(jnp.bfloat16)[None, :, None, None]
    real_part = coefficients[:, :, 0] * scale
    imag_part = coefficients[:, :, 1] * scale
    return jnp.einsum(
        "jrvl,ro->vljo", real_part, cosine_table, preferred_element_type=jnp.float32
    ) - jnp.einsum("jrvl,ro->vljo", imag_part, sine_table, preferred_element_type=jnp.float32)


def adjoint_fourier(grid_field, factor, cosine_table, sine_table):
    real_part = (
        jnp.einsum("vljo,ro->jrvl", grid_field, cosine_table, preferred_element_type=jnp.float32)
        * factor[None, :, None, None]
    )
    imag_part = (
        -jnp.einsum("vljo,ro->jrvl", grid_field, sine_table, preferred_element_type=jnp.float32)
        * factor[None, :, None, None]
    )
    stacked = jnp.stack([real_part, imag_part], axis=2).astype(jnp.bfloat16)
    return stacked.reshape(stacked.shape[0], -1)


def network_grads(features, tangent, w_in, w_out, bias):
    preact = jnp.dot(w_in.T, features, preferred_element_type=jnp.float32) + bias[:, None]
    logistic = jax.nn.sigmoid(preact)
    hidden = (preact * logistic).astype(jnp.bfloat16)
    hidden_grad = jnp.dot(w_out, tangent, preferred_element_type=jnp.float32)
    preact_grad = hidden_grad * (logistic * (1.0 + preact * (1.0 - logistic)))
    preact_low = preact_grad.astype(jnp.bfloat16)
    out_grad = lax.dot_general(
        hidden, tangent, (((1,), (1,)), ((), ())), preferred_element_type=jnp.float32
    )
    in_grad = lax.dot_general(
        features, preact_low, (((1,), (1,)), ((), ())), preferred_element_type=jnp.float32
    )
    bias_grad = jnp.sum(preact_grad, axis=1)
    column_grad = jnp.dot(w_in, preact_low, preferred_element_type=jnp.float32)
    return (in_grad, out_grad, bias_grad, column_grad)


def shards(checkpoints, final_cot, obs_cot, obs_time, wave_order, legendre, w_in, w_out, bias):
    level_count = lax.axis_size("lev")
    local_waves = legendre.shape[0]
    wave_count = wave_order.shape[0]
    lat_count = legendre.shape[1]
    field_count = final_cot.shape[0]
    local_levels = final_cot.shape[1]
    all_levels = local_levels * level_count
    local_lat = obs_cot.shape[3]
    local_lon = obs_cot.shape[4]
    lon_count = local_lon * level_count
    step_count = checkpoints.shape[0]
    row_start = lax.axis_index(BAND) * local_waves
    my_waves = lax.dynamic_slice_in_dim(wave_order, row_start, local_waves)
    degrees = jnp.arange(wave_count, dtype=jnp.int32)
    upper_mask = degrees[None, None, :] >= my_waves[:, None, None]
    masked = jnp.where(upper_mask, legendre, jnp.zeros_like(legendre))
    cosine_table, sine_table = tables(wave_order, lon_count)
    weight_m = jnp.where(wave_order == 0, 1.0, 2.0).astype(jnp.float32)
    inverse_lon = jnp.full((wave_count,), 1.0 / lon_count, jnp.float32)
    degree_float = degrees.astype(jnp.float32)
    damping = 1.0 / (1.0 + 2.0 * degree_float * (degree_float + 1.0) / (wave_count * wave_count))
    feature_count = field_count * all_levels
    column_count = local_lat * local_lon
    state_sums = jnp.stack(
        [synth_legendre(masked, checkpoints[step]) for step in range(step_count)], axis=2
    )
    state_sums = state_sums.reshape(lat_count, -1)
    state_rows = two_step_exchange(state_sums, (("band_0", "band_1"), "band_2"), (1, 0), 0, 1)
    state_rows = state_rows.reshape(local_lat, wave_count, step_count, 2, field_count, local_levels)
    state_grids = jnp.stack(
        [
            synth_fourier(state_rows[:, :, step], weight_m, cosine_table, sine_table).astype(
                jnp.bfloat16
            )
            for step in range(step_count)
        ]
    )
    state_columns = lax.all_to_all(state_grids, "lev", split_axis=4, concat_axis=2, tiled=True)
    adjoint = final_cot
    grad_w_in = jnp.zeros((feature_count, w_in.shape[1]), jnp.float32)
    grad_w_out = jnp.zeros((w_in.shape[1], feature_count), jnp.float32)
    grad_bias = jnp.zeros((w_in.shape[1],), jnp.float32)
    for step in reversed(range(step_count)):
        damped = damping * adjoint
        tangent_sums = synth_legendre(masked, dt_scale * damped).reshape(lat_count, -1)
        tangent_rows = two_step_exchange(
            tangent_sums, (("band_0", "band_1"), "band_2"), (0, 1), 0, 1
        )
        tangent_rows = tangent_rows.reshape(local_lat, wave_count, 2, field_count, local_levels)
        tangent_grid = synth_fourier(tangent_rows, inverse_lon, cosine_table, sine_table).astype(
            jnp.bfloat16
        )
        tangent_cols = lax.all_to_all(tangent_grid, "lev", split_axis=3, concat_axis=1, tiled=True)
        features = state_columns[step].reshape(feature_count, column_count)
        tangent = tangent_cols.reshape(feature_count, column_count)
        in_grad, out_grad, bias_grad, column_grad = network_grads(
            features, tangent, w_in, w_out, bias
        )
        in_grad, out_grad, bias_grad = packed_total((in_grad, out_grad, bias_grad), BAND_LEV)
        grad_w_in = grad_w_in + in_grad
        grad_w_out = grad_w_out + out_grad
        grad_bias = grad_bias + bias_grad
        obs_weight = (obs_time == step).astype(jnp.float32)
        column_grad = column_grad.reshape(field_count, all_levels, local_lat, local_lon)
        column_grad = column_grad + jnp.einsum("i,ivljo->vljo", obs_weight, obs_cot)
        level_grad = lax.all_to_all(
            column_grad.astype(jnp.bfloat16), "lev", split_axis=1, concat_axis=3, tiled=True
        )
        back_rows = adjoint_fourier(level_grad, weight_m, cosine_table, sine_table)
        back_local = lax.all_to_all(back_rows, BAND, split_axis=1, concat_axis=0, tiled=True)
        back_local = back_local.reshape(lat_count, local_waves, 2, field_count, local_levels)
        adjoint = damped + jnp.einsum(
            "rjn,jrcvl->vlcrn", masked, back_local, preferred_element_type=jnp.float32
        )
    return (adjoint, grad_w_in, grad_w_out, grad_bias)


def solution(mesh):
    torus = Mesh(
        mesh.devices.reshape(4, 4, 2, mesh.shape["lev"]), ("band_0", "band_1", "band_2", "lev")
    )
    placed = (
        P(None, None, "lev", None, BAND, None),
        P(None, "lev", None, BAND, None),
        P(None, None, None, BAND, "lev"),
        P(),
        P(),
        P(BAND, None, None),
        P(),
        P(),
        P(),
    )
    return jax.shard_map(
        shards,
        mesh=torus,
        in_specs=placed,
        out_specs=(P(None, "lev", None, BAND, None), P(), P(), P()),
        check_vma=False,
    )
```

profile of v0, /device:TPU:1, one launch (start us, length us, event | category | flops | bytes accessed | tf_op | source)
XLA Modules:
  0.0 948.7 jit_solution(14873412488811951413)
XLA Ops:
  12.9 20.2 %copy.168 = bf16[256,8,4,2,4,8]{5,4,3,2,1,0:T(4,128)(2,1)} copy(bf16[256,8,4,2,4,8]{0,5,3,4,1,2:T(8,128)(2,1)S(1)} %pad_maximum_fusion) | data formatting | bytes 2097152 | tf_op jit(solution)/shard_map/stack | solution.py:129
  33.1 24.5 %reshape_reshape_reshape.16 = bf16[16,2,8,2048]{3,2,1,0:T(8,128)(2,1)S(1)} reshape(bf16[256,8,4,2,4,8]{5,4,3,2,1,0:T(4,128)(2,1)} %copy.168) | data formatting | bytes 2097152 | tf_op jit(solution)/shard_map/reshape;reshape;reshape | solution.py:28
  65.5 5.4 copy.159
  70.9 7.7 reshape_reshape_reshape.15
  78.6 7.8 all-to-all-start
  87.5 6.7 all-to-all-done
  94.2 5.3 all_to_all.249
  103.8 6.0 reshape_reshape.15
  124.0 5.3 copy.165
  129.3 6.4 reshape.334
  141.9 20.6 %reshape_reshape.16 = bf16[8,256,4,2,4,8]{5,4,3,2,1,0:T(4,128)(2,1)} reshape(bf16[8,32,2048]{2,1,0:T(8,128)(2,1)S(1)} %copy.171) | data formatting | bytes 2097152 | tf_op jit(solution)/shard_map/reshape;reshape | solution.py:134
  162.6 10.5 %fusion.354 = (bf16[8,256,1,2,4,8]{5,4,3,2,1,0:T(4,128)(2,1)S(1)}, bf16[8,256,1,2,4,8]{5,4,3,2,1,0:T(4,128)(2,1)S(1)}, bf16[8,256,2,4,8]{4,3,2,1,0:T(4,128)(2,1)S(1)}, bf16[8,256,1,2,4,8]{5,4,3,2,1,0:T(4,128)(2,1)}) fusion(bf16[8,256,4,2,4,8]{5,4,3,2,1,0:T(4,128)(2,1)} %reshape_reshape.16), kind=kLoop, calls=%fused_computation.434 | loop fusion | bytes 2097152 | tf_op jit(solution)/shard_map/slice | solution.py:137
  180.0 9.9 %fusion.14 = (bf16[8,256,4,8]{3,2,1,0:T(4,128)(2,1)}, bf16[8,256,4,8]{3,2,1,0:T(4,128)(2,1)}, bf16[8,256,4,8]{3,2,1,0:T(4,128)(2,1)}, bf16[8,256,4,8]{3,2,1,0:T(...) fusion(bf16[8,256,2,4,8]{4,3,1,0,2:T(4,128)(2,1)S(1)} %bitcast., ...), kind=kLoop, calls=%fused_computation.29 | loop fusion | flops 524288 | bytes 2097664 | tf_op jit(solution)/shard_map/mul | solution.py:68
  234.9 20.1 %copy.184 = bf16[4,4,8,8,512]{2,1,3,0,4:T(4,128)(2,1)} copy(bf16[4,4,8,8,512]{4,2,1,3,0:T(8,128)(2,1)S(1)} %pad_maximum_fusion.1) | data formatting | bytes 2097152 | tf_op jit(solution)/shard_map/stack | solution.py:135
  255.0 21.2 %reshape.332 = bf16[4,2,65536]{2,1,0:T(2,128)(2,1)} reshape(bf16[512,4,8,4,8]{4,3,2,1,0:T(4,128)(2,1)} %bitcast.649) | data formatting | bytes 2097152
  283.0 6.0 reshape.335
  289.0 6.7 copy.166
  295.7 21.7 %reshape.333 = bf16[512,4,8,4,8]{4,3,2,1,0:T(4,128)(2,1)} reshape(bf16[4,2,65536]{2,1,0:T(2,128)(2,1)S(1)} %all-to-all-done.5) | data formatting | bytes 2097152
  317.5 20.9 %copy.185 = bf16[4,4,8,8,4,128]{5,3,2,4,1,0:T(8,128)(2,1)S(1)} copy(bf16[4,4,8,8,4,128]{2,1,3,0,5,4:T(4,128)(2,1)} %bitcast.650) | data formatting | bytes 2097152 | tf_op jit(solution)/shard_map/all_to_all | solution.py:143
  362.8 7.1 convert_element_type.248
  370.7 10.6 %all-to-all-start.7 = ((bf16[8,32,512]{2,0,1:T(8,128)(2,1)}), bf16[8,32,512]{2,0,1:T(8,128)(2,1)S(1)}, u32[]{:S(2)}, u32[]{:S(2)}) async-start(bf16[8,32,512]{2,0,1:T(8,128)(2,1)} %copy.191), calls=%async_computation.7 | async-start | bytes 524288 | tf_op jit(solution)/shard_map/all_to_all | solution.py:175
  383.6 6.6 all-to-all-done.7
  390.2 5.9 reshape.328
  396.1 6.2 fusion.360
  402.7 5.4 copy.194
  408.2 7.7 reshape_reshape_reshape.17
  421.6 5.6 all-to-all-done.8
  427.2 5.6 all_to_all.250
  432.9 6.0 reshape_reshape.17
  451.0 5.3 copy.200
  456.3 6.4 reshape.336
  466.9 5.6 all-to-all-done.10
  472.4 6.0 reshape.337
  478.4 6.7 copy.201
  505.8 7.1 convert_element_type.256
  513.7 6.9 all-to-all-start.12
  521.5 8.0 all-to-all-done.12
  529.5 5.9 reshape.329
  535.4 5.6 fusion.361
  541.5 5.4 copy.210
  546.9 7.7 reshape_reshape_reshape.18
  560.0 6.0 all-to-all-done.13
  571.3 6.0 reshape_reshape.18
  594.0 5.3 copy.216
  599.3 6.4 reshape.338
  615.4 6.0 reshape.339
  621.3 6.1 copy.217
  652.3 7.1 convert_element_type.264
  660.2 6.9 all-to-all-start.17
  668.4 7.6 all-to-all-done.17
  676.0 5.9 reshape.330
  681.9 5.6 fusion.362
  688.0 5.4 copy.226
  693.4 7.8 reshape_reshape_reshape.19
  706.3 6.3 all-to-all-done.18
  717.9 6.0 reshape_reshape.19
  736.8 5.3 copy.232
  742.1 6.5 reshape.340
  758.2 6.0 reshape.341
  764.1 6.1 copy.233
  792.7 7.1 convert_element_type.272
  800.0 15.7 %all_to_all.253 = bf16[8,32,512]{2,0,1:T(8,128)(2,1)S(1)} all-to-all(bf16[8,32,512]{2,0,1:T(8,128)(2,1)S(1)} %copy.239), channel_id=1, replica_groups=mesh['band_0'=4,'band_1'=4,'band_2'=2,'lev'=4] {'band_0','band_1','band_2'}, dimensions={1} | all-to-all | bytes 524288 | tf_op jit(solution)/shard_map/all_to_all | solution.py:175
  815.8 5.9 reshape.331
  827.9 109.5 %all-reduce.3.cloned.1.call-done = (f32[131584]{0:T(1024)}, f32[131584]{0:T(1024)}, f32[131584]{0:T(1024)}, f32[131584]{0:T(1024)}) async-done(((f32[131584]{0:T(1024)}, f32[131584]{0:T(1024)}, f32[131584]{0:T(1024)}, f32[131584]{0:T(1024)}), (f32[131584]{0:T(1024)}, f32[131584]{0:T(1024)}, f32[131584]{0:T(1024)}, f32[131584]{0:T(1024)})) %all-reduce.3.cloned.1.call-update) | async-done | bytes 2105360 | tf_op jit(solution)/shard_map/psum | solution.py:44
  (302 shorter events, 300.6 us)
Async XLA Ops:
  7.2 273.6 %copy-start = (f32[4,4,32,8,128]{4,3,2,1,0:T(8,128)S(1)}, f32[4,4,32,8,128]{4,3,2,1,0:T(8,128)}, u32[]{:S(2)}) copy-start(f32[4,4,32,8,128]{4,3,2,1,0:T(8,128)} %param.11) | copy-start | bytes 6291460
  7.2 3.7 copy-start.38
  58.6 20.0 %all-to-all-start.3 = ((bf16[16,2,8,2048]{3,2,0,1:T(8,128)(2,1)}), bf16[16,2,8,2048]{3,2,0,1:T(8,128)(2,1)S(1)}, u32[]{:S(2)}, u32[]{:S(2)}) async-start(bf16[16,2,8,2048]{3,2,0,1:T(8,128)(2,1)} %copy.169), calls=%async_computation.3 | async-start | bytes 2097152 | tf_op jit(solution)/shard_map/all_to_all | solution.py:30
  63.6 7.3 copy-start.52
  78.6 8.9 copy-start.33
  78.6 15.6 %all-to-all-start = ((bf16[16,2,8,512]{3,2,1,0:T(8,128)(2,1)}), bf16[16,2,8,512]{3,2,1,0:T(8,128)(2,1)S(1)}, u32[]{:S(2)}, u32[]{:S(2)}) async-start(bf16[16,2,8,512]{3,2,1,0:T(8,128)(2,1)} %reshape_reshape_reshape.15), calls=%async_computation | async-start | bytes 524288 | tf_op jit(solution)/shard_map/all_to_all | solution.py:30
  87.5 269.6 %copy-start.34 = (f32[256]{0:T(256)}, f32[256]{0:T(256)S(1)}, u32[]{:S(2)}) copy-start(f32[256]{0:T(256)S(1)} %get-tuple-element.50) | copy-start | bytes 3076
  99.5 36.3 %all-to-all-start.4 = ((bf16[16,2,8,2048]{3,2,1,0:T(8,128)(2,1)}), bf16[16,2,8,2048]{3,2,1,0:T(8,128)(2,1)S(1)}, u32[]{:S(2)}, u32[]{:S(2)}) async-start(bf16[16,2,8,2048]{3,2,1,0:T(8,128)(2,1)} %copy.170), calls=%async_computation.4 | async-start | bytes 2097152 | tf_op jit(solution)/shard_map/all_to_all | solution.py:30
  135.8 4.4 copy-start.5
  135.8 140.5 %all-to-all-start.2 = ((bf16[4,2,16384]{2,1,0:T(2,128)(2,1)}), bf16[4,2,16384]{2,1,0:T(2,128)(2,1)S(1)}, u32[]{:S(2)}, u32[]{:S(2)}) async-start(bf16[4,2,16384]{2,1,0:T(2,128)(2,1)} %reshape.334), calls=%async_computation.2 | async-start | bytes 524288 | tf_op jit(solution)/shard_map/all_to_all | solution.py:158
  231.4 2.4 copy-start.18
  231.4 2.5 copy-start.20
  231.4 2.5 copy-start.21
  276.3 4.6 copy-start.50
  276.3 19.5 %all-to-all-start.5 = ((bf16[4,2,65536]{2,1,0:T(2,128)(2,1)}), bf16[4,2,65536]{2,1,0:T(2,128)(2,1)S(1)}, u32[]{:S(2)}, u32[]{:S(2)}) async-start(bf16[4,2,65536]{2,1,0:T(2,128)(2,1)} %reshape.332), calls=%async_computation.5 | async-start | bytes 2097152 | tf_op jit(solution)/shard_map/all_to_all | solution.py:143
  345.0 10.0 %all-to-all-start.6 = ((bf16[4,32,8,128]{3,2,0,1:T(8,128)(2,1)}), bf16[4,32,8,128]{3,2,0,1:T(8,128)(2,1)S(1)}, u32[]{:S(2)}, u32[]{:S(2)}) async-start(bf16[4,32,8,128]{3,2,0,1:T(8,128)(2,1)} %copy.187), calls=%async_computation.6 | async-start | bytes 524288 | tf_op jit(solution)/shard_map/all_to_all | solution.py:171
  362.8 18.5 %copy-start.51 = (s32[4]{0:T(128)S(1)}, s32[4]{0:T(128)}, u32[]{:S(2)}) copy-start(s32[4]{0:T(128)} %param.12) | copy-start | bytes 52
  370.7 19.5 %all-to-all-start.7 = ((bf16[8,32,512]{2,0,1:T(8,128)(2,1)}), bf16[8,32,512]{2,0,1:T(8,128)(2,1)S(1)}, u32[]{:S(2)}, u32[]{:S(2)}) async-start(bf16[8,32,512]{2,0,1:T(8,128)(2,1)} %copy.191), calls=%async_computation.7 | async-start | bytes 524288 | tf_op jit(solution)/shard_map/all_to_all | solution.py:175
  390.2 5.9 copy-start.43
  390.2 5.9 copy-start.53
  396.1 6.2 copy-start.39
  415.8 11.4 %all-to-all-start.8 = ((bf16[16,2,8,512]{3,2,1,0:T(8,128)(2,1)}), bf16[16,2,8,512]{3,2,1,0:T(8,128)(2,1)S(1)}, u32[]{:S(2)}, u32[]{:S(2)}) async-start(bf16[16,2,8,512]{3,2,1,0:T(8,128)(2,1)} %reshape_reshape_reshape.17), calls=%async_computation.8 | async-start | bytes 524288 | tf_op jit(solution)/shard_map/all_to_all | solution.py:30
  456.3 10.0 %copy-start.8 = (bf16[1,4,4,8,8,128]{5,4,3,2,1,0:T(8,128)(2,1)S(1)}, bf16[1,4,4,8,8,128]{5,4,3,2,1,0:T(8,128)(2,1)}, u32[]{:S(2)}) copy-start(bf16[1,4,4,8,8,128]{5,4,3,2,1,0:T(8,128)(2,1)} %get-tuple-element.48) | copy-start | bytes 786436
  462.8 9.6 %all-to-all-start.10 = ((bf16[4,2,16384]{2,1,0:T(2,128)(2,1)}), bf16[4,2,16384]{2,1,0:T(2,128)(2,1)S(1)}, u32[]{:S(2)}, u32[]{:S(2)}) async-start(bf16[4,2,16384]{2,1,0:T(2,128)(2,1)} %reshape.336), calls=%async_computation.10 | async-start | bytes 524288 | tf_op jit(solution)/shard_map/all_to_all | solution.py:158
  466.8 18.3 %copy-start.12 = (f32[1024,512]{1,0:T(8,128)}, f32[1024,512]{1,0:T(8,128)S(1)}, u32[]{:S(2)}) copy-start(f32[1024,512]{1,0:T(8,128)S(1)} %fusion.167) | copy-start | bytes 6291460
  487.6 4.8 copy-start.26
  489.0 8.9 all-to-all-start.11
  492.4 3.2 copy-start.4
  492.4 3.2 copy-start.11
  505.8 14.9 %copy-start.31 = (f32[65536]{0:T(1024)S(1)}, f32[65536]{0:T(1024)}, u32[]{:S(2)}) copy-start(f32[65536]{0:T(1024)} %convolution_bitcast_fusion.3) | copy-start | bytes 786436
  513.7 15.7 %all-to-all-start.12 = ((bf16[8,32,512]{2,0,1:T(8,128)(2,1)}), bf16[8,32,512]{2,0,1:T(8,128)(2,1)S(1)}, u32[]{:S(2)}, u32[]{:S(2)}) async-start(bf16[8,32,512]{2,0,1:T(8,128)(2,1)} %copy.207), calls=%async_computation.12 | async-start | bytes 524288 | tf_op jit(solution)/shard_map/all_to_all | solution.py:175
  529.5 6.0 copy-start.40
  529.5 6.0 copy-start.54
  529.5 6.0 copy-start.57
  546.9 11.3 %copy-start.6 = (bf16[1,4,4,8,8,128]{5,4,3,2,1,0:T(8,128)(2,1)S(1)}, bf16[1,4,4,8,8,128]{5,4,3,2,1,0:T(8,128)(2,1)}, u32[]{:S(2)}) copy-start(bf16[1,4,4,8,8,128]{5,4,3,2,1,0:T(8,128)(2,1)} %get-tuple-element.47) | copy-start | bytes 786436
  554.6 11.4 %all-to-all-start.13 = ((bf16[16,2,8,512]{3,2,1,0:T(8,128)(2,1)}), bf16[16,2,8,512]{3,2,1,0:T(8,128)(2,1)S(1)}, u32[]{:S(2)}, u32[]{:S(2)}) async-start(bf16[16,2,8,512]{3,2,1,0:T(8,128)(2,1)} %reshape_reshape_reshape.18), calls=%async_computation.13 | async-start | bytes 524288 | tf_op jit(solution)/shard_map/all_to_all | solution.py:30
  590.7 3.2 copy-start.23
  605.7 9.6 %all-to-all-start.15 = ((bf16[4,2,16384]{2,1,0:T(2,128)(2,1)}), bf16[4,2,16384]{2,1,0:T(2,128)(2,1)S(1)}, u32[]{:S(2)}, u32[]{:S(2)}) async-start(bf16[4,2,16384]{2,1,0:T(2,128)(2,1)} %reshape.338), calls=%async_computation.15 | async-start | bytes 524288 | tf_op jit(solution)/shard_map/all_to_all | solution.py:158
  621.3 6.1 copy-start.45
  621.3 6.1 copy-start.48
  627.4 2.7 copy-start.28
  630.9 6.0 copy-start.27
  632.8 9.6 %all-to-all-start.16 = ((bf16[4,32,8,128]{3,2,0,1:T(8,128)(2,1)}), bf16[4,32,8,128]{3,2,0,1:T(8,128)(2,1)}, u32[]{:S(2)}, u32[]{:S(2)}) async-start(bf16[4,32,8,128]{3,2,0,1:T(8,128)(2,1)} %copy.219), calls=%async_computation.16 | async-start | bytes 524288 | tf_op jit(solution)/shard_map/all_to_all | solution.py:171
  636.9 3.1 copy-start.9
  640.0 2.5 copy-start.36
  652.3 14.9 %copy-start.32 = (f32[65536]{0:T(1024)S(1)}, f32[65536]{0:T(1024)}, u32[]{:S(2)}) copy-start(f32[65536]{0:T(1024)} %convolution_bitcast_fusion.2) | copy-start | bytes 786436
  659.4 8.6 copy-start.7
  660.2 15.7 %all-to-all-start.17 = ((bf16[8,32,512]{2,0,1:T(8,128)(2,1)}), bf16[8,32,512]{2,0,1:T(8,128)(2,1)S(1)}, u32[]{:S(2)}, u32[]{:S(2)}) async-start(bf16[8,32,512]{2,0,1:T(8,128)(2,1)} %copy.223), calls=%async_computation.17 | async-start | bytes 524288 | tf_op jit(solution)/shard_map/all_to_all | solution.py:175
  676.0 6.0 copy-start.41
  676.0 6.0 copy-start.55
  676.0 6.0 copy-start.56
  693.4 11.4 %copy-start.15 = (f32[1024,512]{1,0:T(8,128)S(1)}, f32[1024,512]{1,0:T(8,128)}, u32[]{:S(2)}) copy-start(f32[1024,512]{1,0:T(8,128)} %fusion.162) | copy-start | bytes 6291460
  693.4 11.4 %copy-start.29 = (bf16[4,8,8,4,128]{4,2,1,3,0:T(8,128)(2,1)S(1)}, bf16[4,8,8,4,128]{4,2,1,3,0:T(8,128)(2,1)}, u32[]{:S(2)}) copy-start(bf16[4,8,8,4,128]{4,2,1,3,0:T(8,128)(2,1)} %copy-done.28) | copy-start | bytes 786436
  693.4 11.4 %copy-start.49 = (f32[512]{0:T(512)S(1)}, f32[512]{0:T(512)}, u32[]{:S(2)}) copy-start(f32[512]{0:T(512)} %param.17) | copy-start | bytes 6148
  701.2 11.4 %all-to-all-start.18 = ((bf16[16,2,8,512]{3,2,1,0:T(8,128)(2,1)}), bf16[16,2,8,512]{3,2,1,0:T(8,128)(2,1)S(1)}, u32[]{:S(2)}, u32[]{:S(2)}) async-start(bf16[16,2,8,512]{3,2,1,0:T(8,128)(2,1)} %reshape_reshape_reshape.19), calls=%async_computation.18 | async-start | bytes 524288 | tf_op jit(solution)/shard_map/all_to_all | solution.py:30
  742.1 10.0 %copy-start.30 = (f32[65536]{0:T(1024)S(1)}, f32[65536]{0:T(1024)}, u32[]{:S(2)}) copy-start(f32[65536]{0:T(1024)} %convolution_bitcast_fusion.1) | copy-start | bytes 786436
  748.5 9.6 %all-to-all-start.20 = ((bf16[4,2,16384]{2,1,0:T(2,128)(2,1)}), bf16[4,2,16384]{2,1,0:T(2,128)(2,1)S(1)}, u32[]{:S(2)}, u32[]{:S(2)}) async-start(bf16[4,2,16384]{2,1,0:T(2,128)(2,1)} %reshape.340), calls=%async_computation.20 | async-start | bytes 524288 | tf_op jit(solution)/shard_map/all_to_all | solution.py:158
  764.1 6.1 copy-start.46
  770.3 2.7 copy-start.13
  775.2 9.7 %copy-start.37 = (f32[256]{0:T(256)S(1)}, f32[256]{0:T(256)}, u32[]{:S(2)}) copy-start(f32[256]{0:T(256)} %copy-done.34) | copy-start | bytes 3076
  775.9 8.9 all-to-all-start.21
  779.3 158.0 %all-reduce.3.cloned.1.call-start = ((), (), s32[]{:S(2)}) async-start(), calls=%async_computation.23 | async-start | bytes 4227072 | tf_op jit(solution)/shard_map/psum | solution.py:44
  815.8 5.9 copy-start.42
  821.7 120.0 %copy-start.1 = (f32[4,4,32,8,128]{4,3,2,1,0:T(8,128)S(1)}, f32[4,4,32,8,128]{4,3,2,1,0:T(8,128)}, u32[]{:S(2)}) copy-start(f32[4,4,32,8,128]{4,3,2,1,0:T(8,128)} %param.11) | copy-start | bytes 6291460
  (13 other events, 18.9 us)
Sparse Core Ops, SparseCore 0:
  785.6 151.6 all-reduce.2
where the time goes:
time: 959 us; the launch traced here: 949 us
  local copies, waits for them, and re-layouts  483 us (50%)
  waiting for transfers between devices  183 us (19%)
  matrix products  121 us (13%)
  starting transfers between devices  86.9 us (9%)
  blocking collectives  37 us (4%)
  other arithmetic  22.7 us (2%)
  between operations  15.5 us (2%)
    unnamed x145, local copies, waits for them, and re-layouts  120 us
    psum x1, waiting for transfers between devices, packed_total(): total = lax.psum(jnp.concatenate([a.ravel() for a in arrays]), axis)  109 us
    another operation x6, local copies, waits for them, and re-layouts, turned_blocks(): parts = parts.reshape(*lengths, *parts.shape[1:])  56.4 us
    unnamed x16, matrix products  40.6 us
    convert_element_type x8, local copies, waits for them, and re-layouts, adjoint_fourier(): stacked = jnp.stack([real_part, imag_part], axis=2).astype(jnp.bfloat16)  31.1 us
    all_to_all x6, starting transfers between devices, turned_blocks(): lax.all_to_all(parts, axes[k], split_axis=k, concat_axis=k, tiled=True)  27.6 us
    all_to_all x4, local copies, waits for them, and re-layouts, shards(): lax.all_to_all(tangent_grid, 'lev', split_axis=3, concat_axis=1, tiled=True)  25.7 us
    all_to_all x6, waiting for transfers between devices, turned_blocks(): lax.all_to_all(parts, axes[k], split_axis=k, concat_axis=k, tiled=True)  24.6 us
  transfers between devices with their start and end apart: 19, of which 15 were waited for; matrix products, arithmetic and copies ran while one was open for 26% of the time, Pallas kernels for 0%

commit v1 on v0

v1 whole, which is shorter than its diff:
```python
import functools

import jax
import jax.numpy as jnp
import numpy as np
from jax import lax
from jax.experimental import pallas as pl
from jax.experimental.pallas import tpu as pltpu
from jax.sharding import Mesh
from jax.sharding import PartitionSpec as P

BAND = ("band_0", "band_1", "band_2")
ALL = ("band_0", "band_1", "band_2", "lev")
F32 = jnp.float32
BF16 = jnp.bfloat16

RHO = 8
N = 256
LON = 512
FEAT = 128
HID = 512
STEPS = 4
VL = 32
DEV = 128


def mm(a, b):
    return jnp.dot(a, b, preferred_element_type=F32)


def mm_nt(a, b):
    return lax.dot_general(a, b, (((1,), (1,)), ((), ())), preferred_element_type=F32)


def lane_of(rows, lanes):
    return lax.broadcasted_iota(jnp.int32, (rows, lanes), 1)


def damping_row():
    n = lane_of(1, N).astype(F32)
    return 1.0 / (1.0 + 2.0 * n * (n + 1.0) / (N * N))


def halve(ref, halves):
    for h in range(2):
        halves[h] = ref[:, h * 128 : (h + 1) * 128]


def strided_rows(halves, rho):
    return jnp.concatenate(
        [
            jnp.concatenate(
                [halves[h, pl.ds(p * RHO + rho, VL, stride=2 * RHO), :] for h in range(2)], axis=1
            )
            for p in range(2)
        ],
        axis=0,
    )


def tangent_scale(m):
    return jnp.where(m == 0, 1.0 / LON, 0.5 / LON).astype(F32)


def synth_rho(table, tangent, state, rho, rows_t, rows_s):
    parts = []
    for s in (tangent, state):
        s = s.astype(BF16)
        parts += [s[:VL], s[:VL], s[VL:], s[VL:]]
    sums = mm_nt(table, jnp.concatenate(parts, axis=0))
    even = (lane_of(DEV, 2 * DEV) // VL) % 2 == 0
    both = jnp.where(even, sums[:DEV], sums[DEV:])
    rows_t[pl.ds(rho, DEV, stride=RHO), :] = both[:, :DEV]
    rows_s[pl.ds(rho, DEV, stride=RHO), :] = both[:, DEV:]


def write_chunks(send, rows_t, rows_s):
    send[:, 0] = rows_t[...].reshape(DEV, RHO, 128).astype(BF16)
    send[:, 1] = rows_s[...].reshape(DEV, RHO, 128).astype(BF16)


def first_kernel(
    waves, legendre, final, state, send, damped, table, tall, rows_t, rows_s, final_rows, state_rows
):
    damping = damping_row()
    halve(final, final_rows)
    halve(state.at[0], state_rows)
    degree = lane_of(N, N)
    for rho in range(RHO):
        m = waves[rho]
        kept = jnp.where(degree >= m, legendre[rho].astype(F32), 0.0)
        for h in range(2):
            tall[h] = kept[:, h * 128 : (h + 1) * 128]
        for jj in range(2):
            for h in range(2):
                part = tall[h, pl.ds(jj, DEV, stride=2), :].astype(BF16)
                table[rho, jj * DEV : (jj + 1) * DEV, h * 128 : (h + 1) * 128] = part
        now = damping * strided_rows(final_rows, rho)
        damped[rho] = now
        synth_rho(
            table[rho], now * tangent_scale(m), strided_rows(state_rows, rho), rho, rows_t, rows_s
        )
    write_chunks(send, rows_t, rows_s)


def adjoint_rho(rows, table, rho):
    back = rows[pl.ds(rho, DEV, stride=RHO), :].T
    halves = []
    for p in range(2):
        at = 2 * p * VL
        halves.append(jnp.concatenate([back[at : at + VL], back[at + VL : at + 2 * VL]], axis=1))
    return mm(jnp.concatenate(halves, axis=0).astype(BF16), table)


def turn_kernel(waves, back, damped_in, table, state, send, damped, rows, rows_t, rows_s, state_rows):
    damping = damping_row()
    halve(state.at[0], state_rows)
    rows[...] = back[...].astype(F32).reshape(DEV * RHO, 128)
    for rho in range(RHO):
        now = damping * (damped_in[rho] + adjoint_rho(rows, table[rho], rho))
        damped[rho] = now
        synth_rho(
            table[rho],
            now * tangent_scale(waves[rho]),
            strided_rows(state_rows, rho),
            rho,
            rows_t,
            rows_s,
        )
    write_chunks(send, rows_t, rows_s)


def last_kernel(back, damped_in, table, out, rows, out_rows):
    rows[...] = back[:, 0].astype(F32).reshape(DEV * RHO, 128)
    for rho in range(RHO):
        now = damped_in[rho] + adjoint_rho(rows, table[rho], rho)
        for p in range(2):
            for h in range(2):
                part = now[p * VL : (p + 1) * VL, h * 128 : (h + 1) * 128]
                out_rows[h, pl.ds(p * RHO + rho, VL, stride=2 * RHO), :] = part
    for h in range(2):
        out[:, h * 128 : (h + 1) * 128] = out_rows[h]


def share_kernel(back, bias_part, send):
    total = jnp.sum(back[:, 1].astype(F32), axis=0)
    send[:, 0] = jnp.broadcast_to(total[None], (DEV, 8, 128)).astype(BF16)
    send[:, 1] = jnp.broadcast_to(bias_part[...][None], (DEV, 8, 128)).astype(BF16)


def ending_kernel(parts, w_in_out, w_out_out, bias_out):
    rows = parts[:, 0].astype(F32).reshape(2 * HID, 128)
    w_in_out[...] = rows[:HID].T
    w_out_out[...] = rows[HID:]
    total = jnp.sum(parts[:, 1].astype(F32), axis=0)
    bias_out[...] = total[:4] + total[4:]


def tables_kernel(waves, base, w_in, bias, trig, w_in_t, bias_wide):
    m = lax.broadcasted_iota(jnp.int32, (N, N), 0)
    weight = jnp.where(m == 0, 1.0, 2.0).astype(F32)
    pick = jnp.where(m == waves[...], weight, 0.0).T.astype(BF16)
    both = mm(pick, base[...]).astype(BF16)
    trig[:N] = both[:, :LON]
    trig[N:] = both[:, LON:]
    w_in_t[...] = w_in[...].astype(F32).T.astype(BF16)
    bias_wide[...] = jnp.broadcast_to(bias[...], (128, HID)).T


def obs_kernel(obs_time, obs, out):
    for j in range(8):
        pieces = [obs[i, pl.ds(j, FEAT, stride=8), :] for i in range(4)]
        for step in range(STEPS):
            total = jnp.zeros((FEAT, 128), F32)
            for i in range(4):
                total += jnp.where(obs_time[i] == step, 1.0, 0.0).astype(F32) * pieces[i]
            out[j // 2, step, j % 2] = total.astype(BF16)


def column_kernel(first, last, *refs):
    got, trig, w_in, w_in_t, w_out, bias, obs = refs[:7]
    refs = refs[7:]
    if not first:
        acc_in, accb_in = refs[:2]
        refs = refs[2:]
    send = refs[0]
    if last:
        bias_part = refs[1]
        acc, accb, turned, grid, grads = refs[2:]
    else:
        acc, accb, turned, grid, grads = refs[1:]
    for kind in range(2):
        for y in range(4):
            x = got[:, y, kind].astype(F32).reshape(N, 128).T.astype(BF16)
            for p in range(2):
                for jj in range(2):
                    at = (2 * p + jj) * VL
                    turned[kind, jj, y * VL : (y + 1) * VL, p * N : (p + 1) * N] = x[at : at + VL]
    for kind in range(2):
        for jj in range(2):
            g = mm(turned[kind, jj], trig[...])
            g = jnp.concatenate(
                [g[(y * 4 + v) * 8 : (y * 4 + v + 1) * 8] for v in range(4) for y in range(4)], axis=0
            ).astype(BF16)
            for half in range(2):
                grid[kind, 2 * jj + half] = g[:, half * 256 : (half + 1) * 256]
    if first:
        acc[...] = jnp.zeros_like(acc)
        accb[...] = jnp.zeros_like(accb)
    else:
        acc[...] = acc_in[...]
        accb[...] = accb_in[...]

    def block(cb, carry):
        tangent = grid[0, cb]
        features = grid[1, cb]
        back = jnp.zeros((FEAT, 256), F32)
        for hb in range(2):
            rows = slice(hb * 256, (hb + 1) * 256)
            wide = bias[rows, :]
            pre = mm(w_in_t[rows, :], features) + jnp.concatenate([wide, wide], axis=1)
            logistic = 0.5 * jnp.tanh(0.5 * pre) + 0.5
            hidden = (pre * logistic).astype(BF16)
            pre_grad = mm(w_out[rows, :], tangent) * (logistic * (1.0 + pre * (1.0 - logistic)))
            low = pre_grad.astype(BF16)
            acc[rows, :] += mm_nt(low, features)
            acc[hb * 256 + HID : (hb + 1) * 256 + HID, :] += mm_nt(hidden, tangent)
            accb[rows, :] += pre_grad[:, :128] + pre_grad[:, 128:]
            back += mm(w_in[:, rows], low)
        jj = cb // 2
        half = cb % 2
        seen = jnp.concatenate([obs[2 * half + k, 0, jj] for k in range(2)], axis=1)
        back += seen.astype(F32)
        back = jnp.concatenate(
            [back[(v * 4 + y) * 8 : (v * 4 + y + 1) * 8] for y in range(4) for v in range(4)], axis=0
        )
        grads[jj, half] = back.astype(BF16)
        return carry

    lax.fori_loop(0, 4, block, 0)

    real = (lane_of(N, 2 * 128) // 64) % 2 == 0
    for pair in range(2):
        rows = []
        for y in (2 * pair, 2 * pair + 1):
            for p in range(2):
                for jj in range(2):
                    rows.append(
                        jnp.concatenate(
                            [grads[jj, half, y * VL : (y + 1) * VL, :] for half in range(2)], axis=1
                        )
                    )
        rows = jnp.concatenate(rows, axis=0)
        mixed = jnp.where(real, mm_nt(trig[:N], rows), mm_nt(trig[N:], rows))
        for k in range(2):
            chunk = mixed[:, k * 128 : (k + 1) * 128].reshape(32, 8, 128).astype(BF16)
            if last:
                send[:, 2 * pair + k, 0] = chunk
            else:
                send[:, 2 * pair + k] = chunk
    if last:
        send[:, :, 1] = acc[...].reshape(32, 4, 8, 128).astype(BF16)
        ones = jnp.ones((8, 128), F32)
        sums = lax.dot_general(
            ones,
            accb[...],
            (((1,), (1,)), ((), ())),
            preferred_element_type=F32,
            precision=lax.Precision.HIGHEST,
        )
        for k in range(4):
            part = sums[:1, k * 128 : (k + 1) * 128]
            high = part.astype(BF16).astype(F32)
            bias_part[k : k + 1, :] = high
            bias_part[k + 4 : k + 5, :] = part - high


VMEM = pl.BlockSpec(memory_space=pltpu.VMEM)
SMEM = pl.BlockSpec(memory_space=pltpu.SMEM)


def shape(dims, kind):
    return jax.ShapeDtypeStruct(dims, kind)


def cost(flops, nbytes):
    return pl.CostEstimate(flops=flops, bytes_accessed=nbytes, transcendentals=0)


def state_spec(step):
    return pl.BlockSpec((1, 512, N), lambda i: (step, 0, 0))


def whole(dims):
    return pl.BlockSpec(dims, lambda i: (0,) * len(dims))


def call(body, ins, outs, scratch, in_specs, name, flops, nbytes):
    many = isinstance(outs, (list, tuple))
    outs_list = list(outs) if many else [outs]
    out_specs = [whole(o.shape) for o in outs_list]
    return pl.pallas_call(
        body,
        grid=(1,),
        out_shape=outs_list if many else outs,
        in_specs=in_specs,
        out_specs=out_specs if many else out_specs[0],
        scratch_shapes=scratch,
        cost_estimate=cost(flops, nbytes),
        name=name,
    )(*ins)


def exchange(array, axes):
    return lax.all_to_all(array, axes, split_axis=0, concat_axis=0, tiled=True)


def trig_base():
    phase = (np.arange(N)[:, None] * np.arange(LON)[None, :]) % LON
    angle = 2.0 * np.pi / LON * phase
    return jnp.asarray(np.concatenate([np.cos(angle), -np.sin(angle)], axis=1), BF16)


def shards(checkpoints, final_cot, obs_cot, obs_time, wave_order, legendre, w_in, w_out, bias):
    waves = lax.dynamic_slice_in_dim(wave_order, lax.axis_index(BAND) * RHO, RHO)
    states = checkpoints.reshape(STEPS, 512, N)
    final = final_cot.reshape(512, N)
    seen = obs_cot.reshape(4, FEAT * 8, 128)
    chunks = shape((DEV, 2, RHO, 128), BF16)
    tall = pltpu.VMEM((DEV * RHO, 128), F32)
    halves = pltpu.VMEM((2, 512, 128), F32)

    send, damped, table = call(
        first_kernel,
        (waves, legendre, final, states),
        (chunks, shape((RHO, 64, N), F32), shape((RHO, N, N), BF16)),
        [pltpu.VMEM((2, N, 128), F32), tall, tall, halves, halves],
        [SMEM, whole(legendre.shape), whole(final.shape), state_spec(STEPS - 1)],
        "first",
        300_000_000,
        4_000_000,
    )
    trig, w_in_t, bias_wide = call(
        tables_kernel,
        (wave_order.reshape(1, N), trig_base(), w_in, bias.reshape(1, HID)),
        (shape((2 * N, LON), BF16), shape((HID, FEAT), BF16), shape((HID, 128), F32)),
        [],
        [whole((1, N)), whole((N, 2 * LON)), whole(w_in.shape), whole((1, HID))],
        "tables",
        140_000_000,
        1_500_000,
    )
    obs_parts = call(
        obs_kernel,
        (obs_time, seen),
        shape((4, STEPS, 2, FEAT, 128), BF16),
        [],
        [SMEM, whole(seen.shape)],
        "obs",
        10_000_000,
        3_000_000,
    )
    obs_cols = exchange(obs_parts, ("lev",))

    sums = ()
    for step in reversed(range(STEPS)):
        first = step == STEPS - 1
        last = step == 0
        got = exchange(send, ALL).reshape(32, 4, 2, RHO, 128)
        acc_shapes = [shape((2 * HID, 128), F32), shape((HID, 128), F32)]
        scratch = [
            pltpu.VMEM((2, 2, FEAT, 2 * N), BF16),
            pltpu.VMEM((2, 4, FEAT, 256), BF16),
            pltpu.VMEM((2, 2, FEAT, 256), BF16),
        ]
        if last:
            outs = [shape((32, 4, 2, RHO, 128), BF16), shape((8, 128), F32)]
            scratch = [pltpu.VMEM(a.shape, F32) for a in acc_shapes] + scratch
        else:
            outs = [shape((32, 4, RHO, 128), BF16)] + acc_shapes
        ins = (got, trig, w_in, w_in_t, w_out, bias_wide, obs_cols) + tuple(sums)
        specs = [whole(a.shape) for a in ins]
        specs[6] = pl.BlockSpec((4, 1, 2, FEAT, 128), functools.partial(lambda s, i: (0, s, 0, 0, 0), step))
        back, *sums = call(
            functools.partial(column_kernel, first, last),
            ins,
            outs,
            scratch,
            specs,
            f"columns_{step}",
            1_200_000_000,
            3_000_000,
        )
        if not last:
            back = exchange(back.reshape(DEV, RHO, 128), ALL)
            send, damped = call(
                turn_kernel,
                (waves, back, damped, table, states),
                (chunks, shape((RHO, 64, N), F32)),
                [tall, tall, tall, halves],
                [SMEM, whole(back.shape), whole(damped.shape), whole(table.shape), state_spec(step - 1)],
                f"turn_{step}",
                400_000_000,
                4_000_000,
            )
    back = exchange(back.reshape(DEV, 2, RHO, 128), ALL)
    (bias_part,) = sums
    parts = call(
        share_kernel,
        (back, bias_part),
        chunks,
        [],
        [whole(back.shape), whole(bias_part.shape)],
        "share",
        1_000_000,
        1_000_000,
    )
    parts = exchange(parts, ALL)
    adjoint = call(
        last_kernel,
        (back, damped, table),
        shape((512, N), F32),
        [tall, halves],
        [whole(back.shape), whole(damped.shape), whole(table.shape)],
        "last",
        100_000_000,
        3_000_000,
    )
    grad_w_in, grad_w_out, grad_bias = call(
        ending_kernel,
        (parts,),
        (shape((FEAT, HID), F32), shape((HID, FEAT), F32), shape((4, 128), F32)),
        [],
        [whole(parts.shape)],
        "ending",
        1_000_000,
        1_500_000,
    )
    return (adjoint.reshape(final_cot.shape), grad_w_in, grad_w_out, grad_bias.reshape(HID))


def solution(mesh):
    torus = Mesh(mesh.devices.reshape(4, 4, 2, mesh.shape["lev"]), ("band_0", "band_1", "band_2", "lev"))
    placed = (
        P(None, None, "lev", None, BAND, None),
        P(None, "lev", None, BAND, None),
        P(None, None, None, BAND, "lev"),
        P(),
        P(),
        P(BAND, None, None),
        P(),
        P(),
        P(),
    )
    return jax.shard_map(
        shards,
        mesh=torus,
        in_specs=placed,
        out_specs=(P(None, "lev", None, BAND, None), P(), P(), P()),
        check_vma=False,
    )
```

time: 959 us -> 235 us (0.25)
  local copies, waits for them, and re-layouts: 483 us -> 3.07 us
  waiting for transfers between devices: 183 us -> 34.7 us
  matrix products: 121 us -> 0 us
  blocking collectives: 37 us -> 124 us
  starting transfers between devices: 86.9 us -> 18.6 us
  Pallas kernels: 0 us -> 53.2 us
  other arithmetic: 22.7 us -> 0 us
  between operations: 15.5 us -> 0.68 us
    another operation x17 -> x0, local copies, waits for them, and re-layouts: 155 us -> none  [the longest x6 56.4 us: turned_blocks(): parts = parts.reshape(*lengths, *parts.shape[1:])]
    unnamed x145 -> x6, local copies, waits for them, and re-layouts: 120 us -> 1.8 us
    psum x1 -> x0, waiting for transfers between devices: 109 us -> none  [packed_total(): total = lax.psum(jnp.concatenate([a.ravel() for a in arrays]), axis)]
    all_to_all x5 -> x7, blocking collectives: 37 us -> 124 us  [exchange(): return lax.all_to_all(array, axes, split_axis=0, concat_axis=0, tiled=True)]
    dot_general x44 -> x0, matrix products: 80.6 us -> none  [the longest x4 22.4 us: shards(): jnp.einsum('rjn,jrcvl->vlcrn', masked, back_local, preferred_element_type...]
    convert_element_type x20 -> x0, local copies, waits for them, and re-layouts: 77 us -> none  [the longest x8 31.1 us: adjoint_fourier(): stacked = jnp.stack([real_part, imag_part], axis=2).astype(jnp.bfloat16)]
    all_to_all x18 -> x3, starting transfers between devices: 86.9 us -> 18.6 us  [exchange(): return lax.all_to_all(array, axes, split_axis=0, concat_axis=0, tiled=True)]
    pallas_call x0 -> x13, Pallas kernels: none -> 53.2 us  [call(): pl.pallas_call(body, grid=(1,), out_shape=outs_list if many else outs, in...]
  transfers between devices with their start and end apart: 19 -> 3, of which waited for: 15 -> 3; matrix products, arithmetic and copies ran while one was open for 26% -> 0% of each run, Pallas kernels for 0% -> 4%
where the time goes in v1:
time: 235 us; the launch traced here: 234 us
  blocking collectives  124 us (53%)
  Pallas kernels  53.2 us (23%)
  waiting for transfers between devices  34.7 us (15%)
  starting transfers between devices  18.6 us (8%)
  local copies, waits for them, and re-layouts  3.07 us (1%)
    all_to_all x7, blocking collectives, exchange(): return lax.all_to_all(array, axes, split_axis=0, concat_axis=0, tiled=True)  124 us
    pallas_call x13, Pallas kernels, call(): pl.pallas_call(body, grid=(1,), out_shape=outs_list if many else outs, in...  53.2 us
    all_to_all x3, waiting for transfers between devices, exchange(): return lax.all_to_all(array, axes, split_axis=0, concat_axis=0, tiled=True)  34.7 us
    all_to_all x3, starting transfers between devices, exchange(): return lax.all_to_all(array, axes, split_axis=0, concat_axis=0, tiled=True)  18.6 us
  transfers between devices with their start and end apart: 3, of which 3 were waited for; matrix products, arithmetic and copies ran while one was open for 0% of the time, Pallas kernels for 4%

profile of v1, /device:TPU:1, one launch (start us, length us, event | category | flops | bytes accessed | tf_op | source)
XLA Modules:
  0.0 234.0 jit_solution(4705510283603957424)
XLA Ops:
  0.6 1.3 dynamic_slice.3.waves
  1.9 3.6 %first.1 = (bf16[128,2,8,128]{3,2,1,0:T(8,128)(2,1)}, f32[8,64,256]{2,1,0:T(8,128)}, bf16[8,256,256]{2,1,0:T(8,128)(2,1)}) custom-call(s32[8]{0:T(128)} %dynamic_slice.3.waves, bf16[8,256,256]{2,1,0:T(8,128)(2,1)} %legendre.1, f32[512,256]{1,0:T(8,128)} %bitcast.26, f32[4,512,256]{2,1,0:T(8,128)} %bitcast.15), custom_call_target="tpu_custom_call" | custom-call | flops 300000000 | bytes 4000000 | tf_op jit(solution)/shard_map/first/pallas_call | solution.py:302
  5.5 11.5 %all-to-all-start = ((bf16[128,2,8,128]{3,2,1,0:T(8,128)(2,1)}), bf16[128,2,8,128]{3,2,1,0:T(8,128)(2,1)S(1)}, u32[]{:S(2)}, u32[]{:S(2)}) async-start(bf16[128,2,8,128]{3,2,1,0:T(8,128)(2,1)} %get-tuple-element.30), calls=%async_computation | async-start | bytes 1048576 | tf_op jit(solution)/shard_map/all_to_all | solution.py:315
  17.0 3.5 %obs.1 = bf16[4,4,2,128,128]{4,3,2,1,0:T(8,128)(2,1)} custom-call(s32[4]{0:T(128)} %obs_time.1, f32[4,1024,128]{2,1,0:T(8,128)} %bitcast.19), custom_call_target="tpu_custom_call" | custom-call | flops 10000000 | bytes 3000000 | tf_op jit(solution)/shard_map/obs/pallas_call | solution.py:302
  20.5 10.6 %all-to-all-done = bf16[128,2,8,128]{3,2,1,0:T(8,128)(2,1)S(1)} async-done(((bf16[128,2,8,128]{3,2,1,0:T(8,128)(2,1)}), bf16[128,2,8,128]{3,2,1,0:T(8,128)(2,1)S(1)}, u32[]{:S(2)}, u32[]{:S(2)}) %all-to-all-start) | async-done | bytes 524320 | tf_op jit(solution)/shard_map/all_to_all | solution.py:315
  31.1 0.0 copy-start.2
  31.1 3.5 %all-to-all-start.1 = ((bf16[4,4,2,128,128]{4,3,2,1,0:T(8,128)(2,1)}), bf16[4,4,2,128,128]{4,3,2,1,0:T(8,128)(2,1)S(1)}, u32[]{:S(2)}, u32[]{:S(2)}) async-start(bf16[4,4,2,128,128]{4,3,2,1,0:T(8,128)(2,1)} %obs.1), calls=%async_computation.1 | async-start | bytes 2097152 | tf_op jit(solution)/shard_map/all_to_all | solution.py:315
  34.7 2.3 tables.1
  37.0 12.7 %all-to-all-done.1.refs_6_ = bf16[4,4,2,128,128]{4,3,2,1,0:T(8,128)(2,1)S(1)} async-done(((bf16[4,4,2,128,128]{4,3,2,1,0:T(8,128)(2,1)}), bf16[4,4,2,128,128]{4,3,2,1,0:T(8,128)(2,1)S(1)}, u32[]{:S(2)}, u32[]{:S(2)}) %all-to-all-start.1) | async-done | bytes 1048608 | tf_op jit(solution)/shard_map/all_to_all | solution.py:315
  49.7 0.0 copy-start.1
  49.7 0.0 copy-done.2
  49.7 1.0 copy-done.1
  50.7 6.0 %columns_3.1 = (bf16[32,4,8,128]{3,2,1,0:T(8,128)(2,1)}, f32[1024,128]{1,0:T(8,128)}, f32[512,128]{1,0:T(8,128)}) custom-call(bf16[32,4,2,8,128]{4,3,2,1,0:T(8,128)(2,1)} %bitcast.21, bf16[512,512]{1,0:T(8,128)(2,1)} %get-tuple-element.31.refs_1_, bf16[128,512]{1,0:T(8,128)(2,1)} %refs_2_.7, bf16[512,128]{1,0:T(8,128)(2,1)} %get-tuple-element.32.refs_3_, ...), custom_call_target="tpu_custom_call" | custom-call | flops 1200000000 | bytes 3000000 | tf_op jit(solution)/shard_map/columns_3/pallas_call | solution.py:302
  56.7 16.8 %all_to_all.50.back = bf16[128,8,128]{2,1,0:T(8,128)(2,1)} all-to-all(bf16[128,8,128]{2,1,0:T(8,128)(2,1)} %bitcast.29), channel_id=1, replica_groups=mesh['band_0'=4,'band_1'=4,'band_2'=2,'lev'=4] {'band_0','band_1','band_..., dimensions={0} | all-to-all | bytes 524288 | tf_op jit(solution)/shard_map/all_to_all | solution.py:315
  73.5 4.0 %turn_3.1 = (bf16[128,2,8,128]{3,2,1,0:T(8,128)(2,1)}, f32[8,64,256]{2,1,0:T(8,128)}) custom-call(s32[8]{0:T(128)} %dynamic_slice.3.waves, bf16[128,8,128]{2,1,0:T(8,128)(2,1)} %all_to_all.50.back, f32[8,64,256]{2,1,0:T(8,128)} %get-tuple-element.35.damped_in, bf16[8,256,256]{2,1,0:T(8,128)(2,1)} %get-tuple-element.36.table, f32[4,512,256]{2,1,0:T(8,128)} %bitcast.16), custom_call_target="tpu_custom_call" | custom-call | flops 400000000 | bytes 4000000 | tf_op jit(solution)/shard_map/turn_3/pallas_call | solution.py:302
  77.5 18.8 %all_to_all.51 = bf16[128,2,8,128]{3,2,1,0:T(8,128)(2,1)} all-to-all(bf16[128,2,8,128]{3,2,1,0:T(8,128)(2,1)} %get-tuple-element.37), channel_id=1, replica_groups=mesh['band_0'=4,'band_1'=4,'band_2'=2,'lev'=4] {'band_0','band_1','band_..., dimensions={0} | all-to-all | bytes 1048576 | tf_op jit(solution)/shard_map/all_to_all | solution.py:315
  96.3 6.3 %columns_2.1 = (bf16[32,4,8,128]{3,2,1,0:T(8,128)(2,1)}, f32[1024,128]{1,0:T(8,128)}, f32[512,128]{1,0:T(8,128)}) custom-call(bf16[32,4,2,8,128]{4,3,2,1,0:T(8,128)(2,1)} %bitcast.24, bf16[512,512]{1,0:T(8,128)(2,1)} %get-tuple-element.31.refs_1_, bf16[128,512]{1,0:T(8,128)(2,1)} %refs_2_.7, bf16[512,128]{1,0:T(8,128)(2,1)} %get-tuple-element.32.refs_3_, ...), custom_call_target="tpu_custom_call" | custom-call | flops 1200000000 | bytes 3000000 | tf_op jit(solution)/shard_map/columns_2/pallas_call | solution.py:302
  102.6 15.9 %all_to_all.52.back = bf16[128,8,128]{2,1,0:T(8,128)(2,1)} all-to-all(bf16[128,8,128]{2,1,0:T(8,128)(2,1)} %bitcast.27), channel_id=1, replica_groups=mesh['band_0'=4,'band_1'=4,'band_2'=2,'lev'=4] {'band_0','band_1','band_..., dimensions={0} | all-to-all | bytes 524288 | tf_op jit(solution)/shard_map/all_to_all | solution.py:315
  118.5 4.0 %turn_2.1 = (bf16[128,2,8,128]{3,2,1,0:T(8,128)(2,1)}, f32[8,64,256]{2,1,0:T(8,128)}) custom-call(s32[8]{0:T(128)} %dynamic_slice.3.waves, bf16[128,8,128]{2,1,0:T(8,128)(2,1)} %all_to_all.52.back, f32[8,64,256]{2,1,0:T(8,128)} %get-tuple-element.41.damped_in, bf16[8,256,256]{2,1,0:T(8,128)(2,1)} %get-tuple-element.36.table, f32[4,512,256]{2,1,0:T(8,128)} %bitcast.17), custom_call_target="tpu_custom_call" | custom-call | flops 400000000 | bytes 4000000 | tf_op jit(solution)/shard_map/turn_2/pallas_call | solution.py:302
  122.5 18.8 %all_to_all.53 = bf16[128,2,8,128]{3,2,1,0:T(8,128)(2,1)} all-to-all(bf16[128,2,8,128]{3,2,1,0:T(8,128)(2,1)} %get-tuple-element.42), channel_id=1, replica_groups=mesh['band_0'=4,'band_1'=4,'band_2'=2,'lev'=4] {'band_0','band_1','band_..., dimensions={0} | all-to-all | bytes 1048576 | tf_op jit(solution)/shard_map/all_to_all | solution.py:315
  141.3 6.3 %columns_1.1 = (bf16[32,4,8,128]{3,2,1,0:T(8,128)(2,1)}, f32[1024,128]{1,0:T(8,128)}, f32[512,128]{1,0:T(8,128)}) custom-call(bf16[32,4,2,8,128]{4,3,2,1,0:T(8,128)(2,1)} %bitcast.25, bf16[512,512]{1,0:T(8,128)(2,1)} %get-tuple-element.31.refs_1_, bf16[128,512]{1,0:T(8,128)(2,1)} %refs_2_.7, bf16[512,128]{1,0:T(8,128)(2,1)} %get-tuple-element.32.refs_3_, ...), custom_call_target="tpu_custom_call" | custom-call | flops 1200000000 | bytes 3000000 | tf_op jit(solution)/shard_map/columns_1/pallas_call | solution.py:302
  147.6 15.9 %all_to_all.54.back = bf16[128,8,128]{2,1,0:T(8,128)(2,1)} all-to-all(bf16[128,8,128]{2,1,0:T(8,128)(2,1)} %bitcast.28), channel_id=1, replica_groups=mesh['band_0'=4,'band_1'=4,'band_2'=2,'lev'=4] {'band_0','band_1','band_..., dimensions={0} | all-to-all | bytes 524288 | tf_op jit(solution)/shard_map/all_to_all | solution.py:315
  163.5 4.0 %turn_1.1 = (bf16[128,2,8,128]{3,2,1,0:T(8,128)(2,1)}, f32[8,64,256]{2,1,0:T(8,128)}) custom-call(s32[8]{0:T(128)} %dynamic_slice.3.waves, bf16[128,8,128]{2,1,0:T(8,128)(2,1)} %all_to_all.54.back, f32[8,64,256]{2,1,0:T(8,128)} %get-tuple-element.46.damped_in, bf16[8,256,256]{2,1,0:T(8,128)(2,1)} %get-tuple-element.36.table, f32[4,512,256]{2,1,0:T(8,128)} %bitcast.18), custom_call_target="tpu_custom_call" | custom-call | flops 400000000 | bytes 4000000 | tf_op jit(solution)/shard_map/turn_1/pallas_call | solution.py:302
  167.5 18.8 %all_to_all.55 = bf16[128,2,8,128]{3,2,1,0:T(8,128)(2,1)} all-to-all(bf16[128,2,8,128]{3,2,1,0:T(8,128)(2,1)} %get-tuple-element.47), channel_id=1, replica_groups=mesh['band_0'=4,'band_1'=4,'band_2'=2,'lev'=4] {'band_0','band_1','band_..., dimensions={0} | all-to-all | bytes 1048576 | tf_op jit(solution)/shard_map/all_to_all | solution.py:315
  186.3 6.4 %columns_0.1 = (bf16[32,4,2,8,128]{4,3,2,1,0:T(8,128)(2,1)}, f32[8,128]{1,0:T(8,128)}) custom-call(bf16[32,4,2,8,128]{4,3,2,1,0:T(8,128)(2,1)} %bitcast.22, bf16[512,512]{1,0:T(8,128)(2,1)} %get-tuple-element.31.refs_1_, bf16[128,512]{1,0:T(8,128)(2,1)} %refs_2_.7, bf16[512,128]{1,0:T(8,128)(2,1)} %get-tuple-element.32.refs_3_, bf16[512,128]{1,0:T(8,128)(2,1)} %refs_4_.7, ...), custom_call_target="tpu_custom_call" | custom-call | flops 1200000000 | bytes 3000000 | tf_op jit(solution)/shard_map/columns_0/pallas_call | solution.py:302
  192.7 18.7 %all_to_all.56.back = bf16[128,2,8,128]{3,2,1,0:T(8,128)(2,1)} all-to-all(bf16[128,2,8,128]{3,2,1,0:T(8,128)(2,1)} %bitcast.23), channel_id=1, replica_groups=mesh['band_0'=4,'band_1'=4,'band_2'=2,'lev'=4] {'band_0','band_1','band_..., dimensions={0} | all-to-all | bytes 1048576 | tf_op jit(solution)/shard_map/all_to_all | solution.py:315
  211.5 2.0 share.1
  213.5 3.6 %all-to-all-start.9 = ((bf16[128,2,8,128]{3,2,1,0:T(8,128)(2,1)}), bf16[128,2,8,128]{3,2,1,0:T(8,128)(2,1)S(1)}, u32[]{:S(2)}, u32[]{:S(2)}) async-start(bf16[128,2,8,128]{3,2,1,0:T(8,128)(2,1)} %share.1), calls=%async_computation.9 | async-start | bytes 1048576 | tf_op jit(solution)/shard_map/all_to_all | solution.py:315
  217.1 2.9 %last.1 = f32[512,256]{1,0:T(8,128)} custom-call(bf16[128,2,8,128]{3,2,1,0:T(8,128)(2,1)} %all_to_all.56.back, f32[8,64,256]{2,1,0:T(8,128)} %get-tuple-element.51.damped_in, bf16[8,256,256]{2,1,0:T(8,128)(2,1)} %get-tuple-element.36.table), custom_call_target="tpu_custom_call" | custom-call | flops 100000000 | bytes 3000000 | tf_op jit(solution)/shard_map/last/pallas_call | solution.py:302
  219.9 11.4 %all-to-all-done.9.parts = bf16[128,2,8,128]{3,2,1,0:T(8,128)(2,1)S(1)} async-done(((bf16[128,2,8,128]{3,2,1,0:T(8,128)(2,1)}), bf16[128,2,8,128]{3,2,1,0:T(8,128)(2,1)S(1)}, u32[]{:S(2)}, u32[]{:S(2)}) %all-to-all-start.9) | async-done | bytes 524320 | tf_op jit(solution)/shard_map/all_to_all | solution.py:315
  231.3 0.0 copy-start
  231.3 0.8 copy-done
  232.1 1.9 ending.1
Async XLA Ops:
  5.5 25.6 %all-to-all-start = ((bf16[128,2,8,128]{3,2,1,0:T(8,128)(2,1)}), bf16[128,2,8,128]{3,2,1,0:T(8,128)(2,1)S(1)}, u32[]{:S(2)}, u32[]{:S(2)}) async-start(bf16[128,2,8,128]{3,2,1,0:T(8,128)(2,1)} %get-tuple-element.30), calls=%async_computation | async-start | bytes 1048576 | tf_op jit(solution)/shard_map/all_to_all | solution.py:315
  31.1 18.5 %copy-start.2 = (bf16[128,2,8,128]{3,2,1,0:T(8,128)(2,1)}, bf16[128,2,8,128]{3,2,1,0:T(8,128)(2,1)S(1)}, u32[]{:S(2)}) copy-start(bf16[128,2,8,128]{3,2,1,0:T(8,128)(2,1)S(1)} %all-to-all-done) | copy-start | bytes 1572868
  31.1 18.5 %all-to-all-start.1 = ((bf16[4,4,2,128,128]{4,3,2,1,0:T(8,128)(2,1)}), bf16[4,4,2,128,128]{4,3,2,1,0:T(8,128)(2,1)S(1)}, u32[]{:S(2)}, u32[]{:S(2)}) async-start(bf16[4,4,2,128,128]{4,3,2,1,0:T(8,128)(2,1)} %obs.1), calls=%async_computation.1 | async-start | bytes 2097152 | tf_op jit(solution)/shard_map/all_to_all | solution.py:315
  49.7 1.0 copy-start.1
  213.5 17.8 %all-to-all-start.9 = ((bf16[128,2,8,128]{3,2,1,0:T(8,128)(2,1)}), bf16[128,2,8,128]{3,2,1,0:T(8,128)(2,1)S(1)}, u32[]{:S(2)}, u32[]{:S(2)}) async-start(bf16[128,2,8,128]{3,2,1,0:T(8,128)(2,1)} %share.1), calls=%async_computation.9 | async-start | bytes 1048576 | tf_op jit(solution)/shard_map/all_to_all | solution.py:315
  231.3 0.8 copy-start

commit v2 on v1

--- a/solution.py
+++ b/solution.py
@@ -83,11 +83,12 @@
     waves, legendre, final, state, send, damped, table, tall, rows_t, rows_s, final_rows, state_rows
 ):
     damping = damping_row()
+    band = lax.axis_index(BAND)
     halve(final, final_rows)
     halve(state.at[0], state_rows)
     degree = lane_of(N, N)
     for rho in range(RHO):
-        m = waves[rho]
+        m = waves[band * RHO + rho]
         kept = jnp.where(degree >= m, legendre[rho].astype(F32), 0.0)
         for h in range(2):
             tall[h] = kept[:, h * 128 : (h + 1) * 128]
@@ -112,16 +113,35 @@
     return mm(jnp.concatenate(halves, axis=0).astype(BF16), table)
 
 
-def turn_kernel(waves, back, damped_in, table, state, send, damped, rows, rows_t, rows_s, state_rows):
+def turn_kernel(
+    step,
+    waves,
+    back,
+    damped_in,
+    table,
+    states_hbm,
+    send,
+    damped,
+    rows,
+    rows_t,
+    rows_s,
+    state_rows,
+    state,
+    sem,
+):
+    copy = pltpu.make_async_copy(states_hbm.at[step], state, sem)
+    copy.start()
     damping = damping_row()
-    halve(state.at[0], state_rows)
+    band = lax.axis_index(BAND)
     rows[...] = back[...].astype(F32).reshape(DEV * RHO, 128)
+    copy.wait()
+    halve(state, state_rows)
     for rho in range(RHO):
         now = damping * (damped_in[rho] + adjoint_rho(rows, table[rho], rho))
         damped[rho] = now
         synth_rho(
             table[rho],
-            now * tangent_scale(waves[rho]),
+            now * tangent_scale(waves[band * RHO + rho]),
             strided_rows(state_rows, rho),
             rho,
             rows_t,
@@ -167,31 +187,45 @@
     bias_wide[...] = jnp.broadcast_to(bias[...], (128, HID)).T
 
 
-def obs_kernel(obs_time, obs, out):
-    for j in range(8):
-        pieces = [obs[i, pl.ds(j, FEAT, stride=8), :] for i in range(4)]
-        for step in range(STEPS):
-            total = jnp.zeros((FEAT, 128), F32)
-            for i in range(4):
-                total += jnp.where(obs_time[i] == step, 1.0, 0.0).astype(F32) * pieces[i]
-            out[j // 2, step, j % 2] = total.astype(BF16)
-
-
-def column_kernel(first, last, *refs):
-    got, trig, w_in, w_in_t, w_out, bias, obs = refs[:7]
-    refs = refs[7:]
+def obs_kernel(obs_time, obs, *outs):
+    lev = lax.axis_index("lev")
+    for k in range(4):
+        to = lax.rem(lev + k, 4)
+        for jj in range(2):
+            pieces = [obs[i, pl.ds(2 * to + jj, FEAT, stride=8), :] for i in range(4)]
+            for step in range(STEPS):
+                total = jnp.zeros((FEAT, 128), F32)
+                for i in range(4):
+                    total += jnp.where(obs_time[i] == step, 1.0, 0.0).astype(F32) * pieces[i]
+                if step == STEPS - 1:
+                    outs[k][0, jj] = total.astype(BF16)
+                else:
+                    outs[4 + k][step, jj] = total.astype(BF16)
+
+
+def column_kernel(first, last, step, *refs):
+    got, trig, w_in, w_in_t, w_out, bias = refs[:6]
+    obs_parts = refs[6:10]
+    refs = refs[10:]
     if not first:
         acc_in, accb_in = refs[:2]
         refs = refs[2:]
     send = refs[0]
     if last:
         bias_part = refs[1]
-        acc, accb, turned, grid, grads = refs[2:]
+        acc, accb, turned, grid, grads, obs, sems = refs[2:]
     else:
-        acc, accb, turned, grid, grads = refs[1:]
+        acc, accb, turned, grid, grads, obs, sems = refs[1:]
+    lev = lax.axis_index("lev")
+    copies = [
+        pltpu.make_async_copy(obs_parts[k].at[step], obs.at[lax.rem(lev + 4 - k, 4)], sems.at[k])
+        for k in range(4)
+    ]
+    for copy in copies:
+        copy.start()
     for kind in range(2):
         for y in range(4):
-            x = got[:, y, kind].astype(F32).reshape(N, 128).T.astype(BF16)
+            x = got[:, y, kind].reshape(N, 128).T
             for p in range(2):
                 for jj in range(2):
                     at = (2 * p + jj) * VL
@@ -211,6 +245,9 @@
         acc[...] = acc_in[...]
         accb[...] = accb_in[...]
 
+    for copy in copies:
+        copy.wait()
+
     def block(cb, carry):
         tangent = grid[0, cb]
         features = grid[1, cb]
@@ -229,7 +266,7 @@
             back += mm(w_in[:, rows], low)
         jj = cb // 2
         half = cb % 2
-        seen = jnp.concatenate([obs[2 * half + k, 0, jj] for k in range(2)], axis=1)
+        seen = jnp.concatenate([obs[2 * half + k, jj] for k in range(2)], axis=1)
         back += seen.astype(F32)
         back = jnp.concatenate(
             [back[(v * 4 + y) * 8 : (v * 4 + y + 1) * 8] for y in range(4) for v in range(4)], axis=0
@@ -237,13 +274,13 @@
         grads[jj, half] = back.astype(BF16)
         return carry
 
-    lax.fori_loop(0, 4, block, 0)
+    lax.fori_loop(0, 4, block, 0, unroll=True)
 
     real = (lane_of(N, 2 * 128) // 64) % 2 == 0
     for pair in range(2):
         rows = []
         for y in (2 * pair, 2 * pair + 1):
-            for p in range(2):
+            for _ in range(2):
                 for jj in range(2):
                     rows.append(
                         jnp.concatenate(
@@ -277,6 +314,7 @@
 
 VMEM = pl.BlockSpec(memory_space=pltpu.VMEM)
 SMEM = pl.BlockSpec(memory_space=pltpu.SMEM)
+HBM = pl.BlockSpec(memory_space=pltpu.HBM)
 
 
 def shape(dims, kind):
@@ -287,15 +325,15 @@
     return pl.CostEstimate(flops=flops, bytes_accessed=nbytes, transcendentals=0)
 
 
-def state_spec(step):
-    return pl.BlockSpec((1, 512, N), lambda i: (step, 0, 0))
-
-
 def whole(dims):
     return pl.BlockSpec(dims, lambda i: (0,) * len(dims))
 
 
-def call(body, ins, outs, scratch, in_specs, name, flops, nbytes):
+VMEM_LIMIT = 20 * 1024 * 1024
+BIG = 63_000_000
+
+
+def call(body, ins, outs, scratch, in_specs, flops, nbytes, vmem=VMEM_LIMIT):
     many = isinstance(outs, (list, tuple))
     outs_list = list(outs) if many else [outs]
     out_specs = [whole(o.shape) for o in outs_list]
@@ -307,7 +345,7 @@
         out_specs=out_specs if many else out_specs[0],
         scratch_shapes=scratch,
         cost_estimate=cost(flops, nbytes),
-        name=name,
+        compiler_params=pltpu.CompilerParams(vmem_limit_bytes=vmem),
     )(*ins)
 
 
@@ -321,24 +359,30 @@
     return jnp.asarray(np.concatenate([np.cos(angle), -np.sin(angle)], axis=1), BF16)
 
 
-def shards(checkpoints, final_cot, obs_cot, obs_time, wave_order, legendre, w_in, w_out, bias):
-    waves = lax.dynamic_slice_in_dim(wave_order, lax.axis_index(BAND) * RHO, RHO)
+def program(checkpoints, final_cot, obs_cot, obs_time, wave_order, legendre, w_in, w_out, bias):
     states = checkpoints.reshape(STEPS, 512, N)
     final = final_cot.reshape(512, N)
     seen = obs_cot.reshape(4, FEAT * 8, 128)
+    state_spec = pl.BlockSpec((1, 512, N), lambda i: (STEPS - 1, 0, 0))
     chunks = shape((DEV, 2, RHO, 128), BF16)
     tall = pltpu.VMEM((DEV * RHO, 128), F32)
     halves = pltpu.VMEM((2, 512, 128), F32)
 
     send, damped, table = call(
         first_kernel,
-        (waves, legendre, final, states),
+        (wave_order, legendre, final, states),
         (chunks, shape((RHO, 64, N), F32), shape((RHO, N, N), BF16)),
-        [pltpu.VMEM((2, N, 128), F32), tall, tall, halves, halves],
-        [SMEM, whole(legendre.shape), whole(final.shape), state_spec(STEPS - 1)],
-        "first",
+        [
+            pltpu.VMEM((2, N, 128), F32),
+            tall,
+            tall,
+            halves,
+            halves,
+        ],
+        [SMEM, whole(legendre.shape), whole(final.shape), state_spec],
         300_000_000,
         4_000_000,
+        BIG,
     )
     trig, w_in_t, bias_wide = call(
         tables_kernel,
@@ -346,21 +390,25 @@
         (shape((2 * N, LON), BF16), shape((HID, FEAT), BF16), shape((HID, 128), F32)),
         [],
         [whole((1, N)), whole((N, 2 * LON)), whole(w_in.shape), whole((1, HID))],
-        "tables",
         140_000_000,
         1_500_000,
+        BIG,
     )
     obs_parts = call(
         obs_kernel,
         (obs_time, seen),
-        shape((4, STEPS, 2, FEAT, 128), BF16),
+        [shape((1, 2, FEAT, 128), BF16)] * 4 + [shape((STEPS - 1, 2, FEAT, 128), BF16)] * 4,
         [],
         [SMEM, whole(seen.shape)],
-        "obs",
         10_000_000,
         3_000_000,
-    )
-    obs_cols = exchange(obs_parts, ("lev",))
+        BIG,
+    )
+    obs_cols = []
+    for k, part in enumerate(obs_parts):
+        if k % 4:
+            part = lax.ppermute(part, "lev", [(i, (i + k) % 4) for i in range(4)])
+        obs_cols.append(part)
 
     sums = ()
     for step in reversed(range(STEPS)):
@@ -372,34 +420,37 @@
             pltpu.VMEM((2, 2, FEAT, 2 * N), BF16),
             pltpu.VMEM((2, 4, FEAT, 256), BF16),
             pltpu.VMEM((2, 2, FEAT, 256), BF16),
+            pltpu.VMEM((4, 2, FEAT, 128), BF16),
+            pltpu.SemaphoreType.DMA((4,)),
         ]
         if last:
             outs = [shape((32, 4, 2, RHO, 128), BF16), shape((8, 128), F32)]
             scratch = [pltpu.VMEM(a.shape, F32) for a in acc_shapes] + scratch
         else:
             outs = [shape((32, 4, RHO, 128), BF16)] + acc_shapes
-        ins = (got, trig, w_in, w_in_t, w_out, bias_wide, obs_cols) + tuple(sums)
+        obs_now = obs_cols[:4] if first else obs_cols[4:]
+        ins = (got, trig, w_in, w_in_t, w_out, bias_wide, *obs_now) + tuple(sums)
         specs = [whole(a.shape) for a in ins]
-        specs[6] = pl.BlockSpec((4, 1, 2, FEAT, 128), functools.partial(lambda s, i: (0, s, 0, 0, 0), step))
+        for k in range(4):
+            specs[6 + k] = HBM
         back, *sums = call(
-            functools.partial(column_kernel, first, last),
+            functools.partial(column_kernel, first, last, step % (STEPS - 1)),
             ins,
             outs,
             scratch,
             specs,
-            f"columns_{step}",
             1_200_000_000,
             3_000_000,
+            BIG if first else VMEM_LIMIT,
         )
         if not last:
             back = exchange(back.reshape(DEV, RHO, 128), ALL)
             send, damped = call(
-                turn_kernel,
-                (waves, back, damped, table, states),
+                functools.partial(turn_kernel, step - 1),
+                (wave_order, back, damped, table, states),
                 (chunks, shape((RHO, 64, N), F32)),
-                [tall, tall, tall, halves],
-                [SMEM, whole(back.shape), whole(damped.shape), whole(table.shape), state_spec(step - 1)],
-                f"turn_{step}",
+                [tall, tall, tall, halves, pltpu.VMEM(final.shape, F32), pltpu.SemaphoreType.DMA],
+                [SMEM, whole(back.shape), whole(damped.shape), whole(table.shape), HBM],
                 400_000_000,
                 4_000_000,
             )
@@ -411,7 +462,6 @@
         chunks,
         [],
         [whole(back.shape), whole(bias_part.shape)],
-        "share",
         1_000_000,
         1_000_000,
     )
@@ -422,7 +472,6 @@
         shape((512, N), F32),
         [tall, halves],
         [whole(back.shape), whole(damped.shape), whole(table.shape)],
-        "last",
         100_000_000,
         3_000_000,
     )
@@ -432,7 +481,6 @@
         (shape((FEAT, HID), F32), shape((HID, FEAT), F32), shape((4, 128), F32)),
         [],
         [whole(parts.shape)],
-        "ending",
         1_000_000,
         1_500_000,
     )
@@ -453,7 +501,7 @@
         P(),
     )
     return jax.shard_map(
-        shards,
+        program,
         mesh=torus,
         in_specs=placed,
         out_specs=(P(None, "lev", None, BAND, None), P(), P(), P()),

time: 235 us -> 215 us (0.915)
  blocking collectives: 124 us -> 104 us
  Pallas kernels: 53.2 us -> 36.3 us
  local copies, waits for them, and re-layouts: 3.07 us -> 14.8 us
  starting transfers between devices: 18.6 us -> 29.8 us
  waiting for transfers between devices: 34.7 us -> 28.1 us
    all_to_all x3, waiting for transfers between devices: 34.7 us -> 14.3 us  [exchange(): return lax.all_to_all(array, axes, split_axis=0, concat_axis=0, tiled=True)]
    all_to_all x7 -> x6, blocking collectives: 124 us -> 104 us  [exchange(): return lax.all_to_all(array, axes, split_axis=0, concat_axis=0, tiled=True)]
    pallas_call x13, Pallas kernels: 53.2 us -> 36.3 us  [call(): pl.pallas_call(body, grid=(1,), out_shape=outs_list if many else outs, in...]
    ppermute x0 -> x6, waiting for transfers between devices: none -> 13.8 us  [program(): part = lax.ppermute(part, 'lev', [(i, (i + k) % 4) for i in range(4)])]
    unnamed x6 -> x60, local copies, waits for them, and re-layouts: 1.8 us -> 14.8 us
    ppermute x0 -> x6, starting transfers between devices: none -> 10.1 us  [program(): part = lax.ppermute(part, 'lev', [(i, (i + k) % 4) for i in range(4)])]
  transfers between devices with their start and end apart: 3 -> 9, of which waited for: 3 -> 6; matrix products, arithmetic and copies ran while one was open for 0% -> 0% of each run, Pallas kernels for 4% -> 3%
where the time goes in v2:
time: 215 us; the launch traced here: 214 us
  blocking collectives  104 us (48%)
  Pallas kernels  36.3 us (17%)
  starting transfers between devices  29.8 us (14%)
  waiting for transfers between devices  28.1 us (13%)
  local copies, waits for them, and re-layouts  14.8 us (7%)
    all_to_all x6, blocking collectives, exchange(): return lax.all_to_all(array, axes, split_axis=0, concat_axis=0, tiled=True)  104 us
    pallas_call x13, Pallas kernels, call(): pl.pallas_call(body, grid=(1,), out_shape=outs_list if many else outs, in...  36.3 us
    all_to_all x3, starting transfers between devices, exchange(): return lax.all_to_all(array, axes, split_axis=0, concat_axis=0, tiled=True)  19.8 us
    unnamed x60, local copies, waits for them, and re-layouts  14.8 us
    all_to_all x3, waiting for transfers between devices, exchange(): return lax.all_to_all(array, axes, split_axis=0, concat_axis=0, tiled=True)  14.3 us
    ppermute x6, waiting for transfers between devices, program(): part = lax.ppermute(part, 'lev', [(i, (i + k) % 4) for i in range(4)])  13.8 us
    ppermute x6, starting transfers between devices, program(): part = lax.ppermute(part, 'lev', [(i, (i + k) % 4) for i in range(4)])  10.1 us
  transfers between devices with their start and end apart: 9, of which 6 were waited for; matrix products, arithmetic and copies ran while one was open for 0% of the time, Pallas kernels for 3%

profile of v2, /device:TPU:1, one launch (start us, length us, event | category | flops | bytes accessed | tf_op | source)
XLA Modules:
  0.0 214.2 jit_solution(4212949013128474453)
XLA Ops:
  0.6 3.6 %shard_map.129 = (bf16[128,2,8,128]{3,2,1,0:T(8,128)(2,1)}, f32[8,64,256]{2,1,0:T(8,128)}, bf16[8,256,256]{2,1,0:T(8,128)(2,1)}) custom-call(s32[256]{0:T(256)} %waves.7, bf16[8,256,256]{2,1,0:T(8,128)(2,1)} %legendre.1, f32[512,256]{1,0:T(8,128)} %bitcast.28, f32[4,512,256]{2,1,0:T(8,128)} %bitcast.15), custom_call_target="tpu_custom_call" | custom-call | flops 300000000 | bytes 4000000 | tf_op jit(solution)/shard_map/pallas_call | solution.py:340
  4.3 11.5 %all-to-all-start = ((bf16[128,2,8,128]{3,2,1,0:T(8,128)(2,1)}), bf16[128,2,8,128]{3,2,1,0:T(8,128)(2,1)S(1)}, u32[]{:S(2)}, u32[]{:S(2)}) async-start(bf16[128,2,8,128]{3,2,1,0:T(8,128)(2,1)} %get-tuple-element.38), calls=%async_computation | async-start | bytes 1048576 | tf_op jit(solution)/shard_map/all_to_all | solution.py:353
  15.8 3.4 %shard_map.131 = (bf16[1,2,128,128]{3,2,1,0:T(8,128)(2,1)}, bf16[1,2,128,128]{3,2,1,0:T(8,128)(2,1)}, bf16[1,2,128,128]{3,2,1,0:T(8,128)(2,1)}, bf16[1,2,128,128...) custom-call(s32[4]{0:T(128)} %obs_time.1, ...), custom_call_target="tpu_custom_call" | custom-call | flops 10000000 | bytes 3000000 | tf_op jit(solution)/shard_map/pallas_call | solution.py:340
  19.1 1.4 collective-permute-start
  20.5 2.5 %collective-permute-start.1 = (bf16[1,2,128,128]{3,2,1,0:T(8,128)(2,1)}, bf16[1,2,128,128]{3,2,1,0:T(8,128)(2,1)S(1)}, u32[]{:S(2)}, u32[]{:S(2)}) collective-permute-start(bf16[1,2,128,128]{3,2,1,0:T(8,128)(2,1)} %get-tuple-element.44), channel_id=1, source_target_pairs={{0,2},{1,3},{2,0},{3,1},{4,6},{5,7},{6,4},{7,5},{8,10},{9,11},{10,... | collective-permute-start | bytes 196616 | tf_op jit(solution)/shard_map/ppermute | solution.py:410
  22.9 1.1 collective-permute-start.2
  24.0 2.3 %shard_map.130 = (bf16[512,512]{1,0:T(8,128)(2,1)}, bf16[512,128]{1,0:T(8,128)(2,1)}, f32[512,128]{1,0:T(8,128)}) custom-call(s32[1,256]{1,0:T(1,128)} %bitcast.24, bf16[256,1024]{1,0:T(8,128)(2,1)} %constant.2.clone.base, bf16[128,512]{1,0:T(8,128)(2,1)} %refs_2_.7, f32[1,512]{1,0:T(1,128)} %bitcast.30), custom_call_target="tpu_custom_call" | custom-call | flops 140000000 | bytes 1500000 | tf_op jit(solution)/shard_map/pallas_call | solution.py:340
  26.4 0.3 collective-permute-done.refs_7_
  26.7 1.9 collective-permute-done.1.refs_8_
  28.5 0.0 collective-permute-done.2.refs_9_
  28.5 1.3 all-to-all-done
  29.9 0.8 copy-done.26
  30.7 0.0 copy-done.27
  30.7 0.0 copy-done.28
  30.7 0.0 copy-done.29
  30.7 0.0 copy-start.1
  30.7 0.0 copy-start.9
  30.7 5.8 %shard_map.132 = (bf16[32,4,8,128]{3,2,1,0:T(8,128)(2,1)}, f32[1024,128]{1,0:T(8,128)}, f32[512,128]{1,0:T(8,128)}) custom-call(bf16[32,4,2,8,128]{4,3,2,1,0:T(8,128)(2,1)} %bitcast.27, bf16[512,512]{1,0:T(8,128)(2,1)} %get-tuple-element.39.refs_1_, bf16[128,512]{1,0:T(8,128)(2,1)} %refs_2_.7, bf16[512,128]{1,0:T(8,128)(2,1)} %get-tuple-element.40.refs_3_, ...), custom_call_target="tpu_custom_call" | custom-call | flops 1200000000 | bytes 3000000 | tf_op jit(solution)/shard_map/pallas_call | solution.py:340
  36.5 18.7 %all_to_all.45.back = bf16[128,8,128]{2,1,0:T(8,128)(2,1)S(1)} all-to-all(bf16[128,8,128]{2,1,0:T(8,128)(2,1)} %bitcast.29), channel_id=1, replica_groups=mesh['band_0'=4,'band_1'=4,'band_2'=2,'lev'=4] {'band_0','band_1','band_..., dimensions={0} | all-to-all | bytes 524288 | tf_op jit(solution)/shard_map/all_to_all | solution.py:353
  55.1 0.0 copy-done
  55.1 0.0 copy-start.2
  55.2 1.0 copy-done.2
  56.2 2.2 %shard_map.133 = (bf16[128,2,8,128]{3,2,1,0:T(8,128)(2,1)S(1)}, f32[8,64,256]{2,1,0:T(8,128)S(1)}) custom-call(s32[256]{0:T(256)S(1)} %copy-done.9, bf16[128,8,128]{2,1,0:T(8,128)(2,1)S(1)} %all_to_all.45.back, f32[8,64,256]{2,1,0:T(8,128)S(1)} %copy-done.2, bf16[8,256,256]{2,1,0:T(8,128)(2,1)S(1)} %copy-done.1, f32[4,512,256]{2,1,0:T(8,128)S(1)} %bitcast.16), custom_call_target="tpu_custom_call" | custom-call | flops 400000000 | bytes 4000000 | tf_op jit(solution)/shard_map/pallas_call | solution.py:340
  58.4 0.8 copy-done.3
  59.2 0.8 copy-done.7
  60.0 4.7 %all-to-all-start.2 = ((bf16[128,2,8,128]{3,2,1,0:T(8,128)(2,1)}), bf16[128,2,8,128]{3,2,1,0:T(8,128)(2,1)}, u32[]{:S(2)}, u32[]{:S(2)}) async-start(bf16[128,2,8,128]{3,2,1,0:T(8,128)(2,1)} %copy-done.7), calls=%async_computation.2 | async-start | bytes 1048576 | tf_op jit(solution)/shard_map/all_to_all | solution.py:353
  64.7 1.5 collective-permute-start.3
  66.2 2.5 %collective-permute-start.4 = (bf16[3,2,128,128]{3,2,1,0:T(8,128)(2,1)}, bf16[3,2,128,128]{3,2,1,0:T(8,128)(2,1)S(1)}, u32[]{:S(2)}, u32[]{:S(2)}) collective-permute-start(bf16[3,2,128,128]{3,2,1,0:T(8,128)(2,1)} %get-tuple-element.52), channel_id=1, source_target_pairs={{0,2},{1,3},{2,0},{3,1},{4,6},{5,7},{6,4},{7,5},{8,10},{9,11},{10,... | collective-permute-start | bytes 589832 | tf_op jit(solution)/shard_map/ppermute | solution.py:410
  68.7 1.1 collective-permute-start.5
  69.9 7.6 %collective-permute-done.3.refs_7_ = bf16[3,2,128,128]{3,2,1,0:T(8,128)(2,1)S(1)} collective-permute-done((bf16[3,2,128,128]{3,2,1,0:T(8,128)(2,1)}, bf16[3,2,128,128]{3,2,1,0:T(8,128)(2,1)S(1)}, u32[]{:S(2)}, u32[]{:S(2)}) %collective-permute-start.3) | collective-permute-done | bytes 196640 | tf_op jit(solution)/shard_map/ppermute | solution.py:410
  77.4 0.7 copy-done.15
  78.1 4.1 %collective-permute-done.4.refs_8_ = bf16[3,2,128,128]{3,2,1,0:T(8,128)(2,1)S(1)} collective-permute-done((bf16[3,2,128,128]{3,2,1,0:T(8,128)(2,1)}, bf16[3,2,128,128]{3,2,1,0:T(8,128)(2,1)S(1)}, u32[]{:S(2)}, u32[]{:S(2)}) %collective-permute-start.4) | collective-permute-done | bytes 196640 | tf_op jit(solution)/shard_map/ppermute | solution.py:410
  82.2 0.7 copy-done.17
  82.9 0.0 collective-permute-done.5.refs_9_
  82.9 0.7 copy-done.19
  83.6 0.0 all-to-all-done.2
  83.6 1.0 copy-done.10
  84.7 0.9 copy-done.13
  85.6 0.9 copy-done.16
  86.5 0.9 copy-done.18
  87.5 0.9 copy-done.20
  88.4 0.9 copy-done.22
  89.3 0.9 copy-done.23
  90.2 1.0 copy-done.24
  91.2 0.9 copy-done.25
  92.2 4.5 %shard_map.134 = (bf16[32,4,8,128]{3,2,1,0:T(8,128)(2,1)S(1)}, f32[1024,128]{1,0:T(8,128)S(1)}, f32[512,128]{1,0:T(8,128)S(1)}) custom-call(bf16[32,4,2,8,128]{4,3,2,1,0:T(8,128)(2,1)} %bitcast.7.refs_0_, bf16[512,512]{1,0:T(8,128)(2,1)S(1)} %copy-done.10, bf16[128,512]{1,0:T(8,128)(2,1)S(1)} %copy-done.8, bf16[512,128]{1,0:T(8,128)(2,1)S(1)} %copy-done.23, ...), custom_call_target="tpu_custom_call" | custom-call | flops 1200000000 | bytes 3000000 | tf_op jit(solution)/shard_map/pallas_call | solution.py:340
  96.7 18.0 %all_to_all.46.back = bf16[128,8,128]{2,1,0:T(8,128)(2,1)S(1)} all-to-all(bf16[128,8,128]{2,1,0:T(8,128)(2,1)S(1)} %bitcast.22), channel_id=1, replica_groups=mesh['band_0'=4,'band_1'=4,'band_2'=2,'lev'=4] {'band_0','band_1','band_..., dimensions={0} | all-to-all | bytes 524288 | tf_op jit(solution)/shard_map/all_to_all | solution.py:353
  114.7 2.2 %shard_map.135 = (bf16[128,2,8,128]{3,2,1,0:T(8,128)(2,1)S(1)}, f32[8,64,256]{2,1,0:T(8,128)S(1)}) custom-call(s32[256]{0:T(256)S(1)} %copy-done.9, bf16[128,8,128]{2,1,0:T(8,128)(2,1)S(1)} %all_to_all.46.back, f32[8,64,256]{2,1,0:T(8,128)S(1)} %copy-done.4, bf16[8,256,256]{2,1,0:T(8,128)(2,1)S(1)} %copy-done.1, f32[4,512,256]{2,1,0:T(8,128)S(1)} %bitcast.17), custom_call_target="tpu_custom_call" | custom-call | flops 400000000 | bytes 4000000 | tf_op jit(solution)/shard_map/pallas_call | solution.py:340
  116.9 17.8 %all_to_all.47 = bf16[128,2,8,128]{3,2,1,0:T(8,128)(2,1)S(1)} all-to-all(bf16[128,2,8,128]{3,2,1,0:T(8,128)(2,1)S(1)} %get-tuple-element.58), channel_id=1, replica_groups=mesh['band_0'=4,'band_1'=4,'band_2'=2,'lev'=4] {'band_0','band_1','band_..., dimensions={0} | all-to-all | bytes 1048576 | tf_op jit(solution)/shard_map/all_to_all | solution.py:353
  134.7 3.4 %shard_map.136 = (bf16[32,4,8,128]{3,2,1,0:T(8,128)(2,1)S(1)}, f32[1024,128]{1,0:T(8,128)S(1)}, f32[512,128]{1,0:T(8,128)S(1)}) custom-call(bf16[32,4,2,8,128]{4,3,2,1,0:T(8,128)(2,1)S(1)} %bitcast.21, bf16[512,512]{1,0:T(8,128)(2,1)S(1)} %copy-done.11, bf16[128,512]{1,0:T(8,128)(2,1)S(1)} %copy-done.8, bf16[512,128]{1,0:T(8,128)(2,1)S(1)} %copy-done.23, ...), custom_call_target="tpu_custom_call" | custom-call | flops 1200000000 | bytes 3000000 | tf_op jit(solution)/shard_map/pallas_call | solution.py:340
  138.1 14.6 %all_to_all.48.back = bf16[128,8,128]{2,1,0:T(8,128)(2,1)S(1)} all-to-all(bf16[128,8,128]{2,1,0:T(8,128)(2,1)S(1)} %bitcast.23), channel_id=1, replica_groups=mesh['band_0'=4,'band_1'=4,'band_2'=2,'lev'=4] {'band_0','band_1','band_..., dimensions={0} | all-to-all | bytes 524288 | tf_op jit(solution)/shard_map/all_to_all | solution.py:353
  152.7 2.2 %shard_map.137 = (bf16[128,2,8,128]{3,2,1,0:T(8,128)(2,1)S(1)}, f32[8,64,256]{2,1,0:T(8,128)S(1)}) custom-call(s32[256]{0:T(256)S(1)} %copy-done.9, bf16[128,8,128]{2,1,0:T(8,128)(2,1)S(1)} %all_to_all.48.back, f32[8,64,256]{2,1,0:T(8,128)S(1)} %get-tuple-element.62.damped_in, bf16[8,256,256]{2,1,0:T(8,128)(2,1)S(1)} %copy-done.1, f32[4,512,256]{2,1,0:T(8,128)S(1)} %bitcast.18), custom_call_target="tpu_custom_call" | custom-call | flops 400000000 | bytes 4000000 | tf_op jit(solution)/shard_map/pallas_call | solution.py:340
  154.9 0.0 copy-start.5
  154.9 0.8 copy-done.5
  155.7 17.8 %all_to_all.49 = bf16[128,2,8,128]{3,2,1,0:T(8,128)(2,1)S(1)} all-to-all(bf16[128,2,8,128]{3,2,1,0:T(8,128)(2,1)S(1)} %get-tuple-element.63), channel_id=1, replica_groups=mesh['band_0'=4,'band_1'=4,'band_2'=2,'lev'=4] {'band_0','band_1','band_..., dimensions={0} | all-to-all | bytes 1048576 | tf_op jit(solution)/shard_map/all_to_all | solution.py:353
  173.5 0.0 copy-done.21
  173.5 3.6 %shard_map.138 = (bf16[32,4,2,8,128]{4,3,2,1,0:T(8,128)(2,1)S(1)}, f32[8,128]{1,0:T(8,128)S(1)}) custom-call(bf16[32,4,2,8,128]{4,3,2,1,0:T(8,128)(2,1)S(1)} %bitcast.19, bf16[512,512]{1,0:T(8,128)(2,1)S(1)} %copy-done.11, bf16[128,512]{1,0:T(8,128)(2,1)S(1)} %copy-done.8, bf16[512,128]{1,0:T(8,128)(2,1)S(1)} %copy-done.23, bf16[512,128]{1,0:T(8,128)(2,1)S(1)} %copy-done.22, ...), custom_call_target="tpu_custom_call" | custom-call | flops 1200000000 | bytes 3000000 | tf_op jit(solution)/shard_map/pallas_call | solution.py:340
  177.1 0.0 copy-start.6
  177.1 17.5 %all_to_all.50.back = bf16[128,2,8,128]{3,2,1,0:T(8,128)(2,1)S(1)} all-to-all(bf16[128,2,8,128]{3,2,1,0:T(8,128)(2,1)S(1)} %bitcast.20), channel_id=1, replica_groups=mesh['band_0'=4,'band_1'=4,'band_2'=2,'lev'=4] {'band_0','band_1','band_..., dimensions={0} | all-to-all | bytes 1048576 | tf_op jit(solution)/shard_map/all_to_all | solution.py:353
  194.6 1.0 shard_map.140
  195.5 3.6 %all-to-all-start.8 = ((bf16[128,2,8,128]{3,2,1,0:T(8,128)(2,1)}), bf16[128,2,8,128]{3,2,1,0:T(8,128)(2,1)S(1)}, u32[]{:S(2)}, u32[]{:S(2)}) async-start(bf16[128,2,8,128]{3,2,1,0:T(8,128)(2,1)} %shard_map.140), calls=%async_computation.8 | async-start | bytes 1048576 | tf_op jit(solution)/shard_map/all_to_all | solution.py:353
  199.1 1.3 shard_map.139
  200.4 12.9 %all-to-all-done.8.parts = bf16[128,2,8,128]{3,2,1,0:T(8,128)(2,1)S(1)} async-done(((bf16[128,2,8,128]{3,2,1,0:T(8,128)(2,1)}), bf16[128,2,8,128]{3,2,1,0:T(8,128)(2,1)S(1)}, u32[]{:S(2)}, u32[]{:S(2)}) %all-to-all-start.8) | async-done | bytes 524320 | tf_op jit(solution)/shard_map/all_to_all | solution.py:353
  213.3 0.8 shard_map.141
  (33 shorter events, 0.1 us)
Async XLA Ops:
  4.3 25.6 %all-to-all-start = ((bf16[128,2,8,128]{3,2,1,0:T(8,128)(2,1)}), bf16[128,2,8,128]{3,2,1,0:T(8,128)(2,1)S(1)}, u32[]{:S(2)}, u32[]{:S(2)}) async-start(bf16[128,2,8,128]{3,2,1,0:T(8,128)(2,1)} %get-tuple-element.38), calls=%async_computation | async-start | bytes 1048576 | tf_op jit(solution)/shard_map/all_to_all | solution.py:353
  19.1 7.6 %collective-permute-start = (bf16[1,2,128,128]{3,2,1,0:T(8,128)(2,1)}, bf16[1,2,128,128]{3,2,1,0:T(8,128)(2,1)S(1)}, u32[]{:S(2)}, u32[]{:S(2)}) collective-permute-start(bf16[1,2,128,128]{3,2,1,0:T(8,128)(2,1)} %get-tuple-element.43), channel_id=1, source_target_pairs={{0,1},{1,2},{2,3},{3,0},{4,5},{5,6},{6,7},{7,4},{8,9},{9,10},{10,1... | collective-permute-start | bytes 196616 | tf_op jit(solution)/shard_map/ppermute | solution.py:410
  20.5 8.1 %collective-permute-start.1 = (bf16[1,2,128,128]{3,2,1,0:T(8,128)(2,1)}, bf16[1,2,128,128]{3,2,1,0:T(8,128)(2,1)S(1)}, u32[]{:S(2)}, u32[]{:S(2)}) collective-permute-start(bf16[1,2,128,128]{3,2,1,0:T(8,128)(2,1)} %get-tuple-element.44), channel_id=1, source_target_pairs={{0,2},{1,3},{2,0},{3,1},{4,6},{5,7},{6,4},{7,5},{8,10},{9,11},{10,... | collective-permute-start | bytes 196616 | tf_op jit(solution)/shard_map/ppermute | solution.py:410
  22.9 5.6 %collective-permute-start.2 = (bf16[1,2,128,128]{3,2,1,0:T(8,128)(2,1)}, bf16[1,2,128,128]{3,2,1,0:T(8,128)(2,1)S(1)}, u32[]{:S(2)}, u32[]{:S(2)}) collective-permute-start(bf16[1,2,128,128]{3,2,1,0:T(8,128)(2,1)} %get-tuple-element.45), channel_id=1, source_target_pairs={{0,3},{1,0},{2,1},{3,2},{4,7},{5,4},{6,5},{7,6},{8,11},{9,8},{10,9... | collective-permute-start | bytes 196616 | tf_op jit(solution)/shard_map/ppermute | solution.py:410
  26.7 4.0 %copy-start.27 = (bf16[1,2,128,128]{3,2,1,0:T(8,128)(2,1)}, bf16[1,2,128,128]{3,2,1,0:T(8,128)(2,1)S(1)}, u32[]{:S(2)}) copy-start(bf16[1,2,128,128]{3,2,1,0:T(8,128)(2,1)S(1)} %collective-permute-done.refs_7_) | copy-start | bytes 196612
  28.5 2.1 copy-start.28
  28.5 2.1 copy-start.29
  29.9 0.8 copy-start.26
  30.7 24.5 %copy-start = (f32[4,4,8,2,8,256]{5,4,3,2,1,0:T(8,128)S(1)}, f32[4,4,8,2,8,256]{5,4,3,2,1,0:T(8,128)}, u32[]{:S(2)}) copy-start(f32[4,4,8,2,8,256]{5,4,3,2,1,0:T(8,128)} %param.10) | copy-start | bytes 6291460
  30.7 24.5 %copy-start.1 = (bf16[8,256,256]{2,1,0:T(8,128)(2,1)S(1)}, bf16[8,256,256]{2,1,0:T(8,128)(2,1)}, u32[]{:S(2)}) copy-start(bf16[8,256,256]{2,1,0:T(8,128)(2,1)} %get-tuple-element.48.table) | copy-start | bytes 3145732
  30.7 24.5 %copy-start.9 = (s32[256]{0:T(256)S(1)}, s32[256]{0:T(256)}, u32[]{:S(2)}) copy-start(s32[256]{0:T(256)} %waves.7) | copy-start | bytes 3076
  55.1 1.0 copy-start.2
  56.2 27.4 %copy-start.8 = (bf16[128,512]{1,0:T(8,128)(2,1)S(1)}, bf16[128,512]{1,0:T(8,128)(2,1)}, u32[]{:S(2)}) copy-start(bf16[128,512]{1,0:T(8,128)(2,1)} %refs_2_.7) | copy-start | bytes 393220
  56.2 27.4 %copy-start.12 = (f32[512,128]{1,0:T(8,128)S(1)}, f32[512,128]{1,0:T(8,128)}, u32[]{:S(2)}) copy-start(f32[512,128]{1,0:T(8,128)} %get-tuple-element.41.refs_5_) | copy-start | bytes 786436
  58.4 0.8 copy-start.3
  59.2 0.8 copy-start.7
  60.0 23.6 %all-to-all-start.2 = ((bf16[128,2,8,128]{3,2,1,0:T(8,128)(2,1)}), bf16[128,2,8,128]{3,2,1,0:T(8,128)(2,1)}, u32[]{:S(2)}, u32[]{:S(2)}) async-start(bf16[128,2,8,128]{3,2,1,0:T(8,128)(2,1)} %copy-done.7), calls=%async_computation.2 | async-start | bytes 1048576 | tf_op jit(solution)/shard_map/all_to_all | solution.py:353
  64.7 12.7 %collective-permute-start.3 = (bf16[3,2,128,128]{3,2,1,0:T(8,128)(2,1)}, bf16[3,2,128,128]{3,2,1,0:T(8,128)(2,1)S(1)}, u32[]{:S(2)}, u32[]{:S(2)}) collective-permute-start(bf16[3,2,128,128]{3,2,1,0:T(8,128)(2,1)} %get-tuple-element.51), channel_id=1, source_target_pairs={{0,1},{1,2},{2,3},{3,0},{4,5},{5,6},{6,7},{7,4},{8,9},{9,10},{10,1... | collective-permute-start | bytes 589832 | tf_op jit(solution)/shard_map/ppermute | solution.py:410
  66.2 16.0 %collective-permute-start.4 = (bf16[3,2,128,128]{3,2,1,0:T(8,128)(2,1)}, bf16[3,2,128,128]{3,2,1,0:T(8,128)(2,1)S(1)}, u32[]{:S(2)}, u32[]{:S(2)}) collective-permute-start(bf16[3,2,128,128]{3,2,1,0:T(8,128)(2,1)} %get-tuple-element.52), channel_id=1, source_target_pairs={{0,2},{1,3},{2,0},{3,1},{4,6},{5,7},{6,4},{7,5},{8,10},{9,11},{10,... | collective-permute-start | bytes 589832 | tf_op jit(solution)/shard_map/ppermute | solution.py:410
  68.7 14.2 %collective-permute-start.5 = (bf16[3,2,128,128]{3,2,1,0:T(8,128)(2,1)}, bf16[3,2,128,128]{3,2,1,0:T(8,128)(2,1)S(1)}, u32[]{:S(2)}, u32[]{:S(2)}) collective-permute-start(bf16[3,2,128,128]{3,2,1,0:T(8,128)(2,1)} %get-tuple-element.53), channel_id=1, source_target_pairs={{0,3},{1,0},{2,1},{3,2},{4,7},{5,4},{6,5},{7,6},{8,11},{9,8},{10,9... | collective-permute-start | bytes 589832 | tf_op jit(solution)/shard_map/ppermute | solution.py:410
  77.4 0.7 copy-start.15
  82.2 0.7 copy-start.17
  82.9 0.7 copy-start.19
  83.6 1.0 copy-start.10
  84.7 0.9 copy-start.13
  85.6 0.9 copy-start.16
  86.5 0.9 copy-start.18
  87.5 0.9 copy-start.20
  88.4 0.9 copy-start.22
  89.3 0.9 copy-start.23
  90.2 1.0 copy-start.24
  91.2 0.9 copy-start.25
  92.2 22.5 %copy-start.4 = (f32[8,64,256]{2,1,0:T(8,128)S(1)}, f32[8,64,256]{2,1,0:T(8,128)}, u32[]{:S(2)}) copy-start(f32[8,64,256]{2,1,0:T(8,128)} %copy-done.3) | copy-start | bytes 1572868
  114.6 20.0 %copy-start.11 = (bf16[512,512]{1,0:T(8,128)(2,1)S(1)}, bf16[512,512]{1,0:T(8,128)(2,1)}, u32[]{:S(2)}) copy-start(bf16[512,512]{1,0:T(8,128)(2,1)} %get-tuple-element.39.refs_1_) | copy-start | bytes 1572868
  152.7 20.8 %copy-start.14 = (bf16[3,2,128,128]{3,2,1,0:T(8,128)(2,1)S(1)}, bf16[3,2,128,128]{3,2,1,0:T(8,128)(2,1)}, u32[]{:S(2)}) copy-start(bf16[3,2,128,128]{3,2,1,0:T(8,128)(2,1)} %get-tuple-element.50.refs_6_) | copy-start | bytes 589828
  152.7 20.8 %copy-start.21 = (bf16[3,2,128,128]{3,2,1,0:T(8,128)(2,1)S(1)}, bf16[3,2,128,128]{3,2,1,0:T(8,128)(2,1)}, u32[]{:S(2)}) copy-start(bf16[3,2,128,128]{3,2,1,0:T(8,128)(2,1)} %copy-done.19) | copy-start | bytes 589828
  154.9 0.8 copy-start.5
  177.1 22.0 %copy-start.6 = (f32[8,64,256]{2,1,0:T(8,128)S(1)}, f32[8,64,256]{2,1,0:T(8,128)}, u32[]{:S(2)}) copy-start(f32[8,64,256]{2,1,0:T(8,128)} %copy-done.5) | copy-start | bytes 1572868
  195.5 17.8 %all-to-all-start.8 = ((bf16[128,2,8,128]{3,2,1,0:T(8,128)(2,1)}), bf16[128,2,8,128]{3,2,1,0:T(8,128)(2,1)S(1)}, u32[]{:S(2)}, u32[]{:S(2)}) async-start(bf16[128,2,8,128]{3,2,1,0:T(8,128)(2,1)} %shard_map.140), calls=%async_computation.8 | async-start | bytes 1048576 | tf_op jit(solution)/shard_map/all_to_all | solution.py:353

commit v3 on v2

--- a/solution.py
+++ b/solution.py
@@ -114,28 +114,12 @@
 
 
 def turn_kernel(
-    step,
-    waves,
-    back,
-    damped_in,
-    table,
-    states_hbm,
-    send,
-    damped,
-    rows,
-    rows_t,
-    rows_s,
-    state_rows,
-    state,
-    sem,
+    step, waves, back, damped_in, table, states, send, damped, rows, rows_t, rows_s, state_rows
 ):
-    copy = pltpu.make_async_copy(states_hbm.at[step], state, sem)
-    copy.start()
     damping = damping_row()
     band = lax.axis_index(BAND)
     rows[...] = back[...].astype(F32).reshape(DEV * RHO, 128)
-    copy.wait()
-    halve(state, state_rows)
+    halve(states.at[step], state_rows)
     for rho in range(RHO):
         now = damping * (damped_in[rho] + adjoint_rho(rows, table[rho], rho))
         damped[rho] = now
@@ -176,7 +160,7 @@
     bias_out[...] = total[:4] + total[4:]
 
 
-def tables_kernel(waves, base, w_in, bias, trig, w_in_t, bias_wide):
+def fill_tables(waves, base, w_in, bias, trig, w_in_t, bias_wide):
     m = lax.broadcasted_iota(jnp.int32, (N, N), 0)
     weight = jnp.where(m == 0, 1.0, 2.0).astype(F32)
     pick = jnp.where(m == waves[...], weight, 0.0).T.astype(BF16)
@@ -192,9 +176,9 @@
     for k in range(4):
         to = lax.rem(lev + k, 4)
         for jj in range(2):
-            pieces = [obs[i, pl.ds(2 * to + jj, FEAT, stride=8), :] for i in range(4)]
+            pieces = [obs[i, pl.ds(2 * to + jj, 32, stride=8), :] for i in range(4)]
             for step in range(STEPS):
-                total = jnp.zeros((FEAT, 128), F32)
+                total = jnp.zeros((32, 128), F32)
                 for i in range(4):
                     total += jnp.where(obs_time[i] == step, 1.0, 0.0).astype(F32) * pieces[i]
                 if step == STEPS - 1:
@@ -204,25 +188,52 @@
 
 
 def column_kernel(first, last, step, *refs):
-    got, trig, w_in, w_in_t, w_out, bias = refs[:6]
-    obs_parts = refs[6:10]
-    refs = refs[10:]
-    if not first:
-        acc_in, accb_in = refs[:2]
-        refs = refs[2:]
-    send = refs[0]
-    if last:
-        bias_part = refs[1]
-        acc, accb, turned, grid, grads, obs, sems = refs[2:]
+    collect = step == STEPS - 2
+    refs = list(refs)
+    take = lambda count: [refs.pop(0) for _ in range(count)]
+    got, w_in, w_out = take(3)
+    if first:
+        waves, base, bias_row = take(3)
+        obs_parts = take(4)
+        (send,) = take(1)
+        acc, accb, trig, w_in_t, bias = take(5)
+        turned, grid, grads, obs, sems = refs
+        lev = lax.axis_index("lev")
+        copies = [
+            pltpu.make_async_copy(obs_parts[k].at[0], obs.at[lax.rem(lev + 4 - k, 4)], sems.at[k])
+            for k in range(4)
+        ]
+        for copy in copies:
+            copy.start()
+        others = []
+        fill_tables(waves, base, w_in, bias_row, trig, w_in_t, bias)
     else:
-        acc, accb, turned, grid, grads, obs, sems = refs[1:]
-    lev = lax.axis_index("lev")
-    copies = [
-        pltpu.make_async_copy(obs_parts[k].at[step], obs.at[lax.rem(lev + 4 - k, 4)], sems.at[k])
-        for k in range(4)
-    ]
-    for copy in copies:
-        copy.start()
+        trig, w_in_t, bias, acc_in, accb_in = take(5)
+        if collect:
+            obs_parts = take(4)
+            send, acc, accb, obs_all, turned, grid, grads, sems = refs
+            lev = lax.axis_index("lev")
+            copies, others = [], []
+            for k in range(4):
+                to = lax.rem(lev + 4 - k, 4)
+                copies.append(
+                    pltpu.make_async_copy(obs_parts[k].at[step], obs_all.at[step, to], sems.at[k])
+                )
+                for s in range(step):
+                    others.append(
+                        pltpu.make_async_copy(
+                            obs_parts[k].at[s], obs_all.at[s, to], sems.at[4 * (s + 1) + k]
+                        )
+                    )
+            for copy in copies + others:
+                copy.start()
+        else:
+            copies, others = [], []
+            obs_all, send = take(2)
+            if last:
+                (bias_part,) = take(1)
+            acc, accb, turned, grid, grads = refs
+        obs = obs_all.at[step]
     for kind in range(2):
         for y in range(4):
             x = got[:, y, kind].reshape(N, 128).T
@@ -295,6 +306,8 @@
                 send[:, 2 * pair + k, 0] = chunk
             else:
                 send[:, 2 * pair + k] = chunk
+    for copy in others:
+        copy.wait()
     if last:
         send[:, :, 1] = acc[...].reshape(32, 4, 8, 128).astype(BF16)
         ones = jnp.ones((8, 128), F32)
@@ -331,6 +344,7 @@
 
 VMEM_LIMIT = 20 * 1024 * 1024
 BIG = 63_000_000
+FIRST = 40_000_000
 
 
 def call(body, ins, outs, scratch, in_specs, flops, nbytes, vmem=VMEM_LIMIT):
@@ -384,26 +398,17 @@
         4_000_000,
         BIG,
     )
-    trig, w_in_t, bias_wide = call(
-        tables_kernel,
-        (wave_order.reshape(1, N), trig_base(), w_in, bias.reshape(1, HID)),
-        (shape((2 * N, LON), BF16), shape((HID, FEAT), BF16), shape((HID, 128), F32)),
-        [],
-        [whole((1, N)), whole((N, 2 * LON)), whole(w_in.shape), whole((1, HID))],
-        140_000_000,
-        1_500_000,
-        BIG,
-    )
-    obs_parts = call(
+    obs_shapes = [(1, 2, FEAT, 128)] * 4 + [(STEPS - 1, 2, FEAT, 128)] * 4
+    obs_parts = pl.pallas_call(
         obs_kernel,
-        (obs_time, seen),
-        [shape((1, 2, FEAT, 128), BF16)] * 4 + [shape((STEPS - 1, 2, FEAT, 128), BF16)] * 4,
-        [],
-        [SMEM, whole(seen.shape)],
-        10_000_000,
-        3_000_000,
-        BIG,
-    )
+        grid=(4,),
+        out_shape=[shape(d, BF16) for d in obs_shapes],
+        in_specs=[SMEM, pl.BlockSpec((4, 256, 128), lambda g: (0, g, 0))],
+        out_specs=[pl.BlockSpec(d[:2] + (32, 128), lambda g: (0, 0, g, 0)) for d in obs_shapes],
+        cost_estimate=cost(10_000_000, 3_000_000),
+        compiler_params=pltpu.CompilerParams(vmem_limit_bytes=BIG),
+        name="obs",
+    )(obs_time, seen)
     obs_cols = []
     for k, part in enumerate(obs_parts):
         if k % 4:
@@ -420,37 +425,56 @@
             pltpu.VMEM((2, 2, FEAT, 2 * N), BF16),
             pltpu.VMEM((2, 4, FEAT, 256), BF16),
             pltpu.VMEM((2, 2, FEAT, 256), BF16),
-            pltpu.VMEM((4, 2, FEAT, 128), BF16),
-            pltpu.SemaphoreType.DMA((4,)),
         ]
+        outs = [shape((32, 4, RHO, 128), BF16)] + acc_shapes
+        ins = [got, w_in, w_out]
+        if first:
+            ins += [wave_order.reshape(1, N), trig_base(), bias.reshape(1, HID)]
+            outs += [shape((2 * N, LON), BF16), shape((HID, FEAT), BF16), shape((HID, 128), F32)]
+            scratch += [pltpu.VMEM((4, 2, FEAT, 128), BF16), pltpu.SemaphoreType.DMA((4,))]
+            specs = [whole(a.shape) for a in ins] + [HBM] * 4
+            ins += obs_cols[:4]
+        else:
+            ins += [trig, w_in_t, bias_wide, *sums]
+            specs = [whole(a.shape) for a in ins]
+            if step == STEPS - 2:
+                ins += obs_cols[4:]
+                specs += [HBM] * 4
+                outs.append(shape((STEPS - 1, 4, 2, FEAT, 128), BF16))
+                scratch.append(pltpu.SemaphoreType.DMA((4 * (STEPS - 1),)))
+            else:
+                ins.append(obs_all)
+                specs.append(whole(obs_all.shape))
         if last:
             outs = [shape((32, 4, 2, RHO, 128), BF16), shape((8, 128), F32)]
             scratch = [pltpu.VMEM(a.shape, F32) for a in acc_shapes] + scratch
-        else:
-            outs = [shape((32, 4, RHO, 128), BF16)] + acc_shapes
-        obs_now = obs_cols[:4] if first else obs_cols[4:]
-        ins = (got, trig, w_in, w_in_t, w_out, bias_wide, *obs_now) + tuple(sums)
-        specs = [whole(a.shape) for a in ins]
-        for k in range(4):
-            specs[6 + k] = HBM
         back, *sums = call(
-            functools.partial(column_kernel, first, last, step % (STEPS - 1)),
+            functools.partial(column_kernel, first, last, step),
             ins,
             outs,
             scratch,
             specs,
             1_200_000_000,
             3_000_000,
-            BIG if first else VMEM_LIMIT,
+            FIRST if first else VMEM_LIMIT,
         )
+        if first:
+            trig, w_in_t, bias_wide = sums[2:]
+            sums = sums[:2]
+        elif not last and len(sums) > 2:
+            obs_all = sums.pop()
         if not last:
             back = exchange(back.reshape(DEV, RHO, 128), ALL)
+            ins = [wave_order, back, damped, table, states]
+            specs = [SMEM, whole(back.shape), whole(damped.shape), whole(table.shape), whole(states.shape)]
+            outs = [chunks, shape((RHO, 64, N), F32)]
+            scratch = [tall, tall, tall, halves]
             send, damped = call(
                 functools.partial(turn_kernel, step - 1),
-                (wave_order, back, damped, table, states),
-                (chunks, shape((RHO, 64, N), F32)),
-                [tall, tall, tall, halves, pltpu.VMEM(final.shape, F32), pltpu.SemaphoreType.DMA],
-                [SMEM, whole(back.shape), whole(damped.shape), whole(table.shape), HBM],
+                ins,
+                outs,
+                scratch,
+                specs,
                 400_000_000,
                 4_000_000,
             )

time: 215 us -> 217 us (level)
  Pallas kernels: 36.3 us -> 32.3 us
  local copies, waits for them, and re-layouts: 14.8 us -> 17.5 us
    pallas_call x13 -> x11, Pallas kernels: 36.3 us -> 28.3 us  [call(): pl.pallas_call(body, grid=(1,), out_shape=outs_list if many else outs, in...]
    pallas_call x0 -> x1, Pallas kernels: none -> 3.92 us  [program(): pl.pallas_call(obs_kernel, grid=(4,), out_shape=[shape(d, BF16) for d in...]
    ppermute x6, waiting for transfers between devices: 13.8 us -> 16.7 us  [program(): part = lax.ppermute(part, 'lev', [(i, (i + k) % 4) for i in range(4)])]
    unnamed x60 -> x74, local copies, waits for them, and re-layouts: 14.8 us -> 17.5 us
  transfers between devices with their start and end apart: 9 -> 9, of which waited for: 6 -> 6; matrix products, arithmetic and copies ran while one was open for 0% -> 0% of each run, Pallas kernels for 3% -> 2%
where the time goes in v3:
time: 217 us; the launch traced here: 216 us
  blocking collectives  105 us (48%)
  Pallas kernels  32.3 us (15%)
  starting transfers between devices  29.9 us (14%)
  waiting for transfers between devices  29.9 us (14%)
  local copies, waits for them, and re-layouts  17.5 us (8%)
    all_to_all x6, blocking collectives, exchange(): return lax.all_to_all(array, axes, split_axis=0, concat_axis=0, tiled=True)  105 us
    pallas_call x11, Pallas kernels, call(): pl.pallas_call(body, grid=(1,), out_shape=outs_list if many else outs, in...  28.3 us
    all_to_all x3, starting transfers between devices, exchange(): return lax.all_to_all(array, axes, split_axis=0, concat_axis=0, tiled=True)  19.8 us
    unnamed x74, local copies, waits for them, and re-layouts  17.5 us
    ppermute x6, waiting for transfers between devices, program(): part = lax.ppermute(part, 'lev', [(i, (i + k) % 4) for i in range(4)])  16.7 us
    all_to_all x3, waiting for transfers between devices, exchange(): return lax.all_to_all(array, axes, split_axis=0, concat_axis=0, tiled=True)  13.2 us
    ppermute x6, starting transfers between devices, program(): part = lax.ppermute(part, 'lev', [(i, (i + k) % 4) for i in range(4)])  10.1 us
  transfers between devices with their start and end apart: 9, of which 6 were waited for; matrix products, arithmetic and copies ran while one was open for 0% of the time, Pallas kernels for 2%

profile of v3, /device:TPU:1, one launch (start us, length us, event | category | flops | bytes accessed | tf_op | source)
XLA Modules:
  0.0 215.8 jit_solution(15368858837154638706)
XLA Ops:
  0.6 3.6 %shard_map.129 = (bf16[128,2,8,128]{3,2,1,0:T(8,128)(2,1)}, f32[8,64,256]{2,1,0:T(8,128)}, bf16[8,256,256]{2,1,0:T(8,128)(2,1)}) custom-call(s32[256]{0:T(256)} %waves.7, bf16[8,256,256]{2,1,0:T(8,128)(2,1)} %legendre.1, f32[512,256]{1,0:T(8,128)} %bitcast.30, f32[4,512,256]{2,1,0:T(8,128)} %bitcast.15), custom_call_target="tpu_custom_call" | custom-call | flops 300000000 | bytes 4000000 | tf_op jit(solution)/shard_map/pallas_call | solution.py:354
  4.3 0.0 copy-start.23
  4.3 11.5 %all-to-all-start = ((bf16[128,2,8,128]{3,2,1,0:T(8,128)(2,1)}), bf16[128,2,8,128]{3,2,1,0:T(8,128)(2,1)S(1)}, u32[]{:S(2)}, u32[]{:S(2)}) async-start(bf16[128,2,8,128]{3,2,1,0:T(8,128)(2,1)} %get-tuple-element.39), calls=%async_computation | async-start | bytes 1048576 | tf_op jit(solution)/shard_map/all_to_all | solution.py:367
  15.8 3.9 %obs.1 = (bf16[1,2,128,128]{3,2,1,0:T(8,128)(2,1)}, bf16[1,2,128,128]{3,2,1,0:T(8,128)(2,1)}, bf16[1,2,128,128]{3,2,1,0:T(8,128)(2,1)}, bf16[1,2,128,128]{3,2,1,...) custom-call(s32[4]{0:T(128)} %obs_time.1, ...), custom_call_target="tpu_custom_call" | custom-call | flops 10000000 | bytes 3000000 | tf_op jit(solution)/shard_map/obs/pallas_call | solution.py:402
  19.7 1.4 collective-permute-start
  21.1 2.5 %collective-permute-start.1 = (bf16[1,2,128,128]{3,2,1,0:T(8,128)(2,1)}, bf16[1,2,128,128]{3,2,1,0:T(8,128)(2,1)S(1)}, u32[]{:S(2)}, u32[]{:S(2)}) collective-permute-start(bf16[1,2,128,128]{3,2,1,0:T(8,128)(2,1)} %get-tuple-element.42), channel_id=1, source_target_pairs={{0,2},{1,3},{2,0},{3,1},{4,6},{5,7},{6,4},{7,5},{8,10},{9,11},{10,... | collective-permute-start | bytes 196616 | tf_op jit(solution)/shard_map/ppermute | solution.py:415
  23.6 1.1 collective-permute-start.2
  24.7 2.0 collective-permute-done.refs_7_
  26.7 2.3 %collective-permute-done.1.refs_8_ = bf16[1,2,128,128]{3,2,1,0:T(8,128)(2,1)S(1)} collective-permute-done((bf16[1,2,128,128]{3,2,1,0:T(8,128)(2,1)}, bf16[1,2,128,128]{3,2,1,0:T(8,128)(2,1)S(1)}, u32[]{:S(2)}, u32[]{:S(2)}) %collective-permute-start.1) | collective-permute-done | bytes 65568 | tf_op jit(solution)/shard_map/ppermute | solution.py:415
  29.0 0.0 collective-permute-done.2.refs_9_
  29.0 0.6 copy-done.21
  29.6 0.3 all-to-all-done
  29.9 0.8 copy-done.7
  30.7 0.0 copy-done.10
  30.7 0.0 copy-start.8
  30.7 1.0 copy-done.8
  31.8 0.8 copy-done.20
  32.6 0.8 copy-done.22
  33.4 1.0 copy-done.24
  34.5 3.8 %shard_map.130 = (bf16[32,4,8,128]{3,2,1,0:T(8,128)(2,1)S(1)}, f32[1024,128]{1,0:T(8,128)S(1)}, f32[512,128]{1,0:T(8,128)S(1)}, bf16[512,512]{1,0:T(8,128)(2,1)S...) custom-call(bf16[32,4,2,8,128]{4,3,2,1,0:T(8,128)(2,1)S(1)} %bitcast.19, bf16[128,512]{1,0:T(8,128)(2,1)S(1)} %copy-done.16, ...), custom_call_target="tpu_custom_call" | custom-call | flops 1200000000 | bytes 3000000 | tf_op jit(solution)/shard_map/pallas_call | solution.py:354
  38.3 0.0 copy-start.30
  38.3 0.0 copy-start.33
  38.3 0.0 copy-start.35
  38.3 19.7 %all_to_all.45.back = bf16[128,8,128]{2,1,0:T(8,128)(2,1)S(1)} all-to-all(bf16[128,8,128]{2,1,0:T(8,128)(2,1)S(1)} %bitcast.23), channel_id=1, replica_groups=mesh['band_0'=4,'band_1'=4,'band_2'=2,'lev'=4] {'band_0','band_1','band_..., dimensions={0} | all-to-all | bytes 524288 | tf_op jit(solution)/shard_map/all_to_all | solution.py:367
  58.0 0.0 copy-done
  58.0 2.2 %shard_map.131 = (bf16[128,2,8,128]{3,2,1,0:T(8,128)(2,1)S(1)}, f32[8,64,256]{2,1,0:T(8,128)S(1)}) custom-call(s32[256]{0:T(256)S(1)} %copy-done.10, bf16[128,8,128]{2,1,0:T(8,128)(2,1)S(1)} %all_to_all.45.back, f32[8,64,256]{2,1,0:T(8,128)S(1)} %copy-done.2, bf16[8,256,256]{2,1,0:T(8,128)(2,1)S(1)} %copy-done.1, f32[4,512,256]{2,1,0:T(8,128)S(1)} %bitcast.16), custom_call_target="tpu_custom_call" | custom-call | flops 400000000 | bytes 4000000 | tf_op jit(solution)/shard_map/pallas_call | solution.py:354
  60.3 0.8 copy-done.3
  61.1 0.8 copy-done.9
  61.9 4.7 %all-to-all-start.2 = ((bf16[128,2,8,128]{3,2,1,0:T(8,128)(2,1)}), bf16[128,2,8,128]{3,2,1,0:T(8,128)(2,1)}, u32[]{:S(2)}, u32[]{:S(2)}) async-start(bf16[128,2,8,128]{3,2,1,0:T(8,128)(2,1)} %copy-done.9), calls=%async_computation.2 | async-start | bytes 1048576 | tf_op jit(solution)/shard_map/all_to_all | solution.py:367
  66.6 1.5 collective-permute-start.3
  68.1 2.5 %collective-permute-start.4 = (bf16[3,2,128,128]{3,2,1,0:T(8,128)(2,1)}, bf16[3,2,128,128]{3,2,1,0:T(8,128)(2,1)S(1)}, u32[]{:S(2)}, u32[]{:S(2)}) collective-permute-start(bf16[3,2,128,128]{3,2,1,0:T(8,128)(2,1)} %get-tuple-element.55), channel_id=1, source_target_pairs={{0,2},{1,3},{2,0},{3,1},{4,6},{5,7},{6,4},{7,5},{8,10},{9,11},{10,... | collective-permute-start | bytes 589832 | tf_op jit(solution)/shard_map/ppermute | solution.py:415
  70.6 1.1 collective-permute-start.5
  71.7 7.6 %collective-permute-done.3.refs_9_ = bf16[3,2,128,128]{3,2,1,0:T(8,128)(2,1)S(1)} collective-permute-done((bf16[3,2,128,128]{3,2,1,0:T(8,128)(2,1)}, bf16[3,2,128,128]{3,2,1,0:T(8,128)(2,1)S(1)}, u32[]{:S(2)}, u32[]{:S(2)}) %collective-permute-start.3) | collective-permute-done | bytes 196640 | tf_op jit(solution)/shard_map/ppermute | solution.py:415
  79.3 4.8 %collective-permute-done.4.refs_10_ = bf16[3,2,128,128]{3,2,1,0:T(8,128)(2,1)S(1)} collective-permute-done((bf16[3,2,128,128]{3,2,1,0:T(8,128)(2,1)}, bf16[3,2,128,128]{3,2,1,0:T(8,128)(2,1)S(1)}, u32[]{:S(2)}, u32[]{:S(2)}) %collective-permute-start.4) | collective-permute-done | bytes 196640 | tf_op jit(solution)/shard_map/ppermute | solution.py:415
  84.1 0.7 copy-done.12
  84.8 0.0 collective-permute-done.5.refs_11_
  84.8 0.7 copy-done.14
  85.4 0.0 all-to-all-done.2
  85.5 0.9 copy-done.13
  86.4 0.9 copy-done.15
  87.3 0.9 copy-done.17
  88.2 0.9 copy-done.19
  89.1 1.0 copy-done.26
  90.2 1.0 copy-done.29
  91.2 0.9 copy-done.31
  92.2 0.9 copy-done.34
  93.1 0.9 copy-done.36
  94.0 5.3 %shard_map.132 = (bf16[32,4,8,128]{3,2,1,0:T(8,128)(2,1)S(1)}, f32[1024,128]{1,0:T(8,128)S(1)}, f32[512,128]{1,0:T(8,128)S(1)}, bf16[3,4,2,128,128]{4,3,2,1,0:T(8,128)(2,1)S(1)}) custom-call(bf16[32,4,2,8,128]{4,3,2,1,0:T(8,128)(2,1)} %bitcast.7.refs_0_, bf16[128,512]{1,0:T(8,128)(2,1)S(1)} %copy-done.17, bf16[512,128]{1,0:T(8,128)(2,1)S(1)} %copy-done.19, ...), custom_call_target="tpu_custom_call" | custom-call | flops 1200000000 | bytes 3000000 | tf_op jit(solution)/shard_map/pallas_call | solution.py:354
  99.3 18.0 %all_to_all.46.back = bf16[128,8,128]{2,1,0:T(8,128)(2,1)S(1)} all-to-all(bf16[128,8,128]{2,1,0:T(8,128)(2,1)S(1)} %bitcast.24), channel_id=1, replica_groups=mesh['band_0'=4,'band_1'=4,'band_2'=2,'lev'=4] {'band_0','band_1','band_..., dimensions={0} | all-to-all | bytes 524288 | tf_op jit(solution)/shard_map/all_to_all | solution.py:367
  117.3 2.2 shard_map.133
  119.5 17.8 %all_to_all.47 = bf16[128,2,8,128]{3,2,1,0:T(8,128)(2,1)S(1)} all-to-all(bf16[128,2,8,128]{3,2,1,0:T(8,128)(2,1)S(1)} %get-tuple-element.59), channel_id=1, replica_groups=mesh['band_0'=4,'band_1'=4,'band_2'=2,'lev'=4] {'band_0','band_1','band_..., dimensions={0} | all-to-all | bytes 1048576 | tf_op jit(solution)/shard_map/all_to_all | solution.py:367
  137.3 3.0 %shard_map.134 = (bf16[32,4,8,128]{3,2,1,0:T(8,128)(2,1)S(1)}, f32[1024,128]{1,0:T(8,128)S(1)}, f32[512,128]{1,0:T(8,128)S(1)}) custom-call(bf16[32,4,2,8,128]{4,3,2,1,0:T(8,128)(2,1)S(1)} %bitcast.22, bf16[128,512]{1,0:T(8,128)(2,1)S(1)} %copy-done.17, bf16[512,128]{1,0:T(8,128)(2,1)S(1)} %copy-done.19, bf16[512,512]{1,0:T(8,128)(2,1)S(1)} %copy-done.27, ...), custom_call_target="tpu_custom_call" | custom-call | flops 1200000000 | bytes 3000000 | tf_op jit(solution)/shard_map/pallas_call | solution.py:354
  140.3 14.6 %all_to_all.48.back = bf16[128,8,128]{2,1,0:T(8,128)(2,1)S(1)} all-to-all(bf16[128,8,128]{2,1,0:T(8,128)(2,1)S(1)} %bitcast.25), channel_id=1, replica_groups=mesh['band_0'=4,'band_1'=4,'band_2'=2,'lev'=4] {'band_0','band_1','band_..., dimensions={0} | all-to-all | bytes 524288 | tf_op jit(solution)/shard_map/all_to_all | solution.py:367
  154.9 2.2 shard_map.135
  157.1 0.0 copy-start.5
  157.1 0.8 copy-done.5
  157.9 17.8 %all_to_all.49 = bf16[128,2,8,128]{3,2,1,0:T(8,128)(2,1)S(1)} all-to-all(bf16[128,2,8,128]{3,2,1,0:T(8,128)(2,1)S(1)} %get-tuple-element.65), channel_id=1, replica_groups=mesh['band_0'=4,'band_1'=4,'band_2'=2,'lev'=4] {'band_0','band_1','band_..., dimensions={0} | all-to-all | bytes 1048576 | tf_op jit(solution)/shard_map/all_to_all | solution.py:367
  175.6 3.1 %shard_map.136 = (bf16[32,4,2,8,128]{4,3,2,1,0:T(8,128)(2,1)S(1)}, f32[8,128]{1,0:T(8,128)S(1)}) custom-call(bf16[32,4,2,8,128]{4,3,2,1,0:T(8,128)(2,1)S(1)} %bitcast.20, bf16[128,512]{1,0:T(8,128)(2,1)S(1)} %copy-done.17, bf16[512,128]{1,0:T(8,128)(2,1)S(1)} %copy-done.19, bf16[512,512]{1,0:T(8,128)(2,1)S(1)} %copy-done.27, ...), custom_call_target="tpu_custom_call" | custom-call | flops 1200000000 | bytes 3000000 | tf_op jit(solution)/shard_map/pallas_call | solution.py:354
  178.7 17.5 %all_to_all.50.back = bf16[128,2,8,128]{3,2,1,0:T(8,128)(2,1)S(1)} all-to-all(bf16[128,2,8,128]{3,2,1,0:T(8,128)(2,1)S(1)} %bitcast.21), channel_id=1, replica_groups=mesh['band_0'=4,'band_1'=4,'band_2'=2,'lev'=4] {'band_0','band_1','band_..., dimensions={0} | all-to-all | bytes 1048576 | tf_op jit(solution)/shard_map/all_to_all | solution.py:367
  196.2 1.0 shard_map.138
  197.2 3.5 %all-to-all-start.8 = ((bf16[128,2,8,128]{3,2,1,0:T(8,128)(2,1)}), bf16[128,2,8,128]{3,2,1,0:T(8,128)(2,1)S(1)}, u32[]{:S(2)}, u32[]{:S(2)}) async-start(bf16[128,2,8,128]{3,2,1,0:T(8,128)(2,1)} %shard_map.138), calls=%async_computation.8 | async-start | bytes 1048576 | tf_op jit(solution)/shard_map/all_to_all | solution.py:367
  200.8 1.3 shard_map.137
  202.1 12.9 %all-to-all-done.8.parts = bf16[128,2,8,128]{3,2,1,0:T(8,128)(2,1)S(1)} async-done(((bf16[128,2,8,128]{3,2,1,0:T(8,128)(2,1)}), bf16[128,2,8,128]{3,2,1,0:T(8,128)(2,1)S(1)}, u32[]{:S(2)}, u32[]{:S(2)}) %all-to-all-start.8) | async-done | bytes 524320 | tf_op jit(solution)/shard_map/all_to_all | solution.py:367
  215.0 0.8 shard_map.139
  (46 shorter events, 0.1 us)
Async XLA Ops:
  4.3 26.4 %copy-start.10 = (s32[256]{0:T(256)S(1)}, s32[256]{0:T(256)}, u32[]{:S(2)}) copy-start(s32[256]{0:T(256)} %waves.7) | copy-start | bytes 3076
  4.3 26.4 %copy-start.16 = (bf16[128,512]{1,0:T(8,128)(2,1)S(1)}, bf16[128,512]{1,0:T(8,128)(2,1)}, u32[]{:S(2)}) copy-start(bf16[128,512]{1,0:T(8,128)(2,1)} %refs_1_.7) | copy-start | bytes 393220
  4.3 26.4 %copy-start.18 = (bf16[512,128]{1,0:T(8,128)(2,1)S(1)}, bf16[512,128]{1,0:T(8,128)(2,1)}, u32[]{:S(2)}) copy-start(bf16[512,128]{1,0:T(8,128)(2,1)} %refs_2_.7) | copy-start | bytes 393220
  4.3 26.4 %copy-start.23 = (f32[512]{0:T(512)S(1)}, f32[512]{0:T(512)}, u32[]{:S(2)}) copy-start(f32[512]{0:T(512)} %param.18) | copy-start | bytes 6148
  4.3 25.6 %all-to-all-start = ((bf16[128,2,8,128]{3,2,1,0:T(8,128)(2,1)}), bf16[128,2,8,128]{3,2,1,0:T(8,128)(2,1)S(1)}, u32[]{:S(2)}, u32[]{:S(2)}) async-start(bf16[128,2,8,128]{3,2,1,0:T(8,128)(2,1)} %get-tuple-element.39), calls=%async_computation | async-start | bytes 1048576 | tf_op jit(solution)/shard_map/all_to_all | solution.py:367
  19.7 7.0 %collective-permute-start = (bf16[1,2,128,128]{3,2,1,0:T(8,128)(2,1)}, bf16[1,2,128,128]{3,2,1,0:T(8,128)(2,1)S(1)}, u32[]{:S(2)}, u32[]{:S(2)}) collective-permute-start(bf16[1,2,128,128]{3,2,1,0:T(8,128)(2,1)} %get-tuple-element.41), channel_id=1, source_target_pairs={{0,1},{1,2},{2,3},{3,0},{4,5},{5,6},{6,7},{7,4},{8,9},{9,10},{10,1... | collective-permute-start | bytes 196616 | tf_op jit(solution)/shard_map/ppermute | solution.py:415
  21.1 7.9 %collective-permute-start.1 = (bf16[1,2,128,128]{3,2,1,0:T(8,128)(2,1)}, bf16[1,2,128,128]{3,2,1,0:T(8,128)(2,1)S(1)}, u32[]{:S(2)}, u32[]{:S(2)}) collective-permute-start(bf16[1,2,128,128]{3,2,1,0:T(8,128)(2,1)} %get-tuple-element.42), channel_id=1, source_target_pairs={{0,2},{1,3},{2,0},{3,1},{4,6},{5,7},{6,4},{7,5},{8,10},{9,11},{10,... | collective-permute-start | bytes 196616 | tf_op jit(solution)/shard_map/ppermute | solution.py:415
  23.6 5.4 %collective-permute-start.2 = (bf16[1,2,128,128]{3,2,1,0:T(8,128)(2,1)}, bf16[1,2,128,128]{3,2,1,0:T(8,128)(2,1)S(1)}, u32[]{:S(2)}, u32[]{:S(2)}) collective-permute-start(bf16[1,2,128,128]{3,2,1,0:T(8,128)(2,1)} %get-tuple-element.43), channel_id=1, source_target_pairs={{0,3},{1,0},{2,1},{3,2},{4,7},{5,4},{6,5},{7,6},{8,11},{9,8},{10,9... | collective-permute-start | bytes 196616 | tf_op jit(solution)/shard_map/ppermute | solution.py:415
  29.0 0.6 copy-start.21
  29.9 0.8 copy-start.7
  30.7 1.0 copy-start.8
  31.8 0.8 copy-start.20
  32.6 0.8 copy-start.22
  33.4 1.0 copy-start.24
  34.5 23.6 %copy-start = (f32[4,4,8,2,8,256]{5,4,3,2,1,0:T(8,128)S(1)}, f32[4,4,8,2,8,256]{5,4,3,2,1,0:T(8,128)}, u32[]{:S(2)}) copy-start(f32[4,4,8,2,8,256]{5,4,3,2,1,0:T(8,128)} %param.10) | copy-start | bytes 6291460
  34.5 23.6 %copy-start.1 = (bf16[8,256,256]{2,1,0:T(8,128)(2,1)S(1)}, bf16[8,256,256]{2,1,0:T(8,128)(2,1)}, u32[]{:S(2)}) copy-start(bf16[8,256,256]{2,1,0:T(8,128)(2,1)} %get-tuple-element.46.table) | copy-start | bytes 3145732
  34.5 23.6 %copy-start.2 = (f32[8,64,256]{2,1,0:T(8,128)S(1)}, f32[8,64,256]{2,1,0:T(8,128)}, u32[]{:S(2)}) copy-start(f32[8,64,256]{2,1,0:T(8,128)} %get-tuple-element.45.damped_in) | copy-start | bytes 1572868
  38.3 22.0 %copy-start.25 = (bf16[512,512]{1,0:T(8,128)(2,1)}, bf16[512,512]{1,0:T(8,128)(2,1)S(1)}, u32[]{:S(2)}) copy-start(bf16[512,512]{1,0:T(8,128)(2,1)S(1)} %get-tuple-element.48.refs_3_) | copy-start | bytes 1572868
  38.3 22.0 %copy-start.28 = (f32[1024,128]{1,0:T(8,128)}, f32[1024,128]{1,0:T(8,128)S(1)}, u32[]{:S(2)}) copy-start(f32[1024,128]{1,0:T(8,128)S(1)} %get-tuple-element.51.refs_6_) | copy-start | bytes 1572868
  38.3 22.0 %copy-start.30 = (f32[512,128]{1,0:T(8,128)}, f32[512,128]{1,0:T(8,128)S(1)}, u32[]{:S(2)}) copy-start(f32[512,128]{1,0:T(8,128)S(1)} %get-tuple-element.50.refs_5_) | copy-start | bytes 786436
  38.3 22.0 %copy-start.33 = (f32[512,128]{1,0:T(8,128)}, f32[512,128]{1,0:T(8,128)S(1)}, u32[]{:S(2)}) copy-start(f32[512,128]{1,0:T(8,128)S(1)} %get-tuple-element.52.refs_7_) | copy-start | bytes 786436
  38.3 22.0 %copy-start.35 = (bf16[512,128]{1,0:T(8,128)(2,1)}, bf16[512,128]{1,0:T(8,128)(2,1)S(1)}, u32[]{:S(2)}) copy-start(bf16[512,128]{1,0:T(8,128)(2,1)S(1)} %get-tuple-element.49.refs_4_) | copy-start | bytes 393220
  58.0 27.4 %copy-start.11 = (bf16[3,2,128,128]{3,2,1,0:T(8,128)(2,1)S(1)}, bf16[3,2,128,128]{3,2,1,0:T(8,128)(2,1)}, u32[]{:S(2)}) copy-start(bf16[3,2,128,128]{3,2,1,0:T(8,128)(2,1)} %get-tuple-element.53.refs_8_) | copy-start | bytes 589828
  60.3 0.8 copy-start.3
  61.1 0.8 copy-start.9
  61.9 23.6 %all-to-all-start.2 = ((bf16[128,2,8,128]{3,2,1,0:T(8,128)(2,1)}), bf16[128,2,8,128]{3,2,1,0:T(8,128)(2,1)}, u32[]{:S(2)}, u32[]{:S(2)}) async-start(bf16[128,2,8,128]{3,2,1,0:T(8,128)(2,1)} %copy-done.9), calls=%async_computation.2 | async-start | bytes 1048576 | tf_op jit(solution)/shard_map/all_to_all | solution.py:367
  66.6 12.7 %collective-permute-start.3 = (bf16[3,2,128,128]{3,2,1,0:T(8,128)(2,1)}, bf16[3,2,128,128]{3,2,1,0:T(8,128)(2,1)S(1)}, u32[]{:S(2)}, u32[]{:S(2)}) collective-permute-start(bf16[3,2,128,128]{3,2,1,0:T(8,128)(2,1)} %get-tuple-element.54), channel_id=1, source_target_pairs={{0,1},{1,2},{2,3},{3,0},{4,5},{5,6},{6,7},{7,4},{8,9},{9,10},{10,1... | collective-permute-start | bytes 589832 | tf_op jit(solution)/shard_map/ppermute | solution.py:415
  68.1 16.0 %collective-permute-start.4 = (bf16[3,2,128,128]{3,2,1,0:T(8,128)(2,1)}, bf16[3,2,128,128]{3,2,1,0:T(8,128)(2,1)S(1)}, u32[]{:S(2)}, u32[]{:S(2)}) collective-permute-start(bf16[3,2,128,128]{3,2,1,0:T(8,128)(2,1)} %get-tuple-element.55), channel_id=1, source_target_pairs={{0,2},{1,3},{2,0},{3,1},{4,6},{5,7},{6,4},{7,5},{8,10},{9,11},{10,... | collective-permute-start | bytes 589832 | tf_op jit(solution)/shard_map/ppermute | solution.py:415
  70.6 14.2 %collective-permute-start.5 = (bf16[3,2,128,128]{3,2,1,0:T(8,128)(2,1)}, bf16[3,2,128,128]{3,2,1,0:T(8,128)(2,1)S(1)}, u32[]{:S(2)}, u32[]{:S(2)}) collective-permute-start(bf16[3,2,128,128]{3,2,1,0:T(8,128)(2,1)} %get-tuple-element.56), channel_id=1, source_target_pairs={{0,3},{1,0},{2,1},{3,2},{4,7},{5,4},{6,5},{7,6},{8,11},{9,8},{10,9... | collective-permute-start | bytes 589832 | tf_op jit(solution)/shard_map/ppermute | solution.py:415
  84.1 0.7 copy-start.12
  84.8 0.7 copy-start.14
  85.5 0.9 copy-start.13
  86.4 0.9 copy-start.15
  87.3 0.9 copy-start.17
  88.2 0.9 copy-start.19
  89.1 1.0 copy-start.26
  90.2 1.0 copy-start.29
  91.2 0.9 copy-start.31
  92.2 0.9 copy-start.34
  93.1 0.9 copy-start.36
  94.0 23.3 %copy-start.4 = (f32[8,64,256]{2,1,0:T(8,128)S(1)}, f32[8,64,256]{2,1,0:T(8,128)}, u32[]{:S(2)}) copy-start(f32[8,64,256]{2,1,0:T(8,128)} %copy-done.3) | copy-start | bytes 1572868
  117.3 20.0 %copy-start.27 = (bf16[512,512]{1,0:T(8,128)(2,1)S(1)}, bf16[512,512]{1,0:T(8,128)(2,1)}, u32[]{:S(2)}) copy-start(bf16[512,512]{1,0:T(8,128)(2,1)} %copy-done.25) | copy-start | bytes 1572868
  117.3 20.0 %copy-start.32 = (f32[512,128]{1,0:T(8,128)S(1)}, f32[512,128]{1,0:T(8,128)}, u32[]{:S(2)}) copy-start(f32[512,128]{1,0:T(8,128)} %copy-done.30) | copy-start | bytes 786436
  157.1 0.8 copy-start.5
  178.7 22.0 %copy-start.6 = (f32[8,64,256]{2,1,0:T(8,128)S(1)}, f32[8,64,256]{2,1,0:T(8,128)}, u32[]{:S(2)}) copy-start(f32[8,64,256]{2,1,0:T(8,128)} %copy-done.5) | copy-start | bytes 1572868
  197.2 17.8 %all-to-all-start.8 = ((bf16[128,2,8,128]{3,2,1,0:T(8,128)(2,1)}), bf16[128,2,8,128]{3,2,1,0:T(8,128)(2,1)S(1)}, u32[]{:S(2)}, u32[]{:S(2)}) async-start(bf16[128,2,8,128]{3,2,1,0:T(8,128)(2,1)} %shard_map.138), calls=%async_computation.8 | async-start | bytes 1048576 | tf_op jit(solution)/shard_map/all_to_all | solution.py:367

commit v4 on v3

--- a/solution.py
+++ b/solution.py
@@ -105,12 +105,12 @@
 
 
 def adjoint_rho(rows, table, rho):
-    back = rows[pl.ds(rho, DEV, stride=RHO), :].T
+    back = rows[pl.ds(rho, DEV, stride=RHO), :].astype(BF16).T
     halves = []
     for p in range(2):
         at = 2 * p * VL
         halves.append(jnp.concatenate([back[at : at + VL], back[at + VL : at + 2 * VL]], axis=1))
-    return mm(jnp.concatenate(halves, axis=0).astype(BF16), table)
+    return mm(jnp.concatenate(halves, axis=0), table)
 
 
 def turn_kernel(
@@ -148,16 +148,17 @@
 
 def share_kernel(back, bias_part, send):
     total = jnp.sum(back[:, 1].astype(F32), axis=0)
-    send[:, 0] = jnp.broadcast_to(total[None], (DEV, 8, 128)).astype(BF16)
-    send[:, 1] = jnp.broadcast_to(bias_part[...][None], (DEV, 8, 128)).astype(BF16)
-
-
-def ending_kernel(parts, w_in_out, w_out_out, bias_out):
-    rows = parts[:, 0].astype(F32).reshape(2 * HID, 128)
+    for part, rows in enumerate((total[:4], total[4:], bias_part[...])):
+        send[:, part] = jnp.broadcast_to(rows[None], (DEV, 4, 128)).astype(BF16)
+
+
+def ending_kernel(parts, w_in_out, w_out_out, bias_out, rows):
+    for d in range(DEV):
+        for half in range(2):
+            rows[8 * d + 4 * half : 8 * d + 4 * half + 4, :] = parts[d, half].astype(F32)
     w_in_out[...] = rows[:HID].T
     w_out_out[...] = rows[HID:]
-    total = jnp.sum(parts[:, 1].astype(F32), axis=0)
-    bias_out[...] = total[:4] + total[4:]
+    bias_out[...] = jnp.sum(parts[:, 2].astype(F32), axis=0)
 
 
 def fill_tables(waves, base, w_in, bias, trig, w_in_t, bias_wide):
@@ -176,9 +177,9 @@
     for k in range(4):
         to = lax.rem(lev + k, 4)
         for jj in range(2):
-            pieces = [obs[i, pl.ds(2 * to + jj, 32, stride=8), :] for i in range(4)]
+            pieces = [obs[i, pl.ds(2 * to + jj, 64, stride=8), :] for i in range(4)]
             for step in range(STEPS):
-                total = jnp.zeros((32, 128), F32)
+                total = jnp.zeros((64, 128), F32)
                 for i in range(4):
                     total += jnp.where(obs_time[i] == step, 1.0, 0.0).astype(F32) * pieces[i]
                 if step == STEPS - 1:
@@ -197,38 +198,21 @@
         obs_parts = take(4)
         (send,) = take(1)
         acc, accb, trig, w_in_t, bias = take(5)
-        turned, grid, grads, obs, sems = refs
+        turned, grid, grads, obs = refs
         lev = lax.axis_index("lev")
-        copies = [
-            pltpu.make_async_copy(obs_parts[k].at[0], obs.at[lax.rem(lev + 4 - k, 4)], sems.at[k])
-            for k in range(4)
-        ]
-        for copy in copies:
-            copy.start()
-        others = []
+        for k in range(4):
+            obs[lax.rem(lev + 4 - k, 4)] = obs_parts[k][0]
         fill_tables(waves, base, w_in, bias_row, trig, w_in_t, bias)
     else:
         trig, w_in_t, bias, acc_in, accb_in = take(5)
         if collect:
             obs_parts = take(4)
-            send, acc, accb, obs_all, turned, grid, grads, sems = refs
+            send, acc, accb, obs_all, turned, grid, grads = refs
             lev = lax.axis_index("lev")
-            copies, others = [], []
             for k in range(4):
-                to = lax.rem(lev + 4 - k, 4)
-                copies.append(
-                    pltpu.make_async_copy(obs_parts[k].at[step], obs_all.at[step, to], sems.at[k])
-                )
-                for s in range(step):
-                    others.append(
-                        pltpu.make_async_copy(
-                            obs_parts[k].at[s], obs_all.at[s, to], sems.at[4 * (s + 1) + k]
-                        )
-                    )
-            for copy in copies + others:
-                copy.start()
+                for s in range(STEPS - 1):
+                    obs_all[s, lax.rem(lev + 4 - k, 4)] = obs_parts[k][s]
         else:
-            copies, others = [], []
             obs_all, send = take(2)
             if last:
                 (bias_part,) = take(1)
@@ -256,9 +240,6 @@
         acc[...] = acc_in[...]
         accb[...] = accb_in[...]
 
-    for copy in copies:
-        copy.wait()
-
     def block(cb, carry):
         tangent = grid[0, cb]
         features = grid[1, cb]
@@ -306,8 +287,6 @@
                 send[:, 2 * pair + k, 0] = chunk
             else:
                 send[:, 2 * pair + k] = chunk
-    for copy in others:
-        copy.wait()
     if last:
         send[:, :, 1] = acc[...].reshape(32, 4, 8, 128).astype(BF16)
         ones = jnp.ones((8, 128), F32)
@@ -319,10 +298,7 @@
             precision=lax.Precision.HIGHEST,
         )
         for k in range(4):
-            part = sums[:1, k * 128 : (k + 1) * 128]
-            high = part.astype(BF16).astype(F32)
-            bias_part[k : k + 1, :] = high
-            bias_part[k + 4 : k + 5, :] = part - high
+            bias_part[k : k + 1, :] = sums[:1, k * 128 : (k + 1) * 128]
 
 
 VMEM = pl.BlockSpec(memory_space=pltpu.VMEM)
@@ -401,10 +377,10 @@
     obs_shapes = [(1, 2, FEAT, 128)] * 4 + [(STEPS - 1, 2, FEAT, 128)] * 4
     obs_parts = pl.pallas_call(
         obs_kernel,
-        grid=(4,),
+        grid=(2,),
         out_shape=[shape(d, BF16) for d in obs_shapes],
-        in_specs=[SMEM, pl.BlockSpec((4, 256, 128), lambda g: (0, g, 0))],
-        out_specs=[pl.BlockSpec(d[:2] + (32, 128), lambda g: (0, 0, g, 0)) for d in obs_shapes],
+        in_specs=[SMEM, pl.BlockSpec((4, 512, 128), lambda g: (0, g, 0))],
+        out_specs=[pl.BlockSpec(d[:2] + (64, 128), lambda g: (0, 0, g, 0)) for d in obs_shapes],
         cost_estimate=cost(10_000_000, 3_000_000),
         compiler_params=pltpu.CompilerParams(vmem_limit_bytes=BIG),
         name="obs",
@@ -431,22 +407,21 @@
         if first:
             ins += [wave_order.reshape(1, N), trig_base(), bias.reshape(1, HID)]
             outs += [shape((2 * N, LON), BF16), shape((HID, FEAT), BF16), shape((HID, 128), F32)]
-            scratch += [pltpu.VMEM((4, 2, FEAT, 128), BF16), pltpu.SemaphoreType.DMA((4,))]
-            specs = [whole(a.shape) for a in ins] + [HBM] * 4
+            scratch += [pltpu.VMEM((4, 2, FEAT, 128), BF16)]
             ins += obs_cols[:4]
+            specs = [whole(a.shape) for a in ins]
         else:
             ins += [trig, w_in_t, bias_wide, *sums]
             specs = [whole(a.shape) for a in ins]
             if step == STEPS - 2:
                 ins += obs_cols[4:]
-                specs += [HBM] * 4
+                specs = [whole(a.shape) for a in ins]
                 outs.append(shape((STEPS - 1, 4, 2, FEAT, 128), BF16))
-                scratch.append(pltpu.SemaphoreType.DMA((4 * (STEPS - 1),)))
             else:
                 ins.append(obs_all)
                 specs.append(whole(obs_all.shape))
         if last:
-            outs = [shape((32, 4, 2, RHO, 128), BF16), shape((8, 128), F32)]
+            outs = [shape((32, 4, 2, RHO, 128), BF16), shape((4, 128), F32)]
             scratch = [pltpu.VMEM(a.shape, F32) for a in acc_shapes] + scratch
         back, *sums = call(
             functools.partial(column_kernel, first, last, step),
@@ -483,7 +458,7 @@
     parts = call(
         share_kernel,
         (back, bias_part),
-        chunks,
+        shape((DEV, 3, 4, 128), BF16),
         [],
         [whole(back.shape), whole(bias_part.shape)],
         1_000_000,
@@ -503,7 +478,7 @@
         ending_kernel,
         (parts,),
         (shape((FEAT, HID), F32), shape((HID, FEAT), F32), shape((4, 128), F32)),
-        [],
+        [tall],
         [whole(parts.shape)],
         1_000_000,
         1_500_000,

time: 217 us -> 213 us (0.982)
  Pallas kernels: 32.3 us -> 29.5 us
where the time goes in v4:
time: 213 us; the launch traced here: 212 us
  blocking collectives  104 us (49%)
  starting transfers between devices  29.8 us (14%)
  Pallas kernels  29.5 us (14%)
  waiting for transfers between devices  29.4 us (14%)
  local copies, waits for them, and re-layouts  17.5 us (8%)
    all_to_all x6, blocking collectives, exchange(): return lax.all_to_all(array, axes, split_axis=0, concat_axis=0, tiled=True)  104 us
    pallas_call x11, Pallas kernels, call(): pl.pallas_call(body, grid=(1,), out_shape=outs_list if many else outs, in...  26.5 us
    all_to_all x3, starting transfers between devices, exchange(): return lax.all_to_all(array, axes, split_axis=0, concat_axis=0, tiled=True)  19.8 us
    unnamed x74, local copies, waits for them, and re-layouts  17.5 us
    ppermute x6, waiting for transfers between devices, program(): part = lax.ppermute(part, 'lev', [(i, (i + k) % 4) for i in range(4)])  16.9 us
    all_to_all x3, waiting for transfers between devices, exchange(): return lax.all_to_all(array, axes, split_axis=0, concat_axis=0, tiled=True)  12.5 us
    ppermute x6, starting transfers between devices, program(): part = lax.ppermute(part, 'lev', [(i, (i + k) % 4) for i in range(4)])  10.1 us
  transfers between devices with their start and end apart: 9, of which 6 were waited for; matrix products, arithmetic and copies ran while one was open for 0% of the time, Pallas kernels for 2%

profile of v4, /device:TPU:1, one launch (start us, length us, event | category | flops | bytes accessed | tf_op | source)
XLA Modules:
  0.0 211.6 jit_solution(9947323101806782369)
XLA Ops:
  0.6 3.6 %shard_map.129 = (bf16[128,2,8,128]{3,2,1,0:T(8,128)(2,1)}, f32[8,64,256]{2,1,0:T(8,128)}, bf16[8,256,256]{2,1,0:T(8,128)(2,1)}) custom-call(s32[256]{0:T(256)} %waves.7, bf16[8,256,256]{2,1,0:T(8,128)(2,1)} %legendre.1, f32[512,256]{1,0:T(8,128)} %bitcast.30, f32[4,512,256]{2,1,0:T(8,128)} %bitcast.15), custom_call_target="tpu_custom_call" | custom-call | flops 300000000 | bytes 4000000 | tf_op jit(solution)/shard_map/pallas_call | solution.py:330
  4.3 0.0 copy-start.23
  4.3 11.5 %all-to-all-start = ((bf16[128,2,8,128]{3,2,1,0:T(8,128)(2,1)}), bf16[128,2,8,128]{3,2,1,0:T(8,128)(2,1)S(1)}, u32[]{:S(2)}, u32[]{:S(2)}) async-start(bf16[128,2,8,128]{3,2,1,0:T(8,128)(2,1)} %get-tuple-element.39), calls=%async_computation | async-start | bytes 1048576 | tf_op jit(solution)/shard_map/all_to_all | solution.py:343
  15.8 3.0 %obs.1 = (bf16[1,2,128,128]{3,2,1,0:T(8,128)(2,1)}, bf16[1,2,128,128]{3,2,1,0:T(8,128)(2,1)}, bf16[1,2,128,128]{3,2,1,0:T(8,128)(2,1)}, bf16[1,2,128,128]{3,2,1,...) custom-call(s32[4]{0:T(128)} %obs_time.1, ...), custom_call_target="tpu_custom_call" | custom-call | flops 10000000 | bytes 3000000 | tf_op jit(solution)/shard_map/obs/pallas_call | solution.py:378
  18.8 1.4 collective-permute-start
  20.2 2.5 %collective-permute-start.1 = (bf16[1,2,128,128]{3,2,1,0:T(8,128)(2,1)}, bf16[1,2,128,128]{3,2,1,0:T(8,128)(2,1)S(1)}, u32[]{:S(2)}, u32[]{:S(2)}) collective-permute-start(bf16[1,2,128,128]{3,2,1,0:T(8,128)(2,1)} %get-tuple-element.42), channel_id=1, source_target_pairs={{0,2},{1,3},{2,0},{3,1},{4,6},{5,7},{6,4},{7,5},{8,10},{9,11},{10,... | collective-permute-start | bytes 196616 | tf_op jit(solution)/shard_map/ppermute | solution.py:391
  22.6 1.1 collective-permute-start.2
  23.7 3.0 %collective-permute-done.refs_7_ = bf16[1,2,128,128]{3,2,1,0:T(8,128)(2,1)S(1)} collective-permute-done((bf16[1,2,128,128]{3,2,1,0:T(8,128)(2,1)}, bf16[1,2,128,128]{3,2,1,0:T(8,128)(2,1)S(1)}, u32[]{:S(2)}, u32[]{:S(2)}) %collective-permute-start) | collective-permute-done | bytes 65568 | tf_op jit(solution)/shard_map/ppermute | solution.py:391
  26.7 1.6 collective-permute-done.1.refs_8_
  28.3 0.0 collective-permute-done.2.refs_9_
  28.3 0.6 copy-done.21
  28.9 1.0 all-to-all-done
  29.9 0.8 copy-done.7
  30.7 0.0 copy-done.10
  30.7 0.0 copy-done.18
  30.7 1.0 copy-done.8
  31.7 0.8 copy-done.20
  32.6 0.8 copy-done.22
  33.4 1.0 copy-done.24
  34.5 3.2 %shard_map.130 = (bf16[32,4,8,128]{3,2,1,0:T(8,128)(2,1)S(1)}, f32[1024,128]{1,0:T(8,128)S(1)}, f32[512,128]{1,0:T(8,128)S(1)}, bf16[512,512]{1,0:T(8,128)(2,1)S...) custom-call(bf16[32,4,2,8,128]{4,3,2,1,0:T(8,128)(2,1)S(1)} %bitcast.19, bf16[128,512]{1,0:T(8,128)(2,1)S(1)} %copy-done.16, ...), custom_call_target="tpu_custom_call" | custom-call | flops 1200000000 | bytes 3000000 | tf_op jit(solution)/shard_map/pallas_call | solution.py:330
  37.7 0.0 copy-start.30
  37.7 0.0 copy-start.33
  37.8 0.0 copy-start.35
  37.8 18.7 %all_to_all.45.back = bf16[128,8,128]{2,1,0:T(8,128)(2,1)S(1)} all-to-all(bf16[128,8,128]{2,1,0:T(8,128)(2,1)S(1)} %bitcast.23), channel_id=1, replica_groups=mesh['band_0'=4,'band_1'=4,'band_2'=2,'lev'=4] {'band_0','band_1','band_..., dimensions={0} | all-to-all | bytes 524288 | tf_op jit(solution)/shard_map/all_to_all | solution.py:343
  56.5 0.0 copy-done.2
  56.5 2.2 %shard_map.131 = (bf16[128,2,8,128]{3,2,1,0:T(8,128)(2,1)S(1)}, f32[8,64,256]{2,1,0:T(8,128)S(1)}) custom-call(s32[256]{0:T(256)S(1)} %copy-done.10, bf16[128,8,128]{2,1,0:T(8,128)(2,1)S(1)} %all_to_all.45.back, f32[8,64,256]{2,1,0:T(8,128)S(1)} %copy-done.2, bf16[8,256,256]{2,1,0:T(8,128)(2,1)S(1)} %copy-done.1, f32[4,512,256]{2,1,0:T(8,128)S(1)} %bitcast.16), custom_call_target="tpu_custom_call" | custom-call | flops 400000000 | bytes 4000000 | tf_op jit(solution)/shard_map/pallas_call | solution.py:330
  58.7 0.8 copy-done.3
  59.5 0.8 copy-done.9
  60.3 4.7 %all-to-all-start.2 = ((bf16[128,2,8,128]{3,2,1,0:T(8,128)(2,1)}), bf16[128,2,8,128]{3,2,1,0:T(8,128)(2,1)}, u32[]{:S(2)}, u32[]{:S(2)}) async-start(bf16[128,2,8,128]{3,2,1,0:T(8,128)(2,1)} %copy-done.9), calls=%async_computation.2 | async-start | bytes 1048576 | tf_op jit(solution)/shard_map/all_to_all | solution.py:343
  65.0 1.5 collective-permute-start.3
  66.5 2.5 %collective-permute-start.4 = (bf16[3,2,128,128]{3,2,1,0:T(8,128)(2,1)}, bf16[3,2,128,128]{3,2,1,0:T(8,128)(2,1)S(1)}, u32[]{:S(2)}, u32[]{:S(2)}) collective-permute-start(bf16[3,2,128,128]{3,2,1,0:T(8,128)(2,1)} %get-tuple-element.55), channel_id=1, source_target_pairs={{0,2},{1,3},{2,0},{3,1},{4,6},{5,7},{6,4},{7,5},{8,10},{9,11},{10,... | collective-permute-start | bytes 589832 | tf_op jit(solution)/shard_map/ppermute | solution.py:391
  69.1 1.1 collective-permute-start.5
  70.2 7.6 %collective-permute-done.3.refs_9_ = bf16[3,2,128,128]{3,2,1,0:T(8,128)(2,1)S(1)} collective-permute-done((bf16[3,2,128,128]{3,2,1,0:T(8,128)(2,1)}, bf16[3,2,128,128]{3,2,1,0:T(8,128)(2,1)S(1)}, u32[]{:S(2)}, u32[]{:S(2)}) %collective-permute-start.3) | collective-permute-done | bytes 196640 | tf_op jit(solution)/shard_map/ppermute | solution.py:391
  77.7 4.8 %collective-permute-done.4.refs_10_ = bf16[3,2,128,128]{3,2,1,0:T(8,128)(2,1)S(1)} collective-permute-done((bf16[3,2,128,128]{3,2,1,0:T(8,128)(2,1)}, bf16[3,2,128,128]{3,2,1,0:T(8,128)(2,1)S(1)}, u32[]{:S(2)}, u32[]{:S(2)}) %collective-permute-start.4) | collective-permute-done | bytes 196640 | tf_op jit(solution)/shard_map/ppermute | solution.py:391
  82.5 0.7 copy-done.12
  83.2 0.0 collective-permute-done.5.refs_11_
  83.2 0.7 copy-done.14
  83.9 0.0 all-to-all-done.2
  83.9 0.9 copy-done.13
  84.8 0.9 copy-done.15
  85.8 0.9 copy-done.17
  86.7 0.9 copy-done.19
  87.6 1.0 copy-done.26
  88.6 1.0 copy-done.29
  89.7 0.9 copy-done.31
  90.6 0.9 copy-done.34
  91.6 0.9 copy-done.36
  92.5 4.1 %shard_map.132 = (bf16[32,4,8,128]{3,2,1,0:T(8,128)(2,1)S(1)}, f32[1024,128]{1,0:T(8,128)S(1)}, f32[512,128]{1,0:T(8,128)S(1)}, bf16[3,4,2,128,128]{4,3,2,1,0:T(8,128)(2,1)S(1)}) custom-call(bf16[32,4,2,8,128]{4,3,2,1,0:T(8,128)(2,1)} %bitcast.7.refs_0_, bf16[128,512]{1,0:T(8,128)(2,1)S(1)} %copy-done.17, bf16[512,128]{1,0:T(8,128)(2,1)S(1)} %copy-done.19, ...), custom_call_target="tpu_custom_call" | custom-call | flops 1200000000 | bytes 3000000 | tf_op jit(solution)/shard_map/pallas_call | solution.py:330
  96.5 18.0 %all_to_all.46.back = bf16[128,8,128]{2,1,0:T(8,128)(2,1)S(1)} all-to-all(bf16[128,8,128]{2,1,0:T(8,128)(2,1)S(1)} %bitcast.24), channel_id=1, replica_groups=mesh['band_0'=4,'band_1'=4,'band_2'=2,'lev'=4] {'band_0','band_1','band_..., dimensions={0} | all-to-all | bytes 524288 | tf_op jit(solution)/shard_map/all_to_all | solution.py:343
  114.5 2.1 %shard_map.133 = (bf16[128,2,8,128]{3,2,1,0:T(8,128)(2,1)S(1)}, f32[8,64,256]{2,1,0:T(8,128)S(1)}) custom-call(s32[256]{0:T(256)S(1)} %copy-done.10, bf16[128,8,128]{2,1,0:T(8,128)(2,1)S(1)} %all_to_all.46.back, f32[8,64,256]{2,1,0:T(8,128)S(1)} %copy-done.4, bf16[8,256,256]{2,1,0:T(8,128)(2,1)S(1)} %copy-done.1, f32[4,512,256]{2,1,0:T(8,128)S(1)} %bitcast.17), custom_call_target="tpu_custom_call" | custom-call | flops 400000000 | bytes 4000000 | tf_op jit(solution)/shard_map/pallas_call | solution.py:330
  116.7 17.8 %all_to_all.47 = bf16[128,2,8,128]{3,2,1,0:T(8,128)(2,1)S(1)} all-to-all(bf16[128,2,8,128]{3,2,1,0:T(8,128)(2,1)S(1)} %get-tuple-element.59), channel_id=1, replica_groups=mesh['band_0'=4,'band_1'=4,'band_2'=2,'lev'=4] {'band_0','band_1','band_..., dimensions={0} | all-to-all | bytes 1048576 | tf_op jit(solution)/shard_map/all_to_all | solution.py:343
  134.5 2.9 %shard_map.134 = (bf16[32,4,8,128]{3,2,1,0:T(8,128)(2,1)S(1)}, f32[1024,128]{1,0:T(8,128)S(1)}, f32[512,128]{1,0:T(8,128)S(1)}) custom-call(bf16[32,4,2,8,128]{4,3,2,1,0:T(8,128)(2,1)S(1)} %bitcast.22, bf16[128,512]{1,0:T(8,128)(2,1)S(1)} %copy-done.17, bf16[512,128]{1,0:T(8,128)(2,1)S(1)} %copy-done.19, bf16[512,512]{1,0:T(8,128)(2,1)S(1)} %copy-done.27, ...), custom_call_target="tpu_custom_call" | custom-call | flops 1200000000 | bytes 3000000 | tf_op jit(solution)/shard_map/pallas_call | solution.py:330
  137.4 14.7 %all_to_all.48.back = bf16[128,8,128]{2,1,0:T(8,128)(2,1)S(1)} all-to-all(bf16[128,8,128]{2,1,0:T(8,128)(2,1)S(1)} %bitcast.25), channel_id=1, replica_groups=mesh['band_0'=4,'band_1'=4,'band_2'=2,'lev'=4] {'band_0','band_1','band_..., dimensions={0} | all-to-all | bytes 524288 | tf_op jit(solution)/shard_map/all_to_all | solution.py:343
  152.1 2.1 %shard_map.135 = (bf16[128,2,8,128]{3,2,1,0:T(8,128)(2,1)S(1)}, f32[8,64,256]{2,1,0:T(8,128)S(1)}) custom-call(s32[256]{0:T(256)S(1)} %copy-done.10, bf16[128,8,128]{2,1,0:T(8,128)(2,1)S(1)} %all_to_all.48.back, f32[8,64,256]{2,1,0:T(8,128)S(1)} %get-tuple-element.64.damped_in, bf16[8,256,256]{2,1,0:T(8,128)(2,1)S(1)} %copy-done.1, f32[4,512,256]{2,1,0:T(8,128)S(1)} %bitcast.18), custom_call_target="tpu_custom_call" | custom-call | flops 400000000 | bytes 4000000 | tf_op jit(solution)/shard_map/pallas_call | solution.py:330
  154.2 0.0 copy-start.5
  154.3 0.8 copy-done.5
  155.0 17.8 %all_to_all.49 = bf16[128,2,8,128]{3,2,1,0:T(8,128)(2,1)S(1)} all-to-all(bf16[128,2,8,128]{3,2,1,0:T(8,128)(2,1)S(1)} %get-tuple-element.65), channel_id=1, replica_groups=mesh['band_0'=4,'band_1'=4,'band_2'=2,'lev'=4] {'band_0','band_1','band_..., dimensions={0} | all-to-all | bytes 1048576 | tf_op jit(solution)/shard_map/all_to_all | solution.py:343
  172.8 3.1 %shard_map.136 = (bf16[32,4,2,8,128]{4,3,2,1,0:T(8,128)(2,1)S(1)}, f32[4,128]{1,0:T(4,128)S(1)}) custom-call(bf16[32,4,2,8,128]{4,3,2,1,0:T(8,128)(2,1)S(1)} %bitcast.20, bf16[128,512]{1,0:T(8,128)(2,1)S(1)} %copy-done.17, bf16[512,128]{1,0:T(8,128)(2,1)S(1)} %copy-done.19, bf16[512,512]{1,0:T(8,128)(2,1)S(1)} %copy-done.27, ...), custom_call_target="tpu_custom_call" | custom-call | flops 1200000000 | bytes 3000000 | tf_op jit(solution)/shard_map/pallas_call | solution.py:330
  175.9 17.5 %all_to_all.50.back = bf16[128,2,8,128]{3,2,1,0:T(8,128)(2,1)S(1)} all-to-all(bf16[128,2,8,128]{3,2,1,0:T(8,128)(2,1)S(1)} %bitcast.21), channel_id=1, replica_groups=mesh['band_0'=4,'band_1'=4,'band_2'=2,'lev'=4] {'band_0','band_1','band_..., dimensions={0} | all-to-all | bytes 1048576 | tf_op jit(solution)/shard_map/all_to_all | solution.py:343
  193.4 1.0 shard_map.138
  194.4 3.6 %all-to-all-start.8 = ((bf16[128,3,4,128]{3,2,1,0:T(4,128)(2,1)}), bf16[128,3,4,128]{3,2,1,0:T(4,128)(2,1)S(1)}, u32[]{:S(2)}, u32[]{:S(2)}) async-start(bf16[128,3,4,128]{3,2,1,0:T(4,128)(2,1)} %shard_map.138), calls=%async_computation.8 | async-start | bytes 786432 | tf_op jit(solution)/shard_map/all_to_all | solution.py:343
  197.9 1.3 shard_map.137
  199.2 11.5 %all-to-all-done.8.parts = bf16[128,3,4,128]{3,2,1,0:T(4,128)(2,1)S(1)} async-done(((bf16[128,3,4,128]{3,2,1,0:T(4,128)(2,1)}), bf16[128,3,4,128]{3,2,1,0:T(4,128)(2,1)S(1)}, u32[]{:S(2)}, u32[]{:S(2)}) %all-to-all-start.8) | async-done | bytes 393248 | tf_op jit(solution)/shard_map/all_to_all | solution.py:343
  210.8 0.8 shard_map.139
  (46 shorter events, 0.1 us)
Async XLA Ops:
  4.3 26.4 %copy-start.10 = (s32[256]{0:T(256)S(1)}, s32[256]{0:T(256)}, u32[]{:S(2)}) copy-start(s32[256]{0:T(256)} %waves.7) | copy-start | bytes 3076
  4.3 26.4 %copy-start.16 = (bf16[128,512]{1,0:T(8,128)(2,1)S(1)}, bf16[128,512]{1,0:T(8,128)(2,1)}, u32[]{:S(2)}) copy-start(bf16[128,512]{1,0:T(8,128)(2,1)} %refs_1_.7) | copy-start | bytes 393220
  4.3 26.4 %copy-start.18 = (bf16[512,128]{1,0:T(8,128)(2,1)S(1)}, bf16[512,128]{1,0:T(8,128)(2,1)}, u32[]{:S(2)}) copy-start(bf16[512,128]{1,0:T(8,128)(2,1)} %refs_2_.7) | copy-start | bytes 393220
  4.3 26.4 %copy-start.23 = (f32[512]{0:T(512)S(1)}, f32[512]{0:T(512)}, u32[]{:S(2)}) copy-start(f32[512]{0:T(512)} %param.18) | copy-start | bytes 6148
  4.3 25.6 %all-to-all-start = ((bf16[128,2,8,128]{3,2,1,0:T(8,128)(2,1)}), bf16[128,2,8,128]{3,2,1,0:T(8,128)(2,1)S(1)}, u32[]{:S(2)}, u32[]{:S(2)}) async-start(bf16[128,2,8,128]{3,2,1,0:T(8,128)(2,1)} %get-tuple-element.39), calls=%async_computation | async-start | bytes 1048576 | tf_op jit(solution)/shard_map/all_to_all | solution.py:343
  18.8 7.9 %collective-permute-start = (bf16[1,2,128,128]{3,2,1,0:T(8,128)(2,1)}, bf16[1,2,128,128]{3,2,1,0:T(8,128)(2,1)S(1)}, u32[]{:S(2)}, u32[]{:S(2)}) collective-permute-start(bf16[1,2,128,128]{3,2,1,0:T(8,128)(2,1)} %get-tuple-element.41), channel_id=1, source_target_pairs={{0,1},{1,2},{2,3},{3,0},{4,5},{5,6},{6,7},{7,4},{8,9},{9,10},{10,1... | collective-permute-start | bytes 196616 | tf_op jit(solution)/shard_map/ppermute | solution.py:391
  20.2 8.1 %collective-permute-start.1 = (bf16[1,2,128,128]{3,2,1,0:T(8,128)(2,1)}, bf16[1,2,128,128]{3,2,1,0:T(8,128)(2,1)S(1)}, u32[]{:S(2)}, u32[]{:S(2)}) collective-permute-start(bf16[1,2,128,128]{3,2,1,0:T(8,128)(2,1)} %get-tuple-element.42), channel_id=1, source_target_pairs={{0,2},{1,3},{2,0},{3,1},{4,6},{5,7},{6,4},{7,5},{8,10},{9,11},{10,... | collective-permute-start | bytes 196616 | tf_op jit(solution)/shard_map/ppermute | solution.py:391
  22.6 5.7 %collective-permute-start.2 = (bf16[1,2,128,128]{3,2,1,0:T(8,128)(2,1)}, bf16[1,2,128,128]{3,2,1,0:T(8,128)(2,1)S(1)}, u32[]{:S(2)}, u32[]{:S(2)}) collective-permute-start(bf16[1,2,128,128]{3,2,1,0:T(8,128)(2,1)} %get-tuple-element.43), channel_id=1, source_target_pairs={{0,3},{1,0},{2,1},{3,2},{4,7},{5,4},{6,5},{7,6},{8,11},{9,8},{10,9... | collective-permute-start | bytes 196616 | tf_op jit(solution)/shard_map/ppermute | solution.py:391
  28.3 0.6 copy-start.21
  29.9 0.8 copy-start.7
  30.7 1.0 copy-start.8
  31.7 0.8 copy-start.20
  32.6 0.8 copy-start.22
  33.4 1.0 copy-start.24
  34.5 22.0 %copy-start = (f32[4,4,8,2,8,256]{5,4,3,2,1,0:T(8,128)S(1)}, f32[4,4,8,2,8,256]{5,4,3,2,1,0:T(8,128)}, u32[]{:S(2)}) copy-start(f32[4,4,8,2,8,256]{5,4,3,2,1,0:T(8,128)} %param.10) | copy-start | bytes 6291460
  34.5 22.0 %copy-start.1 = (bf16[8,256,256]{2,1,0:T(8,128)(2,1)S(1)}, bf16[8,256,256]{2,1,0:T(8,128)(2,1)}, u32[]{:S(2)}) copy-start(bf16[8,256,256]{2,1,0:T(8,128)(2,1)} %get-tuple-element.46.table) | copy-start | bytes 3145732
  34.5 22.0 %copy-start.2 = (f32[8,64,256]{2,1,0:T(8,128)S(1)}, f32[8,64,256]{2,1,0:T(8,128)}, u32[]{:S(2)}) copy-start(f32[8,64,256]{2,1,0:T(8,128)} %get-tuple-element.45.damped_in) | copy-start | bytes 1572868
  37.7 20.9 %copy-start.25 = (bf16[512,512]{1,0:T(8,128)(2,1)}, bf16[512,512]{1,0:T(8,128)(2,1)S(1)}, u32[]{:S(2)}) copy-start(bf16[512,512]{1,0:T(8,128)(2,1)S(1)} %get-tuple-element.48.refs_3_) | copy-start | bytes 1572868
  37.7 20.9 %copy-start.28 = (f32[1024,128]{1,0:T(8,128)}, f32[1024,128]{1,0:T(8,128)S(1)}, u32[]{:S(2)}) copy-start(f32[1024,128]{1,0:T(8,128)S(1)} %get-tuple-element.51.refs_6_) | copy-start | bytes 1572868
  37.7 20.9 %copy-start.30 = (f32[512,128]{1,0:T(8,128)}, f32[512,128]{1,0:T(8,128)S(1)}, u32[]{:S(2)}) copy-start(f32[512,128]{1,0:T(8,128)S(1)} %get-tuple-element.50.refs_5_) | copy-start | bytes 786436
  37.7 20.9 %copy-start.33 = (f32[512,128]{1,0:T(8,128)}, f32[512,128]{1,0:T(8,128)S(1)}, u32[]{:S(2)}) copy-start(f32[512,128]{1,0:T(8,128)S(1)} %get-tuple-element.52.refs_7_) | copy-start | bytes 786436
  37.8 20.9 %copy-start.35 = (bf16[512,128]{1,0:T(8,128)(2,1)}, bf16[512,128]{1,0:T(8,128)(2,1)S(1)}, u32[]{:S(2)}) copy-start(bf16[512,128]{1,0:T(8,128)(2,1)S(1)} %get-tuple-element.49.refs_4_) | copy-start | bytes 393220
  56.5 27.4 %copy-start.11 = (bf16[3,2,128,128]{3,2,1,0:T(8,128)(2,1)S(1)}, bf16[3,2,128,128]{3,2,1,0:T(8,128)(2,1)}, u32[]{:S(2)}) copy-start(bf16[3,2,128,128]{3,2,1,0:T(8,128)(2,1)} %get-tuple-element.53.refs_8_) | copy-start | bytes 589828
  58.7 0.8 copy-start.3
  59.5 0.8 copy-start.9
  60.3 23.6 %all-to-all-start.2 = ((bf16[128,2,8,128]{3,2,1,0:T(8,128)(2,1)}), bf16[128,2,8,128]{3,2,1,0:T(8,128)(2,1)}, u32[]{:S(2)}, u32[]{:S(2)}) async-start(bf16[128,2,8,128]{3,2,1,0:T(8,128)(2,1)} %copy-done.9), calls=%async_computation.2 | async-start | bytes 1048576 | tf_op jit(solution)/shard_map/all_to_all | solution.py:343
  65.0 12.7 %collective-permute-start.3 = (bf16[3,2,128,128]{3,2,1,0:T(8,128)(2,1)}, bf16[3,2,128,128]{3,2,1,0:T(8,128)(2,1)S(1)}, u32[]{:S(2)}, u32[]{:S(2)}) collective-permute-start(bf16[3,2,128,128]{3,2,1,0:T(8,128)(2,1)} %get-tuple-element.54), channel_id=1, source_target_pairs={{0,1},{1,2},{2,3},{3,0},{4,5},{5,6},{6,7},{7,4},{8,9},{9,10},{10,1... | collective-permute-start | bytes 589832 | tf_op jit(solution)/shard_map/ppermute | solution.py:391
  66.5 16.0 %collective-permute-start.4 = (bf16[3,2,128,128]{3,2,1,0:T(8,128)(2,1)}, bf16[3,2,128,128]{3,2,1,0:T(8,128)(2,1)S(1)}, u32[]{:S(2)}, u32[]{:S(2)}) collective-permute-start(bf16[3,2,128,128]{3,2,1,0:T(8,128)(2,1)} %get-tuple-element.55), channel_id=1, source_target_pairs={{0,2},{1,3},{2,0},{3,1},{4,6},{5,7},{6,4},{7,5},{8,10},{9,11},{10,... | collective-permute-start | bytes 589832 | tf_op jit(solution)/shard_map/ppermute | solution.py:391
  69.1 14.2 %collective-permute-start.5 = (bf16[3,2,128,128]{3,2,1,0:T(8,128)(2,1)}, bf16[3,2,128,128]{3,2,1,0:T(8,128)(2,1)S(1)}, u32[]{:S(2)}, u32[]{:S(2)}) collective-permute-start(bf16[3,2,128,128]{3,2,1,0:T(8,128)(2,1)} %get-tuple-element.56), channel_id=1, source_target_pairs={{0,3},{1,0},{2,1},{3,2},{4,7},{5,4},{6,5},{7,6},{8,11},{9,8},{10,9... | collective-permute-start | bytes 589832 | tf_op jit(solution)/shard_map/ppermute | solution.py:391
  82.5 0.7 copy-start.12
  83.2 0.7 copy-start.14
  83.9 0.9 copy-start.13
  84.8 0.9 copy-start.15
  85.8 0.9 copy-start.17
  86.7 0.9 copy-start.19
  87.6 1.0 copy-start.26
  88.6 1.0 copy-start.29
  89.7 0.9 copy-start.31
  90.6 0.9 copy-start.34
  91.6 0.9 copy-start.36
  92.5 22.1 %copy-start.4 = (f32[8,64,256]{2,1,0:T(8,128)S(1)}, f32[8,64,256]{2,1,0:T(8,128)}, u32[]{:S(2)}) copy-start(f32[8,64,256]{2,1,0:T(8,128)} %copy-done.3) | copy-start | bytes 1572868
  114.5 20.0 %copy-start.27 = (bf16[512,512]{1,0:T(8,128)(2,1)S(1)}, bf16[512,512]{1,0:T(8,128)(2,1)}, u32[]{:S(2)}) copy-start(bf16[512,512]{1,0:T(8,128)(2,1)} %copy-done.25) | copy-start | bytes 1572868
  114.5 20.0 %copy-start.32 = (f32[512,128]{1,0:T(8,128)S(1)}, f32[512,128]{1,0:T(8,128)}, u32[]{:S(2)}) copy-start(f32[512,128]{1,0:T(8,128)} %copy-done.30) | copy-start | bytes 786436
  154.2 0.8 copy-start.5
  175.9 22.0 %copy-start.6 = (f32[8,64,256]{2,1,0:T(8,128)S(1)}, f32[8,64,256]{2,1,0:T(8,128)}, u32[]{:S(2)}) copy-start(f32[8,64,256]{2,1,0:T(8,128)} %copy-done.5) | copy-start | bytes 1572868
  194.4 16.4 %all-to-all-start.8 = ((bf16[128,3,4,128]{3,2,1,0:T(4,128)(2,1)}), bf16[128,3,4,128]{3,2,1,0:T(4,128)(2,1)S(1)}, u32[]{:S(2)}, u32[]{:S(2)}) async-start(bf16[128,3,4,128]{3,2,1,0:T(4,128)(2,1)} %shard_map.138), calls=%async_computation.8 | async-start | bytes 786432 | tf_op jit(solution)/shard_map/all_to_all | solution.py:343

commit v5 on v4

--- a/solution.py
+++ b/solution.py
@@ -244,8 +244,8 @@
         tangent = grid[0, cb]
         features = grid[1, cb]
         back = jnp.zeros((FEAT, 256), F32)
-        for hb in range(2):
-            rows = slice(hb * 256, (hb + 1) * 256)
+        for hb in range(1):
+            rows = slice(hb * 512, (hb + 1) * 512)
             wide = bias[rows, :]
             pre = mm(w_in_t[rows, :], features) + jnp.concatenate([wide, wide], axis=1)
             logistic = 0.5 * jnp.tanh(0.5 * pre) + 0.5
@@ -253,7 +253,7 @@
             pre_grad = mm(w_out[rows, :], tangent) * (logistic * (1.0 + pre * (1.0 - logistic)))
             low = pre_grad.astype(BF16)
             acc[rows, :] += mm_nt(low, features)
-            acc[hb * 256 + HID : (hb + 1) * 256 + HID, :] += mm_nt(hidden, tangent)
+            acc[hb * 512 + HID : (hb + 1) * 512 + HID, :] += mm_nt(hidden, tangent)
             accb[rows, :] += pre_grad[:, :128] + pre_grad[:, 128:]
             back += mm(w_in[:, rows], low)
         jj = cb // 2

time: 213 us -> 211 us (level)
  no operation moved by 1% of the time
where the time goes in v5:
time: 211 us; the launch traced here: 210 us
  blocking collectives  104 us (49%)
  starting transfers between devices  29.8 us (14%)
  waiting for transfers between devices  29.4 us (14%)
  Pallas kernels  28 us (13%)
  local copies, waits for them, and re-layouts  17.5 us (8%)
    all_to_all x6, blocking collectives, exchange(): return lax.all_to_all(array, axes, split_axis=0, concat_axis=0, tiled=True)  104 us
    pallas_call x11, Pallas kernels, call(): pl.pallas_call(body, grid=(1,), out_shape=outs_list if many else outs, in...  25 us
    all_to_all x3, starting transfers between devices, exchange(): return lax.all_to_all(array, axes, split_axis=0, concat_axis=0, tiled=True)  19.8 us
    unnamed x74, local copies, waits for them, and re-layouts  17.5 us
    ppermute x6, waiting for transfers between devices, program(): part = lax.ppermute(part, 'lev', [(i, (i + k) % 4) for i in range(4)])  16.9 us
    all_to_all x3, waiting for transfers between devices, exchange(): return lax.all_to_all(array, axes, split_axis=0, concat_axis=0, tiled=True)  12.5 us
    ppermute x6, starting transfers between devices, program(): part = lax.ppermute(part, 'lev', [(i, (i + k) % 4) for i in range(4)])  10.1 us
  transfers between devices with their start and end apart: 9, of which 6 were waited for; matrix products, arithmetic and copies ran while one was open for 0% of the time, Pallas kernels for 2%

profile of v5, /device:TPU:1, one launch (start us, length us, event | category | flops | bytes accessed | tf_op | source)
XLA Modules:
  0.0 210.0 jit_solution(4800901934804450750)
XLA Ops:
  0.6 3.6 %shard_map.129 = (bf16[128,2,8,128]{3,2,1,0:T(8,128)(2,1)}, f32[8,64,256]{2,1,0:T(8,128)}, bf16[8,256,256]{2,1,0:T(8,128)(2,1)}) custom-call(s32[256]{0:T(256)} %waves.7, bf16[8,256,256]{2,1,0:T(8,128)(2,1)} %legendre.1, f32[512,256]{1,0:T(8,128)} %bitcast.30, f32[4,512,256]{2,1,0:T(8,128)} %bitcast.15), custom_call_target="tpu_custom_call" | custom-call | flops 300000000 | bytes 4000000 | tf_op jit(solution)/shard_map/pallas_call | solution.py:330
  4.3 0.0 copy-start.23
  4.3 11.5 %all-to-all-start = ((bf16[128,2,8,128]{3,2,1,0:T(8,128)(2,1)}), bf16[128,2,8,128]{3,2,1,0:T(8,128)(2,1)S(1)}, u32[]{:S(2)}, u32[]{:S(2)}) async-start(bf16[128,2,8,128]{3,2,1,0:T(8,128)(2,1)} %get-tuple-element.39), calls=%async_computation | async-start | bytes 1048576 | tf_op jit(solution)/shard_map/all_to_all | solution.py:343
  15.8 3.0 %obs.1 = (bf16[1,2,128,128]{3,2,1,0:T(8,128)(2,1)}, bf16[1,2,128,128]{3,2,1,0:T(8,128)(2,1)}, bf16[1,2,128,128]{3,2,1,0:T(8,128)(2,1)}, bf16[1,2,128,128]{3,2,1,...) custom-call(s32[4]{0:T(128)} %obs_time.1, ...), custom_call_target="tpu_custom_call" | custom-call | flops 10000000 | bytes 3000000 | tf_op jit(solution)/shard_map/obs/pallas_call | solution.py:378
  18.8 1.4 collective-permute-start
  20.2 2.5 %collective-permute-start.1 = (bf16[1,2,128,128]{3,2,1,0:T(8,128)(2,1)}, bf16[1,2,128,128]{3,2,1,0:T(8,128)(2,1)S(1)}, u32[]{:S(2)}, u32[]{:S(2)}) collective-permute-start(bf16[1,2,128,128]{3,2,1,0:T(8,128)(2,1)} %get-tuple-element.42), channel_id=1, source_target_pairs={{0,2},{1,3},{2,0},{3,1},{4,6},{5,7},{6,4},{7,5},{8,10},{9,11},{10,... | collective-permute-start | bytes 196616 | tf_op jit(solution)/shard_map/ppermute | solution.py:391
  22.6 1.1 collective-permute-start.2
  23.7 3.0 %collective-permute-done.refs_7_ = bf16[1,2,128,128]{3,2,1,0:T(8,128)(2,1)S(1)} collective-permute-done((bf16[1,2,128,128]{3,2,1,0:T(8,128)(2,1)}, bf16[1,2,128,128]{3,2,1,0:T(8,128)(2,1)S(1)}, u32[]{:S(2)}, u32[]{:S(2)}) %collective-permute-start) | collective-permute-done | bytes 65568 | tf_op jit(solution)/shard_map/ppermute | solution.py:391
  26.7 1.6 collective-permute-done.1.refs_8_
  28.3 0.0 collective-permute-done.2.refs_9_
  28.3 0.6 copy-done.21
  28.9 1.0 all-to-all-done
  29.9 0.8 copy-done.7
  30.7 0.0 copy-done.10
  30.7 0.0 copy-done.18
  30.7 1.0 copy-done.8
  31.7 0.8 copy-done.20
  32.6 0.8 copy-done.22
  33.4 1.0 copy-done.24
  34.5 2.8 %shard_map.130 = (bf16[32,4,8,128]{3,2,1,0:T(8,128)(2,1)S(1)}, f32[1024,128]{1,0:T(8,128)S(1)}, f32[512,128]{1,0:T(8,128)S(1)}, bf16[512,512]{1,0:T(8,128)(2,1)S...) custom-call(bf16[32,4,2,8,128]{4,3,2,1,0:T(8,128)(2,1)S(1)} %bitcast.19, bf16[128,512]{1,0:T(8,128)(2,1)S(1)} %copy-done.16, ...), custom_call_target="tpu_custom_call" | custom-call | flops 1200000000 | bytes 3000000 | tf_op jit(solution)/shard_map/pallas_call | solution.py:330
  37.3 0.0 copy-start.30
  37.3 0.0 copy-start.33
  37.3 18.7 %all_to_all.45.back = bf16[128,8,128]{2,1,0:T(8,128)(2,1)S(1)} all-to-all(bf16[128,8,128]{2,1,0:T(8,128)(2,1)S(1)} %bitcast.23), channel_id=1, replica_groups=mesh['band_0'=4,'band_1'=4,'band_2'=2,'lev'=4] {'band_0','band_1','band_..., dimensions={0} | all-to-all | bytes 524288 | tf_op jit(solution)/shard_map/all_to_all | solution.py:343
  56.0 0.0 copy-done.2
  56.1 2.2 %shard_map.131 = (bf16[128,2,8,128]{3,2,1,0:T(8,128)(2,1)S(1)}, f32[8,64,256]{2,1,0:T(8,128)S(1)}) custom-call(s32[256]{0:T(256)S(1)} %copy-done.10, bf16[128,8,128]{2,1,0:T(8,128)(2,1)S(1)} %all_to_all.45.back, f32[8,64,256]{2,1,0:T(8,128)S(1)} %copy-done.2, bf16[8,256,256]{2,1,0:T(8,128)(2,1)S(1)} %copy-done.1, f32[4,512,256]{2,1,0:T(8,128)S(1)} %bitcast.16), custom_call_target="tpu_custom_call" | custom-call | flops 400000000 | bytes 4000000 | tf_op jit(solution)/shard_map/pallas_call | solution.py:330
  58.2 0.0 copy-done.25
  58.3 0.8 copy-done.3
  59.1 0.8 copy-done.9
  59.9 4.7 %all-to-all-start.2 = ((bf16[128,2,8,128]{3,2,1,0:T(8,128)(2,1)}), bf16[128,2,8,128]{3,2,1,0:T(8,128)(2,1)}, u32[]{:S(2)}, u32[]{:S(2)}) async-start(bf16[128,2,8,128]{3,2,1,0:T(8,128)(2,1)} %copy-done.9), calls=%async_computation.2 | async-start | bytes 1048576 | tf_op jit(solution)/shard_map/all_to_all | solution.py:343
  64.6 1.5 collective-permute-start.3
  66.1 2.5 %collective-permute-start.4 = (bf16[3,2,128,128]{3,2,1,0:T(8,128)(2,1)}, bf16[3,2,128,128]{3,2,1,0:T(8,128)(2,1)S(1)}, u32[]{:S(2)}, u32[]{:S(2)}) collective-permute-start(bf16[3,2,128,128]{3,2,1,0:T(8,128)(2,1)} %get-tuple-element.55), channel_id=1, source_target_pairs={{0,2},{1,3},{2,0},{3,1},{4,6},{5,7},{6,4},{7,5},{8,10},{9,11},{10,... | collective-permute-start | bytes 589832 | tf_op jit(solution)/shard_map/ppermute | solution.py:391
  68.6 1.1 collective-permute-start.5
  69.7 7.6 %collective-permute-done.3.refs_9_ = bf16[3,2,128,128]{3,2,1,0:T(8,128)(2,1)S(1)} collective-permute-done((bf16[3,2,128,128]{3,2,1,0:T(8,128)(2,1)}, bf16[3,2,128,128]{3,2,1,0:T(8,128)(2,1)S(1)}, u32[]{:S(2)}, u32[]{:S(2)}) %collective-permute-start.3) | collective-permute-done | bytes 196640 | tf_op jit(solution)/shard_map/ppermute | solution.py:391
  77.3 4.8 %collective-permute-done.4.refs_10_ = bf16[3,2,128,128]{3,2,1,0:T(8,128)(2,1)S(1)} collective-permute-done((bf16[3,2,128,128]{3,2,1,0:T(8,128)(2,1)}, bf16[3,2,128,128]{3,2,1,0:T(8,128)(2,1)S(1)}, u32[]{:S(2)}, u32[]{:S(2)}) %collective-permute-start.4) | collective-permute-done | bytes 196640 | tf_op jit(solution)/shard_map/ppermute | solution.py:391
  82.1 0.7 copy-done.12
  82.8 0.0 collective-permute-done.5.refs_11_
  82.8 0.7 copy-done.14
  83.5 0.0 all-to-all-done.2
  83.5 0.9 copy-done.13
  84.4 0.9 copy-done.15
  85.3 0.9 copy-done.17
  86.2 0.9 copy-done.19
  87.1 1.0 copy-done.26
  88.2 1.0 copy-done.29
  89.2 0.9 copy-done.31
  90.2 0.9 copy-done.34
  91.1 0.9 copy-done.36
  92.0 3.7 %shard_map.132 = (bf16[32,4,8,128]{3,2,1,0:T(8,128)(2,1)S(1)}, f32[1024,128]{1,0:T(8,128)S(1)}, f32[512,128]{1,0:T(8,128)S(1)}, bf16[3,4,2,128,128]{4,3,2,1,0:T(8,128)(2,1)S(1)}) custom-call(bf16[32,4,2,8,128]{4,3,2,1,0:T(8,128)(2,1)} %bitcast.7.refs_0_, bf16[128,512]{1,0:T(8,128)(2,1)S(1)} %copy-done.17, bf16[512,128]{1,0:T(8,128)(2,1)S(1)} %copy-done.19, ...), custom_call_target="tpu_custom_call" | custom-call | flops 1200000000 | bytes 3000000 | tf_op jit(solution)/shard_map/pallas_call | solution.py:330
  95.7 18.0 %all_to_all.46.back = bf16[128,8,128]{2,1,0:T(8,128)(2,1)S(1)} all-to-all(bf16[128,8,128]{2,1,0:T(8,128)(2,1)S(1)} %bitcast.24), channel_id=1, replica_groups=mesh['band_0'=4,'band_1'=4,'band_2'=2,'lev'=4] {'band_0','band_1','band_..., dimensions={0} | all-to-all | bytes 524288 | tf_op jit(solution)/shard_map/all_to_all | solution.py:343
  113.7 2.2 %shard_map.133 = (bf16[128,2,8,128]{3,2,1,0:T(8,128)(2,1)S(1)}, f32[8,64,256]{2,1,0:T(8,128)S(1)}) custom-call(s32[256]{0:T(256)S(1)} %copy-done.10, bf16[128,8,128]{2,1,0:T(8,128)(2,1)S(1)} %all_to_all.46.back, f32[8,64,256]{2,1,0:T(8,128)S(1)} %copy-done.4, bf16[8,256,256]{2,1,0:T(8,128)(2,1)S(1)} %copy-done.1, f32[4,512,256]{2,1,0:T(8,128)S(1)} %bitcast.17), custom_call_target="tpu_custom_call" | custom-call | flops 400000000 | bytes 4000000 | tf_op jit(solution)/shard_map/pallas_call | solution.py:330
  115.9 17.8 %all_to_all.47 = bf16[128,2,8,128]{3,2,1,0:T(8,128)(2,1)S(1)} all-to-all(bf16[128,2,8,128]{3,2,1,0:T(8,128)(2,1)S(1)} %get-tuple-element.59), channel_id=1, replica_groups=mesh['band_0'=4,'band_1'=4,'band_2'=2,'lev'=4] {'band_0','band_1','band_..., dimensions={0} | all-to-all | bytes 1048576 | tf_op jit(solution)/shard_map/all_to_all | solution.py:343
  133.7 2.6 %shard_map.134 = (bf16[32,4,8,128]{3,2,1,0:T(8,128)(2,1)S(1)}, f32[1024,128]{1,0:T(8,128)S(1)}, f32[512,128]{1,0:T(8,128)S(1)}) custom-call(bf16[32,4,2,8,128]{4,3,2,1,0:T(8,128)(2,1)S(1)} %bitcast.22, bf16[128,512]{1,0:T(8,128)(2,1)S(1)} %copy-done.17, bf16[512,128]{1,0:T(8,128)(2,1)S(1)} %copy-done.19, bf16[512,512]{1,0:T(8,128)(2,1)S(1)} %copy-done.27, ...), custom_call_target="tpu_custom_call" | custom-call | flops 1200000000 | bytes 3000000 | tf_op jit(solution)/shard_map/pallas_call | solution.py:330
  136.2 14.6 %all_to_all.48.back = bf16[128,8,128]{2,1,0:T(8,128)(2,1)S(1)} all-to-all(bf16[128,8,128]{2,1,0:T(8,128)(2,1)S(1)} %bitcast.25), channel_id=1, replica_groups=mesh['band_0'=4,'band_1'=4,'band_2'=2,'lev'=4] {'band_0','band_1','band_..., dimensions={0} | all-to-all | bytes 524288 | tf_op jit(solution)/shard_map/all_to_all | solution.py:343
  150.9 2.2 %shard_map.135 = (bf16[128,2,8,128]{3,2,1,0:T(8,128)(2,1)S(1)}, f32[8,64,256]{2,1,0:T(8,128)S(1)}) custom-call(s32[256]{0:T(256)S(1)} %copy-done.10, bf16[128,8,128]{2,1,0:T(8,128)(2,1)S(1)} %all_to_all.48.back, f32[8,64,256]{2,1,0:T(8,128)S(1)} %get-tuple-element.64.damped_in, bf16[8,256,256]{2,1,0:T(8,128)(2,1)S(1)} %copy-done.1, f32[4,512,256]{2,1,0:T(8,128)S(1)} %bitcast.18), custom_call_target="tpu_custom_call" | custom-call | flops 400000000 | bytes 4000000 | tf_op jit(solution)/shard_map/pallas_call | solution.py:330
  153.0 0.0 copy-start.5
  153.1 0.8 copy-done.5
  153.8 17.8 %all_to_all.49 = bf16[128,2,8,128]{3,2,1,0:T(8,128)(2,1)S(1)} all-to-all(bf16[128,2,8,128]{3,2,1,0:T(8,128)(2,1)S(1)} %get-tuple-element.65), channel_id=1, replica_groups=mesh['band_0'=4,'band_1'=4,'band_2'=2,'lev'=4] {'band_0','band_1','band_..., dimensions={0} | all-to-all | bytes 1048576 | tf_op jit(solution)/shard_map/all_to_all | solution.py:343
  171.6 2.7 %shard_map.136 = (bf16[32,4,2,8,128]{4,3,2,1,0:T(8,128)(2,1)S(1)}, f32[4,128]{1,0:T(4,128)S(1)}) custom-call(bf16[32,4,2,8,128]{4,3,2,1,0:T(8,128)(2,1)S(1)} %bitcast.20, bf16[128,512]{1,0:T(8,128)(2,1)S(1)} %copy-done.17, bf16[512,128]{1,0:T(8,128)(2,1)S(1)} %copy-done.19, bf16[512,512]{1,0:T(8,128)(2,1)S(1)} %copy-done.27, ...), custom_call_target="tpu_custom_call" | custom-call | flops 1200000000 | bytes 3000000 | tf_op jit(solution)/shard_map/pallas_call | solution.py:330
  174.4 17.5 %all_to_all.50.back = bf16[128,2,8,128]{3,2,1,0:T(8,128)(2,1)S(1)} all-to-all(bf16[128,2,8,128]{3,2,1,0:T(8,128)(2,1)S(1)} %bitcast.21), channel_id=1, replica_groups=mesh['band_0'=4,'band_1'=4,'band_2'=2,'lev'=4] {'band_0','band_1','band_..., dimensions={0} | all-to-all | bytes 1048576 | tf_op jit(solution)/shard_map/all_to_all | solution.py:343
  191.8 1.0 shard_map.138
  192.8 3.6 %all-to-all-start.8 = ((bf16[128,3,4,128]{3,2,1,0:T(4,128)(2,1)}), bf16[128,3,4,128]{3,2,1,0:T(4,128)(2,1)S(1)}, u32[]{:S(2)}, u32[]{:S(2)}) async-start(bf16[128,3,4,128]{3,2,1,0:T(4,128)(2,1)} %shard_map.138), calls=%async_computation.8 | async-start | bytes 786432 | tf_op jit(solution)/shard_map/all_to_all | solution.py:343
  196.4 1.3 shard_map.137
  197.7 11.5 %all-to-all-done.8.parts = bf16[128,3,4,128]{3,2,1,0:T(4,128)(2,1)S(1)} async-done(((bf16[128,3,4,128]{3,2,1,0:T(4,128)(2,1)}), bf16[128,3,4,128]{3,2,1,0:T(4,128)(2,1)S(1)}, u32[]{:S(2)}, u32[]{:S(2)}) %all-to-all-start.8) | async-done | bytes 393248 | tf_op jit(solution)/shard_map/all_to_all | solution.py:343
  209.2 0.8 shard_map.139
  (46 shorter events, 0.1 us)
Async XLA Ops:
  4.3 26.4 %copy-start.10 = (s32[256]{0:T(256)S(1)}, s32[256]{0:T(256)}, u32[]{:S(2)}) copy-start(s32[256]{0:T(256)} %waves.7) | copy-start | bytes 3076
  4.3 26.4 %copy-start.16 = (bf16[128,512]{1,0:T(8,128)(2,1)S(1)}, bf16[128,512]{1,0:T(8,128)(2,1)}, u32[]{:S(2)}) copy-start(bf16[128,512]{1,0:T(8,128)(2,1)} %refs_1_.7) | copy-start | bytes 393220
  4.3 26.4 %copy-start.18 = (bf16[512,128]{1,0:T(8,128)(2,1)S(1)}, bf16[512,128]{1,0:T(8,128)(2,1)}, u32[]{:S(2)}) copy-start(bf16[512,128]{1,0:T(8,128)(2,1)} %refs_2_.7) | copy-start | bytes 393220
  4.3 26.4 %copy-start.23 = (f32[512]{0:T(512)S(1)}, f32[512]{0:T(512)}, u32[]{:S(2)}) copy-start(f32[512]{0:T(512)} %param.18) | copy-start | bytes 6148
  4.3 25.6 %all-to-all-start = ((bf16[128,2,8,128]{3,2,1,0:T(8,128)(2,1)}), bf16[128,2,8,128]{3,2,1,0:T(8,128)(2,1)S(1)}, u32[]{:S(2)}, u32[]{:S(2)}) async-start(bf16[128,2,8,128]{3,2,1,0:T(8,128)(2,1)} %get-tuple-element.39), calls=%async_computation | async-start | bytes 1048576 | tf_op jit(solution)/shard_map/all_to_all | solution.py:343
  18.8 7.9 %collective-permute-start = (bf16[1,2,128,128]{3,2,1,0:T(8,128)(2,1)}, bf16[1,2,128,128]{3,2,1,0:T(8,128)(2,1)S(1)}, u32[]{:S(2)}, u32[]{:S(2)}) collective-permute-start(bf16[1,2,128,128]{3,2,1,0:T(8,128)(2,1)} %get-tuple-element.41), channel_id=1, source_target_pairs={{0,1},{1,2},{2,3},{3,0},{4,5},{5,6},{6,7},{7,4},{8,9},{9,10},{10,1... | collective-permute-start | bytes 196616 | tf_op jit(solution)/shard_map/ppermute | solution.py:391
  20.2 8.1 %collective-permute-start.1 = (bf16[1,2,128,128]{3,2,1,0:T(8,128)(2,1)}, bf16[1,2,128,128]{3,2,1,0:T(8,128)(2,1)S(1)}, u32[]{:S(2)}, u32[]{:S(2)}) collective-permute-start(bf16[1,2,128,128]{3,2,1,0:T(8,128)(2,1)} %get-tuple-element.42), channel_id=1, source_target_pairs={{0,2},{1,3},{2,0},{3,1},{4,6},{5,7},{6,4},{7,5},{8,10},{9,11},{10,... | collective-permute-start | bytes 196616 | tf_op jit(solution)/shard_map/ppermute | solution.py:391
  22.6 5.7 %collective-permute-start.2 = (bf16[1,2,128,128]{3,2,1,0:T(8,128)(2,1)}, bf16[1,2,128,128]{3,2,1,0:T(8,128)(2,1)S(1)}, u32[]{:S(2)}, u32[]{:S(2)}) collective-permute-start(bf16[1,2,128,128]{3,2,1,0:T(8,128)(2,1)} %get-tuple-element.43), channel_id=1, source_target_pairs={{0,3},{1,0},{2,1},{3,2},{4,7},{5,4},{6,5},{7,6},{8,11},{9,8},{10,9... | collective-permute-start | bytes 196616 | tf_op jit(solution)/shard_map/ppermute | solution.py:391
  28.3 0.6 copy-start.21
  29.9 0.8 copy-start.7
  30.7 1.0 copy-start.8
  31.7 0.8 copy-start.20
  32.6 0.8 copy-start.22
  33.4 1.0 copy-start.24
  34.5 21.6 %copy-start = (f32[4,4,8,2,8,256]{5,4,3,2,1,0:T(8,128)S(1)}, f32[4,4,8,2,8,256]{5,4,3,2,1,0:T(8,128)}, u32[]{:S(2)}) copy-start(f32[4,4,8,2,8,256]{5,4,3,2,1,0:T(8,128)} %param.10) | copy-start | bytes 6291460
  34.5 21.6 %copy-start.1 = (bf16[8,256,256]{2,1,0:T(8,128)(2,1)S(1)}, bf16[8,256,256]{2,1,0:T(8,128)(2,1)}, u32[]{:S(2)}) copy-start(bf16[8,256,256]{2,1,0:T(8,128)(2,1)} %get-tuple-element.46.table) | copy-start | bytes 3145732
  34.5 21.6 %copy-start.2 = (f32[8,64,256]{2,1,0:T(8,128)S(1)}, f32[8,64,256]{2,1,0:T(8,128)}, u32[]{:S(2)}) copy-start(f32[8,64,256]{2,1,0:T(8,128)} %get-tuple-element.45.damped_in) | copy-start | bytes 1572868
  37.3 21.0 %copy-start.25 = (bf16[512,512]{1,0:T(8,128)(2,1)}, bf16[512,512]{1,0:T(8,128)(2,1)S(1)}, u32[]{:S(2)}) copy-start(bf16[512,512]{1,0:T(8,128)(2,1)S(1)} %get-tuple-element.48.refs_3_) | copy-start | bytes 1572868
  37.3 21.0 %copy-start.28 = (f32[1024,128]{1,0:T(8,128)}, f32[1024,128]{1,0:T(8,128)S(1)}, u32[]{:S(2)}) copy-start(f32[1024,128]{1,0:T(8,128)S(1)} %get-tuple-element.51.refs_6_) | copy-start | bytes 1572868
  37.3 21.0 %copy-start.30 = (f32[512,128]{1,0:T(8,128)}, f32[512,128]{1,0:T(8,128)S(1)}, u32[]{:S(2)}) copy-start(f32[512,128]{1,0:T(8,128)S(1)} %get-tuple-element.50.refs_5_) | copy-start | bytes 786436
  37.3 21.0 %copy-start.33 = (f32[512,128]{1,0:T(8,128)}, f32[512,128]{1,0:T(8,128)S(1)}, u32[]{:S(2)}) copy-start(f32[512,128]{1,0:T(8,128)S(1)} %get-tuple-element.52.refs_7_) | copy-start | bytes 786436
  37.3 21.0 %copy-start.35 = (bf16[512,128]{1,0:T(8,128)(2,1)}, bf16[512,128]{1,0:T(8,128)(2,1)S(1)}, u32[]{:S(2)}) copy-start(bf16[512,128]{1,0:T(8,128)(2,1)S(1)} %get-tuple-element.49.refs_4_) | copy-start | bytes 393220
  56.1 27.4 %copy-start.11 = (bf16[3,2,128,128]{3,2,1,0:T(8,128)(2,1)S(1)}, bf16[3,2,128,128]{3,2,1,0:T(8,128)(2,1)}, u32[]{:S(2)}) copy-start(bf16[3,2,128,128]{3,2,1,0:T(8,128)(2,1)} %get-tuple-element.53.refs_8_) | copy-start | bytes 589828
  58.3 0.8 copy-start.3
  59.1 0.8 copy-start.9
  59.9 23.6 %all-to-all-start.2 = ((bf16[128,2,8,128]{3,2,1,0:T(8,128)(2,1)}), bf16[128,2,8,128]{3,2,1,0:T(8,128)(2,1)}, u32[]{:S(2)}, u32[]{:S(2)}) async-start(bf16[128,2,8,128]{3,2,1,0:T(8,128)(2,1)} %copy-done.9), calls=%async_computation.2 | async-start | bytes 1048576 | tf_op jit(solution)/shard_map/all_to_all | solution.py:343
  64.6 12.7 %collective-permute-start.3 = (bf16[3,2,128,128]{3,2,1,0:T(8,128)(2,1)}, bf16[3,2,128,128]{3,2,1,0:T(8,128)(2,1)S(1)}, u32[]{:S(2)}, u32[]{:S(2)}) collective-permute-start(bf16[3,2,128,128]{3,2,1,0:T(8,128)(2,1)} %get-tuple-element.54), channel_id=1, source_target_pairs={{0,1},{1,2},{2,3},{3,0},{4,5},{5,6},{6,7},{7,4},{8,9},{9,10},{10,1... | collective-permute-start | bytes 589832 | tf_op jit(solution)/shard_map/ppermute | solution.py:391
  66.1 16.0 %collective-permute-start.4 = (bf16[3,2,128,128]{3,2,1,0:T(8,128)(2,1)}, bf16[3,2,128,128]{3,2,1,0:T(8,128)(2,1)S(1)}, u32[]{:S(2)}, u32[]{:S(2)}) collective-permute-start(bf16[3,2,128,128]{3,2,1,0:T(8,128)(2,1)} %get-tuple-element.55), channel_id=1, source_target_pairs={{0,2},{1,3},{2,0},{3,1},{4,6},{5,7},{6,4},{7,5},{8,10},{9,11},{10,... | collective-permute-start | bytes 589832 | tf_op jit(solution)/shard_map/ppermute | solution.py:391
  68.6 14.2 %collective-permute-start.5 = (bf16[3,2,128,128]{3,2,1,0:T(8,128)(2,1)}, bf16[3,2,128,128]{3,2,1,0:T(8,128)(2,1)S(1)}, u32[]{:S(2)}, u32[]{:S(2)}) collective-permute-start(bf16[3,2,128,128]{3,2,1,0:T(8,128)(2,1)} %get-tuple-element.56), channel_id=1, source_target_pairs={{0,3},{1,0},{2,1},{3,2},{4,7},{5,4},{6,5},{7,6},{8,11},{9,8},{10,9... | collective-permute-start | bytes 589832 | tf_op jit(solution)/shard_map/ppermute | solution.py:391
  82.1 0.7 copy-start.12
  82.8 0.7 copy-start.14
  83.5 0.9 copy-start.13
  84.4 0.9 copy-start.15
  85.3 0.9 copy-start.17
  86.2 0.9 copy-start.19
  87.1 1.0 copy-start.26
  88.2 1.0 copy-start.29
  89.2 0.9 copy-start.31
  90.2 0.9 copy-start.34
  91.1 0.9 copy-start.36
  92.0 21.7 %copy-start.4 = (f32[8,64,256]{2,1,0:T(8,128)S(1)}, f32[8,64,256]{2,1,0:T(8,128)}, u32[]{:S(2)}) copy-start(f32[8,64,256]{2,1,0:T(8,128)} %copy-done.3) | copy-start | bytes 1572868
  113.7 20.0 %copy-start.27 = (bf16[512,512]{1,0:T(8,128)(2,1)S(1)}, bf16[512,512]{1,0:T(8,128)(2,1)}, u32[]{:S(2)}) copy-start(bf16[512,512]{1,0:T(8,128)(2,1)} %copy-done.25) | copy-start | bytes 1572868
  113.7 20.0 %copy-start.32 = (f32[512,128]{1,0:T(8,128)S(1)}, f32[512,128]{1,0:T(8,128)}, u32[]{:S(2)}) copy-start(f32[512,128]{1,0:T(8,128)} %copy-done.30) | copy-start | bytes 786436
  153.0 0.8 copy-start.5
  174.3 22.0 %copy-start.6 = (f32[8,64,256]{2,1,0:T(8,128)S(1)}, f32[8,64,256]{2,1,0:T(8,128)}, u32[]{:S(2)}) copy-start(f32[8,64,256]{2,1,0:T(8,128)} %copy-done.5) | copy-start | bytes 1572868
  192.8 16.4 %all-to-all-start.8 = ((bf16[128,3,4,128]{3,2,1,0:T(4,128)(2,1)}), bf16[128,3,4,128]{3,2,1,0:T(4,128)(2,1)S(1)}, u32[]{:S(2)}, u32[]{:S(2)}) async-start(bf16[128,3,4,128]{3,2,1,0:T(4,128)(2,1)} %shard_map.138), calls=%async_computation.8 | async-start | bytes 786432 | tf_op jit(solution)/shard_map/all_to_all | solution.py:343

commit v6 on v5

--- a/solution.py
+++ b/solution.py
@@ -121,11 +121,11 @@
     rows[...] = back[...].astype(F32).reshape(DEV * RHO, 128)
     halve(states.at[step], state_rows)
     for rho in range(RHO):
-        now = damping * (damped_in[rho] + adjoint_rho(rows, table[rho], rho))
-        damped[rho] = now
+        damped[rho] = damping * (damped_in[rho] + adjoint_rho(rows, table[rho], rho))
+    for rho in range(RHO):
         synth_rho(
             table[rho],
-            now * tangent_scale(waves[band * RHO + rho]),
+            damped[rho] * tangent_scale(waves[band * RHO + rho]),
             strided_rows(state_rows, rho),
             rho,
             rows_t,

time: 211 us -> 209 us (level)
  Pallas kernels: 28 us -> 25.8 us
    pallas_call x11, Pallas kernels: 25 us -> 22.8 us  [call(): pl.pallas_call(body, grid=(1,), out_shape=outs_list if many else outs, in...]
where the time goes in v6:
time: 209 us; the launch traced here: 208 us
  blocking collectives  104 us (50%)
  starting transfers between devices  29.8 us (14%)
  waiting for transfers between devices  29.4 us (14%)
  Pallas kernels  25.8 us (12%)
  local copies, waits for them, and re-layouts  17.5 us (8%)
    all_to_all x6, blocking collectives, exchange(): return lax.all_to_all(array, axes, split_axis=0, concat_axis=0, tiled=True)  104 us
    pallas_call x11, Pallas kernels, call(): pl.pallas_call(body, grid=(1,), out_shape=outs_list if many else outs, in...  22.8 us
    all_to_all x3, starting transfers between devices, exchange(): return lax.all_to_all(array, axes, split_axis=0, concat_axis=0, tiled=True)  19.8 us
    unnamed x74, local copies, waits for them, and re-layouts  17.5 us
    ppermute x6, waiting for transfers between devices, program(): part = lax.ppermute(part, 'lev', [(i, (i + k) % 4) for i in range(4)])  16.9 us
    all_to_all x3, waiting for transfers between devices, exchange(): return lax.all_to_all(array, axes, split_axis=0, concat_axis=0, tiled=True)  12.5 us
    ppermute x6, starting transfers between devices, program(): part = lax.ppermute(part, 'lev', [(i, (i + k) % 4) for i in range(4)])  10.1 us
  transfers between devices with their start and end apart: 9, of which 6 were waited for; matrix products, arithmetic and copies ran while one was open for 0% of the time, Pallas kernels for 2%

profile of v6, /device:TPU:1, one launch (start us, length us, event | category | flops | bytes accessed | tf_op | source)
XLA Modules:
  0.0 207.9 jit_solution(6687608852047430663)
XLA Ops:
  0.6 3.6 %shard_map.129 = (bf16[128,2,8,128]{3,2,1,0:T(8,128)(2,1)}, f32[8,64,256]{2,1,0:T(8,128)}, bf16[8,256,256]{2,1,0:T(8,128)(2,1)}) custom-call(s32[256]{0:T(256)} %waves.7, bf16[8,256,256]{2,1,0:T(8,128)(2,1)} %legendre.1, f32[512,256]{1,0:T(8,128)} %bitcast.30, f32[4,512,256]{2,1,0:T(8,128)} %bitcast.15), custom_call_target="tpu_custom_call" | custom-call | flops 300000000 | bytes 4000000 | tf_op jit(solution)/shard_map/pallas_call | solution.py:330
  4.3 0.0 copy-start.23
  4.3 11.5 %all-to-all-start = ((bf16[128,2,8,128]{3,2,1,0:T(8,128)(2,1)}), bf16[128,2,8,128]{3,2,1,0:T(8,128)(2,1)S(1)}, u32[]{:S(2)}, u32[]{:S(2)}) async-start(bf16[128,2,8,128]{3,2,1,0:T(8,128)(2,1)} %get-tuple-element.39), calls=%async_computation | async-start | bytes 1048576 | tf_op jit(solution)/shard_map/all_to_all | solution.py:343
  15.8 3.0 %obs.1 = (bf16[1,2,128,128]{3,2,1,0:T(8,128)(2,1)}, bf16[1,2,128,128]{3,2,1,0:T(8,128)(2,1)}, bf16[1,2,128,128]{3,2,1,0:T(8,128)(2,1)}, bf16[1,2,128,128]{3,2,1,...) custom-call(s32[4]{0:T(128)} %obs_time.1, ...), custom_call_target="tpu_custom_call" | custom-call | flops 10000000 | bytes 3000000 | tf_op jit(solution)/shard_map/obs/pallas_call | solution.py:378
  18.8 1.4 collective-permute-start
  20.2 2.5 %collective-permute-start.1 = (bf16[1,2,128,128]{3,2,1,0:T(8,128)(2,1)}, bf16[1,2,128,128]{3,2,1,0:T(8,128)(2,1)S(1)}, u32[]{:S(2)}, u32[]{:S(2)}) collective-permute-start(bf16[1,2,128,128]{3,2,1,0:T(8,128)(2,1)} %get-tuple-element.42), channel_id=1, source_target_pairs={{0,2},{1,3},{2,0},{3,1},{4,6},{5,7},{6,4},{7,5},{8,10},{9,11},{10,... | collective-permute-start | bytes 196616 | tf_op jit(solution)/shard_map/ppermute | solution.py:391
  22.6 1.1 collective-permute-start.2
  23.7 3.0 %collective-permute-done.refs_7_ = bf16[1,2,128,128]{3,2,1,0:T(8,128)(2,1)S(1)} collective-permute-done((bf16[1,2,128,128]{3,2,1,0:T(8,128)(2,1)}, bf16[1,2,128,128]{3,2,1,0:T(8,128)(2,1)S(1)}, u32[]{:S(2)}, u32[]{:S(2)}) %collective-permute-start) | collective-permute-done | bytes 65568 | tf_op jit(solution)/shard_map/ppermute | solution.py:391
  26.7 1.6 collective-permute-done.1.refs_8_
  28.3 0.0 collective-permute-done.2.refs_9_
  28.3 0.6 copy-done.21
  28.9 1.0 all-to-all-done
  29.9 0.8 copy-done.7
  30.7 0.0 copy-done.10
  30.7 0.0 copy-done.18
  30.7 1.0 copy-done.8
  31.7 0.8 copy-done.20
  32.6 0.8 copy-done.22
  33.4 1.0 copy-done.24
  34.5 2.8 %shard_map.130 = (bf16[32,4,8,128]{3,2,1,0:T(8,128)(2,1)S(1)}, f32[1024,128]{1,0:T(8,128)S(1)}, f32[512,128]{1,0:T(8,128)S(1)}, bf16[512,512]{1,0:T(8,128)(2,1)S...) custom-call(bf16[32,4,2,8,128]{4,3,2,1,0:T(8,128)(2,1)S(1)} %bitcast.19, bf16[128,512]{1,0:T(8,128)(2,1)S(1)} %copy-done.16, ...), custom_call_target="tpu_custom_call" | custom-call | flops 1200000000 | bytes 3000000 | tf_op jit(solution)/shard_map/pallas_call | solution.py:330
  37.3 0.0 copy-start.30
  37.3 0.0 copy-start.33
  37.3 18.7 %all_to_all.45.back = bf16[128,8,128]{2,1,0:T(8,128)(2,1)S(1)} all-to-all(bf16[128,8,128]{2,1,0:T(8,128)(2,1)S(1)} %bitcast.23), channel_id=1, replica_groups=mesh['band_0'=4,'band_1'=4,'band_2'=2,'lev'=4] {'band_0','band_1','band_..., dimensions={0} | all-to-all | bytes 524288 | tf_op jit(solution)/shard_map/all_to_all | solution.py:343
  56.0 0.0 copy-done.2
  56.1 1.5 shard_map.131
  57.6 0.8 copy-done.3
  58.4 0.8 copy-done.9
  59.2 4.7 %all-to-all-start.2 = ((bf16[128,2,8,128]{3,2,1,0:T(8,128)(2,1)}), bf16[128,2,8,128]{3,2,1,0:T(8,128)(2,1)}, u32[]{:S(2)}, u32[]{:S(2)}) async-start(bf16[128,2,8,128]{3,2,1,0:T(8,128)(2,1)} %copy-done.9), calls=%async_computation.2 | async-start | bytes 1048576 | tf_op jit(solution)/shard_map/all_to_all | solution.py:343
  63.9 1.5 collective-permute-start.3
  65.4 2.5 %collective-permute-start.4 = (bf16[3,2,128,128]{3,2,1,0:T(8,128)(2,1)}, bf16[3,2,128,128]{3,2,1,0:T(8,128)(2,1)S(1)}, u32[]{:S(2)}, u32[]{:S(2)}) collective-permute-start(bf16[3,2,128,128]{3,2,1,0:T(8,128)(2,1)} %get-tuple-element.55), channel_id=1, source_target_pairs={{0,2},{1,3},{2,0},{3,1},{4,6},{5,7},{6,4},{7,5},{8,10},{9,11},{10,... | collective-permute-start | bytes 589832 | tf_op jit(solution)/shard_map/ppermute | solution.py:391
  67.9 1.1 collective-permute-start.5
  69.0 7.6 %collective-permute-done.3.refs_9_ = bf16[3,2,128,128]{3,2,1,0:T(8,128)(2,1)S(1)} collective-permute-done((bf16[3,2,128,128]{3,2,1,0:T(8,128)(2,1)}, bf16[3,2,128,128]{3,2,1,0:T(8,128)(2,1)S(1)}, u32[]{:S(2)}, u32[]{:S(2)}) %collective-permute-start.3) | collective-permute-done | bytes 196640 | tf_op jit(solution)/shard_map/ppermute | solution.py:391
  76.6 4.8 %collective-permute-done.4.refs_10_ = bf16[3,2,128,128]{3,2,1,0:T(8,128)(2,1)S(1)} collective-permute-done((bf16[3,2,128,128]{3,2,1,0:T(8,128)(2,1)}, bf16[3,2,128,128]{3,2,1,0:T(8,128)(2,1)S(1)}, u32[]{:S(2)}, u32[]{:S(2)}) %collective-permute-start.4) | collective-permute-done | bytes 196640 | tf_op jit(solution)/shard_map/ppermute | solution.py:391
  81.4 0.7 copy-done.12
  82.1 0.0 collective-permute-done.5.refs_11_
  82.1 0.7 copy-done.14
  82.7 0.0 all-to-all-done.2
  82.8 0.9 copy-done.13
  83.7 0.9 copy-done.15
  84.6 0.9 copy-done.17
  85.5 0.9 copy-done.19
  86.4 1.0 copy-done.26
  87.5 1.0 copy-done.29
  88.5 0.9 copy-done.31
  89.5 0.9 copy-done.34
  90.4 0.9 copy-done.36
  91.3 3.7 %shard_map.132 = (bf16[32,4,8,128]{3,2,1,0:T(8,128)(2,1)S(1)}, f32[1024,128]{1,0:T(8,128)S(1)}, f32[512,128]{1,0:T(8,128)S(1)}, bf16[3,4,2,128,128]{4,3,2,1,0:T(8,128)(2,1)S(1)}) custom-call(bf16[32,4,2,8,128]{4,3,2,1,0:T(8,128)(2,1)} %bitcast.7.refs_0_, bf16[128,512]{1,0:T(8,128)(2,1)S(1)} %copy-done.17, bf16[512,128]{1,0:T(8,128)(2,1)S(1)} %copy-done.19, ...), custom_call_target="tpu_custom_call" | custom-call | flops 1200000000 | bytes 3000000 | tf_op jit(solution)/shard_map/pallas_call | solution.py:330
  95.0 18.0 %all_to_all.46.back = bf16[128,8,128]{2,1,0:T(8,128)(2,1)S(1)} all-to-all(bf16[128,8,128]{2,1,0:T(8,128)(2,1)S(1)} %bitcast.24), channel_id=1, replica_groups=mesh['band_0'=4,'band_1'=4,'band_2'=2,'lev'=4] {'band_0','band_1','band_..., dimensions={0} | all-to-all | bytes 524288 | tf_op jit(solution)/shard_map/all_to_all | solution.py:343
  113.0 1.4 shard_map.133
  114.4 17.8 %all_to_all.47 = bf16[128,2,8,128]{3,2,1,0:T(8,128)(2,1)S(1)} all-to-all(bf16[128,2,8,128]{3,2,1,0:T(8,128)(2,1)S(1)} %get-tuple-element.59), channel_id=1, replica_groups=mesh['band_0'=4,'band_1'=4,'band_2'=2,'lev'=4] {'band_0','band_1','band_..., dimensions={0} | all-to-all | bytes 1048576 | tf_op jit(solution)/shard_map/all_to_all | solution.py:343
  132.2 0.0 copy-done.27
  132.2 2.5 %shard_map.134 = (bf16[32,4,8,128]{3,2,1,0:T(8,128)(2,1)S(1)}, f32[1024,128]{1,0:T(8,128)S(1)}, f32[512,128]{1,0:T(8,128)S(1)}) custom-call(bf16[32,4,2,8,128]{4,3,2,1,0:T(8,128)(2,1)S(1)} %bitcast.22, bf16[128,512]{1,0:T(8,128)(2,1)S(1)} %copy-done.17, bf16[512,128]{1,0:T(8,128)(2,1)S(1)} %copy-done.19, bf16[512,512]{1,0:T(8,128)(2,1)S(1)} %copy-done.27, ...), custom_call_target="tpu_custom_call" | custom-call | flops 1200000000 | bytes 3000000 | tf_op jit(solution)/shard_map/pallas_call | solution.py:330
  134.8 14.7 %all_to_all.48.back = bf16[128,8,128]{2,1,0:T(8,128)(2,1)S(1)} all-to-all(bf16[128,8,128]{2,1,0:T(8,128)(2,1)S(1)} %bitcast.25), channel_id=1, replica_groups=mesh['band_0'=4,'band_1'=4,'band_2'=2,'lev'=4] {'band_0','band_1','band_..., dimensions={0} | all-to-all | bytes 524288 | tf_op jit(solution)/shard_map/all_to_all | solution.py:343
  149.4 1.4 shard_map.135
  150.9 0.0 copy-start.5
  150.9 0.8 copy-done.5
  151.7 17.8 %all_to_all.49 = bf16[128,2,8,128]{3,2,1,0:T(8,128)(2,1)S(1)} all-to-all(bf16[128,2,8,128]{3,2,1,0:T(8,128)(2,1)S(1)} %get-tuple-element.65), channel_id=1, replica_groups=mesh['band_0'=4,'band_1'=4,'band_2'=2,'lev'=4] {'band_0','band_1','band_..., dimensions={0} | all-to-all | bytes 1048576 | tf_op jit(solution)/shard_map/all_to_all | solution.py:343
  169.4 2.7 %shard_map.136 = (bf16[32,4,2,8,128]{4,3,2,1,0:T(8,128)(2,1)S(1)}, f32[4,128]{1,0:T(4,128)S(1)}) custom-call(bf16[32,4,2,8,128]{4,3,2,1,0:T(8,128)(2,1)S(1)} %bitcast.20, bf16[128,512]{1,0:T(8,128)(2,1)S(1)} %copy-done.17, bf16[512,128]{1,0:T(8,128)(2,1)S(1)} %copy-done.19, bf16[512,512]{1,0:T(8,128)(2,1)S(1)} %copy-done.27, ...), custom_call_target="tpu_custom_call" | custom-call | flops 1200000000 | bytes 3000000 | tf_op jit(solution)/shard_map/pallas_call | solution.py:330
  172.1 17.5 %all_to_all.50.back = bf16[128,2,8,128]{3,2,1,0:T(8,128)(2,1)S(1)} all-to-all(bf16[128,2,8,128]{3,2,1,0:T(8,128)(2,1)S(1)} %bitcast.21), channel_id=1, replica_groups=mesh['band_0'=4,'band_1'=4,'band_2'=2,'lev'=4] {'band_0','band_1','band_..., dimensions={0} | all-to-all | bytes 1048576 | tf_op jit(solution)/shard_map/all_to_all | solution.py:343
  189.6 1.0 shard_map.138
  190.6 3.6 %all-to-all-start.8 = ((bf16[128,3,4,128]{3,2,1,0:T(4,128)(2,1)}), bf16[128,3,4,128]{3,2,1,0:T(4,128)(2,1)S(1)}, u32[]{:S(2)}, u32[]{:S(2)}) async-start(bf16[128,3,4,128]{3,2,1,0:T(4,128)(2,1)} %shard_map.138), calls=%async_computation.8 | async-start | bytes 786432 | tf_op jit(solution)/shard_map/all_to_all | solution.py:343
  194.2 1.3 shard_map.137
  195.5 11.5 %all-to-all-done.8.parts = bf16[128,3,4,128]{3,2,1,0:T(4,128)(2,1)S(1)} async-done(((bf16[128,3,4,128]{3,2,1,0:T(4,128)(2,1)}), bf16[128,3,4,128]{3,2,1,0:T(4,128)(2,1)S(1)}, u32[]{:S(2)}, u32[]{:S(2)}) %all-to-all-start.8) | async-done | bytes 393248 | tf_op jit(solution)/shard_map/all_to_all | solution.py:343
  207.0 0.8 shard_map.139
  (46 shorter events, 0.1 us)
Async XLA Ops:
  4.3 26.4 %copy-start.10 = (s32[256]{0:T(256)S(1)}, s32[256]{0:T(256)}, u32[]{:S(2)}) copy-start(s32[256]{0:T(256)} %waves.7) | copy-start | bytes 3076
  4.3 26.4 %copy-start.16 = (bf16[128,512]{1,0:T(8,128)(2,1)S(1)}, bf16[128,512]{1,0:T(8,128)(2,1)}, u32[]{:S(2)}) copy-start(bf16[128,512]{1,0:T(8,128)(2,1)} %refs_1_.7) | copy-start | bytes 393220
  4.3 26.4 %copy-start.18 = (bf16[512,128]{1,0:T(8,128)(2,1)S(1)}, bf16[512,128]{1,0:T(8,128)(2,1)}, u32[]{:S(2)}) copy-start(bf16[512,128]{1,0:T(8,128)(2,1)} %refs_2_.7) | copy-start | bytes 393220
  4.3 26.4 %copy-start.23 = (f32[512]{0:T(512)S(1)}, f32[512]{0:T(512)}, u32[]{:S(2)}) copy-start(f32[512]{0:T(512)} %param.18) | copy-start | bytes 6148
  4.3 25.6 %all-to-all-start = ((bf16[128,2,8,128]{3,2,1,0:T(8,128)(2,1)}), bf16[128,2,8,128]{3,2,1,0:T(8,128)(2,1)S(1)}, u32[]{:S(2)}, u32[]{:S(2)}) async-start(bf16[128,2,8,128]{3,2,1,0:T(8,128)(2,1)} %get-tuple-element.39), calls=%async_computation | async-start | bytes 1048576 | tf_op jit(solution)/shard_map/all_to_all | solution.py:343
  18.8 7.9 %collective-permute-start = (bf16[1,2,128,128]{3,2,1,0:T(8,128)(2,1)}, bf16[1,2,128,128]{3,2,1,0:T(8,128)(2,1)S(1)}, u32[]{:S(2)}, u32[]{:S(2)}) collective-permute-start(bf16[1,2,128,128]{3,2,1,0:T(8,128)(2,1)} %get-tuple-element.41), channel_id=1, source_target_pairs={{0,1},{1,2},{2,3},{3,0},{4,5},{5,6},{6,7},{7,4},{8,9},{9,10},{10,1... | collective-permute-start | bytes 196616 | tf_op jit(solution)/shard_map/ppermute | solution.py:391
  20.2 8.1 %collective-permute-start.1 = (bf16[1,2,128,128]{3,2,1,0:T(8,128)(2,1)}, bf16[1,2,128,128]{3,2,1,0:T(8,128)(2,1)S(1)}, u32[]{:S(2)}, u32[]{:S(2)}) collective-permute-start(bf16[1,2,128,128]{3,2,1,0:T(8,128)(2,1)} %get-tuple-element.42), channel_id=1, source_target_pairs={{0,2},{1,3},{2,0},{3,1},{4,6},{5,7},{6,4},{7,5},{8,10},{9,11},{10,... | collective-permute-start | bytes 196616 | tf_op jit(solution)/shard_map/ppermute | solution.py:391
  22.6 5.7 %collective-permute-start.2 = (bf16[1,2,128,128]{3,2,1,0:T(8,128)(2,1)}, bf16[1,2,128,128]{3,2,1,0:T(8,128)(2,1)S(1)}, u32[]{:S(2)}, u32[]{:S(2)}) collective-permute-start(bf16[1,2,128,128]{3,2,1,0:T(8,128)(2,1)} %get-tuple-element.43), channel_id=1, source_target_pairs={{0,3},{1,0},{2,1},{3,2},{4,7},{5,4},{6,5},{7,6},{8,11},{9,8},{10,9... | collective-permute-start | bytes 196616 | tf_op jit(solution)/shard_map/ppermute | solution.py:391
  28.3 0.6 copy-start.21
  29.9 0.8 copy-start.7
  30.7 1.0 copy-start.8
  31.7 0.8 copy-start.20
  32.6 0.8 copy-start.22
  33.4 1.0 copy-start.24
  34.5 21.6 %copy-start = (f32[4,4,8,2,8,256]{5,4,3,2,1,0:T(8,128)S(1)}, f32[4,4,8,2,8,256]{5,4,3,2,1,0:T(8,128)}, u32[]{:S(2)}) copy-start(f32[4,4,8,2,8,256]{5,4,3,2,1,0:T(8,128)} %param.10) | copy-start | bytes 6291460
  34.5 21.6 %copy-start.1 = (bf16[8,256,256]{2,1,0:T(8,128)(2,1)S(1)}, bf16[8,256,256]{2,1,0:T(8,128)(2,1)}, u32[]{:S(2)}) copy-start(bf16[8,256,256]{2,1,0:T(8,128)(2,1)} %get-tuple-element.46.table) | copy-start | bytes 3145732
  34.5 21.6 %copy-start.2 = (f32[8,64,256]{2,1,0:T(8,128)S(1)}, f32[8,64,256]{2,1,0:T(8,128)}, u32[]{:S(2)}) copy-start(f32[8,64,256]{2,1,0:T(8,128)} %get-tuple-element.45.damped_in) | copy-start | bytes 1572868
  37.3 20.3 %copy-start.25 = (bf16[512,512]{1,0:T(8,128)(2,1)}, bf16[512,512]{1,0:T(8,128)(2,1)S(1)}, u32[]{:S(2)}) copy-start(bf16[512,512]{1,0:T(8,128)(2,1)S(1)} %get-tuple-element.48.refs_3_) | copy-start | bytes 1572868
  37.3 20.3 %copy-start.28 = (f32[1024,128]{1,0:T(8,128)}, f32[1024,128]{1,0:T(8,128)S(1)}, u32[]{:S(2)}) copy-start(f32[1024,128]{1,0:T(8,128)S(1)} %get-tuple-element.51.refs_6_) | copy-start | bytes 1572868
  37.3 20.3 %copy-start.30 = (f32[512,128]{1,0:T(8,128)}, f32[512,128]{1,0:T(8,128)S(1)}, u32[]{:S(2)}) copy-start(f32[512,128]{1,0:T(8,128)S(1)} %get-tuple-element.50.refs_5_) | copy-start | bytes 786436
  37.3 20.3 %copy-start.33 = (f32[512,128]{1,0:T(8,128)}, f32[512,128]{1,0:T(8,128)S(1)}, u32[]{:S(2)}) copy-start(f32[512,128]{1,0:T(8,128)S(1)} %get-tuple-element.52.refs_7_) | copy-start | bytes 786436
  37.3 20.3 %copy-start.35 = (bf16[512,128]{1,0:T(8,128)(2,1)}, bf16[512,128]{1,0:T(8,128)(2,1)S(1)}, u32[]{:S(2)}) copy-start(bf16[512,128]{1,0:T(8,128)(2,1)S(1)} %get-tuple-element.49.refs_4_) | copy-start | bytes 393220
  56.1 26.7 %copy-start.11 = (bf16[3,2,128,128]{3,2,1,0:T(8,128)(2,1)S(1)}, bf16[3,2,128,128]{3,2,1,0:T(8,128)(2,1)}, u32[]{:S(2)}) copy-start(bf16[3,2,128,128]{3,2,1,0:T(8,128)(2,1)} %get-tuple-element.53.refs_8_) | copy-start | bytes 589828
  57.6 0.8 copy-start.3
  58.4 0.8 copy-start.9
  59.2 23.6 %all-to-all-start.2 = ((bf16[128,2,8,128]{3,2,1,0:T(8,128)(2,1)}), bf16[128,2,8,128]{3,2,1,0:T(8,128)(2,1)}, u32[]{:S(2)}, u32[]{:S(2)}) async-start(bf16[128,2,8,128]{3,2,1,0:T(8,128)(2,1)} %copy-done.9), calls=%async_computation.2 | async-start | bytes 1048576 | tf_op jit(solution)/shard_map/all_to_all | solution.py:343
  63.9 12.7 %collective-permute-start.3 = (bf16[3,2,128,128]{3,2,1,0:T(8,128)(2,1)}, bf16[3,2,128,128]{3,2,1,0:T(8,128)(2,1)S(1)}, u32[]{:S(2)}, u32[]{:S(2)}) collective-permute-start(bf16[3,2,128,128]{3,2,1,0:T(8,128)(2,1)} %get-tuple-element.54), channel_id=1, source_target_pairs={{0,1},{1,2},{2,3},{3,0},{4,5},{5,6},{6,7},{7,4},{8,9},{9,10},{10,1... | collective-permute-start | bytes 589832 | tf_op jit(solution)/shard_map/ppermute | solution.py:391
  65.4 16.0 %collective-permute-start.4 = (bf16[3,2,128,128]{3,2,1,0:T(8,128)(2,1)}, bf16[3,2,128,128]{3,2,1,0:T(8,128)(2,1)S(1)}, u32[]{:S(2)}, u32[]{:S(2)}) collective-permute-start(bf16[3,2,128,128]{3,2,1,0:T(8,128)(2,1)} %get-tuple-element.55), channel_id=1, source_target_pairs={{0,2},{1,3},{2,0},{3,1},{4,6},{5,7},{6,4},{7,5},{8,10},{9,11},{10,... | collective-permute-start | bytes 589832 | tf_op jit(solution)/shard_map/ppermute | solution.py:391
  67.9 14.2 %collective-permute-start.5 = (bf16[3,2,128,128]{3,2,1,0:T(8,128)(2,1)}, bf16[3,2,128,128]{3,2,1,0:T(8,128)(2,1)S(1)}, u32[]{:S(2)}, u32[]{:S(2)}) collective-permute-start(bf16[3,2,128,128]{3,2,1,0:T(8,128)(2,1)} %get-tuple-element.56), channel_id=1, source_target_pairs={{0,3},{1,0},{2,1},{3,2},{4,7},{5,4},{6,5},{7,6},{8,11},{9,8},{10,9... | collective-permute-start | bytes 589832 | tf_op jit(solution)/shard_map/ppermute | solution.py:391
  81.4 0.7 copy-start.12
  82.1 0.7 copy-start.14
  82.8 0.9 copy-start.13
  83.7 0.9 copy-start.15
  84.6 0.9 copy-start.17
  85.5 0.9 copy-start.19
  86.4 1.0 copy-start.26
  87.5 1.0 copy-start.29
  88.5 0.9 copy-start.31
  89.5 0.9 copy-start.34
  90.4 0.9 copy-start.36
  91.3 21.7 %copy-start.4 = (f32[8,64,256]{2,1,0:T(8,128)S(1)}, f32[8,64,256]{2,1,0:T(8,128)}, u32[]{:S(2)}) copy-start(f32[8,64,256]{2,1,0:T(8,128)} %copy-done.3) | copy-start | bytes 1572868
  113.0 19.2 %copy-start.27 = (bf16[512,512]{1,0:T(8,128)(2,1)S(1)}, bf16[512,512]{1,0:T(8,128)(2,1)}, u32[]{:S(2)}) copy-start(bf16[512,512]{1,0:T(8,128)(2,1)} %copy-done.25) | copy-start | bytes 1572868
  113.0 19.2 %copy-start.32 = (f32[512,128]{1,0:T(8,128)S(1)}, f32[512,128]{1,0:T(8,128)}, u32[]{:S(2)}) copy-start(f32[512,128]{1,0:T(8,128)} %copy-done.30) | copy-start | bytes 786436
  150.9 0.8 copy-start.5
  172.1 22.0 %copy-start.6 = (f32[8,64,256]{2,1,0:T(8,128)S(1)}, f32[8,64,256]{2,1,0:T(8,128)}, u32[]{:S(2)}) copy-start(f32[8,64,256]{2,1,0:T(8,128)} %copy-done.5) | copy-start | bytes 1572868
  190.6 16.4 %all-to-all-start.8 = ((bf16[128,3,4,128]{3,2,1,0:T(4,128)(2,1)}), bf16[128,3,4,128]{3,2,1,0:T(4,128)(2,1)S(1)}, u32[]{:S(2)}, u32[]{:S(2)}) async-start(bf16[128,3,4,128]{3,2,1,0:T(4,128)(2,1)} %shard_map.138), calls=%async_computation.8 | async-start | bytes 786432 | tf_op jit(solution)/shard_map/all_to_all | solution.py:343
